TPU v7x, 32 devices: a whole 2x2x4 slice. The times are simulated.
32 devices in a mesh: gx: 4 (over x, core), gy: 8 (over z, y).
Axes of the slice: x: 2, y: 2, z: 4, core: 2. Of those that a mesh axis runs over, the one named last changes fastest.
Arguments:
- right_side: float32 [2, 64, 256, 128], P(None, 'gx', 'gy'), may hold values from -6 to 6
- wavenumber: float32 [64, 256, 128], P('gx', 'gy'), may hold values from 0.2 to 1
- pml_layer: int32 [64, 256, 128], P('gx', 'gy'), may hold values from 0 to 3
- aggregate: int32 [64, 256, 128], P('gx', 'gy'), may hold values from 0 to 15, as said below
- coarse_inverse: float32 [2, 512, 512], P(None, ('gx', 'gy')), may hold values from -0.0029296875 to 0.0029296875
Outputs:
- solution: float32 [2, 64, 256, 128], P(None, 'gx', 'gy')
- hessenberg: float32 [2, 5, 4], replicated
Inputs may be any that keep to these rules, and one draw needn't show every extreme that they name: `aggregate`: along the third dimension the value never falls, and every value of 0 to 15 occurs in every column of cells.
All inputs are finite; a program needn't handle non-finite values.
Results may differ from a plain program's by a relative error of at most 0.00015.
Values sent between devices are 32-bit elements; how exact they have to be, the bound alone decides.
No kernel may reach another device: no remote copies, remote signals or barrier semaphores. Data moves between devices by JAX's collectives and lax.ppermute only.
A program may use at most 64 MiB of HBM per device.

v0:
```python
import math

import jax
import jax.numpy as jnp
from jax import lax
from jax.sharding import PartitionSpec as P

ITERS = 4


damping = 0.8
pml_strength = 3.0
epsilon = 1e-06


def with_halo(block, sides, width):
    for axis, dim in sides:
        count = lax.axis_size(axis)
        forward = [(i, i + 1) for i in range(count - 1)]
        backward = [(target, source) for source, target in forward]
        low = lax.ppermute(
            lax.slice_in_dim(block, block.shape[dim] - width, None, axis=dim), axis, forward
        )
        high = lax.ppermute(lax.slice_in_dim(block, 0, width, axis=dim), axis, backward)
        block = jnp.concatenate([low, block, high], axis=dim)
    return block


def coefficients(wavenumber, layer_float):
    wave_sq = wavenumber * wavenumber
    depth = layer_float / 3.0
    absorb = wave_sq * (pml_strength * depth * depth)
    diag_re = 6.0 - wave_sq
    magnitude = diag_re * diag_re + absorb * absorb
    return (wave_sq, absorb, damping * diag_re / magnitude, damping * absorb / magnitude)


def operate_inner(extended, wave_sq, absorb):
    middle = extended[:, 1:-1, 1:-1]
    above = jnp.concatenate([middle[..., 1:], jnp.zeros_like(middle[..., :1])], -1)
    below = jnp.concatenate([jnp.zeros_like(middle[..., :1]), middle[..., :-1]], -1)
    beside = (
        extended[:, 2:, 1:-1]
        + extended[:, :-2, 1:-1]
        + extended[:, 1:-1, 2:]
        + extended[:, 1:-1, :-2]
        + above
        + below
    )
    real_part = (6.0 - wave_sq) * middle[0] - beside[0] + absorb * middle[1]
    imag_part = (6.0 - wave_sq) * middle[1] - beside[1] - absorb * middle[0]
    return jnp.stack([real_part, imag_part])


def smooth(field, scale_re, scale_im):
    return jnp.stack(
        [scale_re * field[0] - scale_im * field[1], scale_re * field[1] + scale_im * field[0]]
    )


def complex_scale(scale_re, scale_im, field):
    return jnp.stack(
        [scale_re * field[0] - scale_im * field[1], scale_re * field[1] + scale_im * field[0]]
    )


def inner_local(left, right):
    return jnp.stack(
        [
            jnp.sum(left[0] * right[0] + left[1] * right[1]),
            jnp.sum(left[0] * right[1] - left[1] * right[0]),
        ]
    )


def least_squares(hessenberg, beta):
    real_h = hessenberg[0]
    imag_h = hessenberg[1]
    stacked = jnp.concatenate(
        [jnp.concatenate([real_h, -imag_h], 1), jnp.concatenate([imag_h, real_h], 1)], 0
    )
    count = stacked.shape[1]
    target = jnp.zeros((stacked.shape[0],), jnp.float32).at[0].set(beta)
    ortho = []
    upper = {}
    for column in range(count):
        vector = stacked[:, column]
        for position in range(column):
            upper[position, column] = jnp.zeros((), jnp.float32)
        for repeat in range(2):
            for position in range(len(ortho)):
                weight = jnp.sum(ortho[position] * vector)
                vector = vector - weight * ortho[position]
                upper[position, column] = upper[position, column] + weight
        norm_value = jnp.sqrt(jnp.sum(vector * vector))
        upper[column, column] = norm_value
        ortho.append(vector / norm_value)
    project = [jnp.sum(basis_vec * target) for basis_vec in ortho]
    solved = [None] * count
    for column in reversed(range(count)):
        total = project[column]
        for later in range(column + 1, count):
            total = total - upper[column, later] * solved[later]
        solved[column] = total / upper[column, column]
    return solved


def restrict(flat_field, flat_ids, levels_count):
    total = flat_ids.shape[0]
    block = math.gcd(total, 16384)
    levels = jnp.arange(levels_count, dtype=jnp.int32)

    def accumulate(step_index, result):
        piece = lax.dynamic_slice_in_dim(flat_field, step_index * block, block, 1)
        labels = lax.dynamic_slice_in_dim(flat_ids, step_index * block, block, 0)
        onehot = (labels[None, :] == levels[:, None]).astype(jnp.float32)
        return result + lax.dot_general(
            piece, onehot, (((1,), (1,)), ((), ())), precision=lax.Precision.HIGHEST
        )

    return lax.fori_loop(0, total // block, accumulate, jnp.zeros((2, levels_count), jnp.float32))


def prolong(values, flat_ids):
    total = flat_ids.shape[0]
    block = math.gcd(total, 16384)
    levels = jnp.arange(values.shape[1], dtype=jnp.int32)

    def place(step_index, result):
        labels = lax.dynamic_slice_in_dim(flat_ids, step_index * block, block, 0)
        onehot = (levels[:, None] == labels[None, :]).astype(jnp.float32)
        piece = jnp.dot(values, onehot, precision=lax.Precision.HIGHEST)
        return lax.dynamic_update_slice_in_dim(result, piece, step_index * block, 1)

    return lax.fori_loop(0, total // block, place, jnp.zeros((2, total), jnp.float32))


def coarse_fix(remainder, flat_ids, coarse_inverse):
    highest = lax.Precision.HIGHEST
    levels_count = coarse_inverse.shape[1]
    total_coarse = coarse_inverse.shape[2]
    partial_value = restrict(remainder.reshape(2, -1), flat_ids, levels_count)
    offset = (lax.axis_index("gx") * lax.axis_size("gy") + lax.axis_index("gy")) * levels_count
    padded = lax.dynamic_update_slice(
        jnp.zeros((2, total_coarse), jnp.float32), partial_value, (jnp.zeros((), jnp.int32), offset)
    )
    whole = lax.psum(padded, ("gx", "gy"))
    own_re = jnp.dot(coarse_inverse[0], whole[0], precision=highest) - jnp.dot(
        coarse_inverse[1], whole[1], precision=highest
    )
    own_im = jnp.dot(coarse_inverse[0], whole[1], precision=highest) + jnp.dot(
        coarse_inverse[1], whole[0], precision=highest
    )
    return prolong(jnp.stack([own_re, own_im]), flat_ids).reshape(remainder.shape)


def operate_near(field, wave_sq, absorb):
    extended = with_halo(field, (("gx", 1), ("gy", 2)), 1)
    return operate_inner(extended, wave_sq, absorb)


def operate_final(field, wave_sq, absorb):
    extended = with_halo(field, (("gx", 1), ("gy", 2)), 1)
    return operate_inner(extended, wave_sq, absorb)


def body(right_side, wavenumber, pml_layer, aggregate, coarse_inverse):
    layer_float = pml_layer.astype(jnp.float32)
    wave_sq, absorb, scale_re, scale_im = coefficients(wavenumber, layer_float)
    flat_ids = aggregate.reshape(-1)
    beta = jnp.sqrt(lax.psum(jnp.sum(right_side * right_side), ("gx", "gy")) + epsilon)
    basis = [right_side / beta]
    directions = []
    columns_re = []
    columns_im = []
    for column in range(ITERS):
        vector = basis[column]
        first = smooth(vector, scale_re, scale_im)
        second = first + smooth(vector - operate_near(first, wave_sq, absorb), scale_re, scale_im)
        remainder = vector - operate_near(second, wave_sq, absorb)
        direction = second + coarse_fix(remainder, flat_ids, coarse_inverse)
        image = operate_final(direction, wave_sq, absorb)
        local_dots = jnp.stack([inner_local(member, image) for member in basis], 1)
        dots, squared = lax.psum((local_dots, jnp.sum(image * image)), ("gx", "gy"))
        for position in range(len(basis)):
            image = image - complex_scale(dots[0, position], dots[1, position], basis[position])
        leftover = squared - jnp.sum(dots * dots)
        length = jnp.sqrt(jnp.maximum(leftover, 0.0) + epsilon)
        tail = jnp.zeros((ITERS - 1 - column,), jnp.float32)
        columns_re.append(jnp.concatenate([dots[0], length[None], tail]))
        columns_im.append(jnp.concatenate([dots[1], jnp.zeros((1,), jnp.float32), tail]))
        directions.append(direction)
        if column + 1 < ITERS:
            basis.append(image / length)
    hessenberg = jnp.stack([jnp.stack(columns_re, 1), jnp.stack(columns_im, 1)])
    solved = least_squares(hessenberg, beta)
    solution = jnp.zeros_like(right_side)
    for column in range(ITERS):
        solution = solution + complex_scale(
            solved[column], solved[ITERS + column], directions[column]
        )
    return (solution, hessenberg)


def solution(mesh):
    return jax.shard_map(
        body,
        mesh=mesh,
        in_specs=(
            P(None, "gx", "gy", None),
            P("gx", "gy", None),
            P("gx", "gy", None),
            P("gx", "gy", None),
            P(None, ("gx", "gy"), None),
        ),
        out_specs=(P(None, "gx", "gy", None), P()),
        check_vma=False,
    )
```

profile of v0, /device:TPU:0, one launch (start us, length us, event | category | flops | bytes accessed | tf_op | source)
XLA Modules:
  0.0 809.8 jit_solution(285482413600228902)
XLA Ops:
  2.5 42.2 %psum.91 = f32[]{:T(128)} all-reduce(f32[]{:T(128)} %multiply_reduce_fusion.3), channel_id=1, replica_groups=mesh['gx'=4,'gy'=8] {'gx','gy'}, use_global_device_ids=true, to_apply=%region_1.0 | all-reduce | flops 1 | bytes 8 | tf_op jit(solution)/shard_map/psum | solution.py:171
  48.0 3.0 collective-permute-start.1
  53.2 5.0 collective-permute-start.3
  62.3 3.0 collective-permute-start.5
  67.5 5.4 collective-permute-start.7
  76.2 7.0 while.117
  83.3 46.5 %psum.92 = f32[2,512]{1,0:T(2,128)S(1)} all-reduce(f32[2,512]{1,0:T(2,128)S(1)} %dynamic_update_slice.40), channel_id=1, replica_groups=mesh['gx'=4,'gy'=8] {'gx','gy'}, use_global_device_ids=true, to_apply=%region_4.0 | all-reduce | flops 1024 | bytes 8192 | tf_op jit(solution)/shard_map/psum | solution.py:147
  134.9 3.0 collective-permute-start.9
  140.2 4.8 collective-permute-start.11
  149.7 43.8 %all-reduce.29 = (f32[2,1]{0,1:T(1,128)S(1)}, f32[]{:T(128)}) all-reduce(f32[2,1]{0,1:T(1,128)S(1)} %maximum_bitcast_fusion.1, f32[]{:T(128)} %multiply_reduce_fusion.2), channel_id=1, replica_groups=mesh['gx'=4,'gy'=8] {'gx','gy'}, use_global_device_ids=true, to_apply=%region_9.0 | all-reduce | flops 3 | bytes 24 | tf_op jit(solution)/shard_map/psum | solution.py:184
  199.2 3.0 collective-permute-start.13
  204.4 5.0 collective-permute-start.15
  214.4 3.4 collective-permute-start.17
  220.2 5.3 collective-permute-start.19
  228.3 2.1 divide_subtract_fusion.2
  230.3 6.9 while.118
  237.5 47.6 %psum.95 = f32[2,512]{1,0:T(2,128)S(1)} all-reduce(f32[2,512]{1,0:T(2,128)S(1)} %dynamic_update_slice.41), channel_id=1, replica_groups=mesh['gx'=4,'gy'=8] {'gx','gy'}, use_global_device_ids=true, to_apply=%region_15.0 | all-reduce | flops 1024 | bytes 8192 | tf_op jit(solution)/shard_map/psum | solution.py:147
  290.5 3.0 collective-permute-start.21
  295.7 4.8 collective-permute-start.23
  306.9 43.6 %all-reduce.28 = (f32[2,2]{0,1:T(2,128)S(1)}, f32[]{:T(128)}) all-reduce(f32[2,2]{0,1:T(2,128)S(1)} %pad_maximum_fusion.166, f32[]{:T(128)} %multiply_reduce_fusion.1), channel_id=1, replica_groups=mesh['gx'=4,'gy'=8] {'gx','gy'}, use_global_device_ids=true, to_apply=%region_22.0 | all-reduce | flops 5 | bytes 40 | tf_op jit(solution)/shard_map/psum | solution.py:184
  357.4 3.0 collective-permute-start.25
  362.6 5.0 collective-permute-start.27
  372.0 3.3 collective-permute-start.29
  377.5 5.4 collective-permute-start.31
  385.8 2.4 divide_subtract_fusion.1
  388.2 6.9 while.119
  395.3 47.6 %psum.98 = f32[2,512]{1,0:T(2,128)S(1)} all-reduce(f32[2,512]{1,0:T(2,128)S(1)} %dynamic_update_slice.42), channel_id=1, replica_groups=mesh['gx'=4,'gy'=8] {'gx','gy'}, use_global_device_ids=true, to_apply=%region_28.0 | all-reduce | flops 1024 | bytes 8192 | tf_op jit(solution)/shard_map/psum | solution.py:147
  448.4 3.0 collective-permute-start.33
  453.6 4.8 collective-permute-start.35
  467.3 43.7 %all-reduce.27 = (f32[2,3]{0,1:T(4,128)S(1)}, f32[]{:T(128)}) all-reduce(f32[2,3]{0,1:T(4,128)S(1)} %pad_maximum_fusion.161, f32[]{:T(128)} %multiply_reduce_fusion), channel_id=1, replica_groups=mesh['gx'=4,'gy'=8] {'gx','gy'}, use_global_device_ids=true, to_apply=%region_37.0 | all-reduce | flops 7 | bytes 56 | tf_op jit(solution)/shard_map/psum | solution.py:184
  513.7 2.5 multiply_subtract_fusion.5
  522.2 3.0 collective-permute-start.37
  528.0 5.1 collective-permute-start.39
  537.5 3.1 collective-permute-start.41
  542.8 5.6 collective-permute-start.43
  550.0 2.8 divide_subtract_fusion
  552.9 6.9 while.120
  560.0 47.0 %psum.101 = f32[2,512]{1,0:T(2,128)S(1)} all-reduce(f32[2,512]{1,0:T(2,128)S(1)} %dynamic_update_slice.43), channel_id=1, replica_groups=mesh['gx'=4,'gy'=8] {'gx','gy'}, use_global_device_ids=true, to_apply=%region_43.0 | all-reduce | flops 1024 | bytes 8192 | tf_op jit(solution)/shard_map/psum | solution.py:147
  608.5 4.3 while.116
  615.6 3.0 collective-permute-start.45
  620.8 4.8 collective-permute-start.47
  636.3 43.7 %all-reduce.26 = (f32[2,4]{0,1:T(4,128)S(1)}, f32[]{:T(128)}) all-reduce(f32[2,4]{0,1:T(4,128)S(1)} %pad_maximum_fusion.162, f32[]{:T(128)} %fusion.133), channel_id=1, replica_groups=mesh['gx'=4,'gy'=8] {'gx','gy'}, use_global_device_ids=true, to_apply=%region_54.0 | all-reduce | flops 9 | bytes 72 | tf_op jit(solution)/shard_map/psum | solution.py:184
  708.7 2.6 multiply_reduce_fusion.41
  715.1 2.6 multiply_reduce_fusion.39
  725.9 3.1 multiply_reduce_fusion.29
  736.5 2.6 multiply_reduce_fusion.19
  740.9 3.1 multiply_reduce_fusion.17
  749.0 2.6 multiply_reduce_fusion.15
  (490 shorter events, 229.9 us)
Async XLA Ops:
  46.7 4.3 collective-permute-start
  48.0 3.9 collective-permute-start.1
  51.9 6.5 collective-permute-start.2
  53.2 6.5 collective-permute-start.3
  61.0 4.3 collective-permute-start.4
  62.3 3.9 collective-permute-start.5
  66.2 7.0 collective-permute-start.6
  67.5 6.9 collective-permute-start.7
  133.6 4.3 collective-permute-start.8
  134.9 3.9 collective-permute-start.9
  138.9 6.3 collective-permute-start.10
  140.2 6.3 collective-permute-start.11
  197.9 4.3 collective-permute-start.12
  199.2 3.9 collective-permute-start.13
  203.1 6.5 collective-permute-start.14
  204.4 6.4 collective-permute-start.15
  213.1 4.7 collective-permute-start.16
  214.4 4.5 collective-permute-start.17
  218.9 6.9 collective-permute-start.18
  220.2 6.6 collective-permute-start.19
  289.2 4.3 collective-permute-start.20
  290.5 3.9 collective-permute-start.21
  294.4 6.3 collective-permute-start.22
  295.7 6.3 collective-permute-start.23
  356.1 4.3 collective-permute-start.24
  357.4 3.9 collective-permute-start.25
  361.3 6.5 collective-permute-start.26
  362.6 6.4 collective-permute-start.27
  370.7 4.6 collective-permute-start.28
  372.0 4.2 collective-permute-start.29
  376.2 6.9 collective-permute-start.30
  377.5 6.6 collective-permute-start.31
  447.1 4.4 collective-permute-start.32
  448.4 3.9 collective-permute-start.33
  452.3 6.3 collective-permute-start.34
  453.6 6.3 collective-permute-start.35
  520.9 5.8 collective-permute-start.36
  522.2 4.5 collective-permute-start.37
  526.7 6.6 collective-permute-start.38
  528.0 6.5 collective-permute-start.39
  536.2 4.6 collective-permute-start.40
  537.5 4.0 collective-permute-start.41
  541.5 7.1 collective-permute-start.42
  542.8 6.8 collective-permute-start.43
  614.3 4.4 collective-permute-start.44
  615.6 3.9 collective-permute-start.45
  619.5 6.3 collective-permute-start.46
  620.8 6.3 collective-permute-start.47
  (68 other events, 938.6 us)
where the time goes:
time: 821 us; the launch traced here: 810 us
  blocking collectives  406 us (49%)
  other arithmetic  135 us (16%)
  starting transfers between devices  129 us (16%)
  between operations  54.8 us (7%)
  matrix products  39.1 us (5%)
  waiting for transfers between devices  23.2 us (3%)
  local copies, waits for them, and re-layouts  22.3 us (3%)
    psum x4, blocking collectives, coarse_fix(): whole = lax.psum(padded, ('gx', 'gy'))  189 us
    psum x4, blocking collectives, body(): dots, squared = lax.psum((local_dots, jnp.sum(image * image)), ('gx', 'gy'))  175 us
    ppermute x24, starting transfers between devices, with_halo(): lax.ppermute(lax.slice_in_dim(block, block.shape[dim] - width, None, axis...  98.2 us
    reduce_sum x34, other arithmetic, least_squares(): weight = jnp.sum(ortho[position] * vector)  64.5 us
    psum x1, blocking collectives, body(): lax.psum(jnp.sum(right_side * right_side), ('gx', 'gy')) + epsilon  42.2 us
    ppermute x24, starting transfers between devices, with_halo(): lax.ppermute(lax.slice_in_dim(block, 0, width, axis=dim), axis, backward)  31 us
    dot_general x16, matrix products, accumulate(): lax.dot_general(piece, onehot, (((1,), (1,)), ((), ())), precision=lax.Pr...  27.2 us
    ppermute x24, waiting for transfers between devices, with_halo(): lax.ppermute(lax.slice_in_dim(block, block.shape[dim] - width, None, axis...  23.1 us
  transfers between devices with their start and end apart: 48, of which 23 were waited for; matrix products, arithmetic and copies ran while one was open for 1% of the time, Pallas kernels for 0%

commit v1 on v0

v1 whole, which is shorter than its diff:
```python
import functools

import jax
import jax.numpy as jnp
from jax import lax
from jax.experimental import pallas as pl
from jax.experimental.pallas import tpu as pltpu
from jax.sharding import PartitionSpec as P

ITERS = 4
HALO = 2 * ITERS
AXES = ("gx", "gy")
AGG = 16
damping = 0.8
pml_strength = 3.0
epsilon = 1e-06
F32 = jnp.float32
VLIMIT = 24 * 1024 * 1024


def lanes(shape):
    return lax.broadcasted_iota(jnp.int32, shape, len(shape) - 1)


def turn(x):
    odd = (lanes(x.shape) // AGG) % 2 == 1
    return jnp.where(odd, pltpu.roll(x, AGG, 1), -pltpu.roll(x, x.shape[1] - AGG, 1))


def turn_rows(x):
    parts = [turn(x[:, i : i + 128]) for i in range(0, x.shape[1], 128)]
    return jnp.concatenate(parts, axis=1)


def pick(row, lane):
    return jnp.broadcast_to(row[:, lane : lane + 1], (8, 128))


def take(table, index):
    rows = index.shape[0]
    src = jnp.broadcast_to(table, (rows, 128))
    return jnp.take_along_axis(src, index, axis=1, mode="promise_in_bounds")


def planes(lo, hi, fn, carry=None, unroll=1):
    if carry is None:
        def go(x, c):
            fn(x)
            return c
        return lax.fori_loop(lo, hi, go, 0, unroll=unroll)
    return lax.fori_loop(lo, hi, fn, carry, unroll=unroll)


def stencil(ref, c, x, y0, y1):
    mid = ref[c, x, 8 + y0 : 8 + y1, :]
    total = (
        ref[c, x - 1, 8 + y0 : 8 + y1, :]
        + ref[c, x + 1, 8 + y0 : 8 + y1, :]
        + ref[c, x, 7 + y0 : 7 + y1, :]
        + ref[c, x, 9 + y0 : 9 + y1, :]
    )
    lane = lanes(mid.shape)
    last = mid.shape[-1] - 1
    total = total + jnp.where(lane == 0, 0.0, pltpu.roll(mid, 1, 1))
    total = total + jnp.where(lane == last, 0.0, pltpu.roll(mid, last, 1))
    return mid, total


def operate_plane(ref, diag, absorb, x, y0, y1):
    d = diag[x, y0:y1, :]
    a = absorb[x, y0:y1, :]
    m0, t0 = stencil(ref, 0, x, y0, y1)
    m1, t1 = stencil(ref, 1, x, y0, y1)
    return d * m0 - t0 + a * m1, d * m1 - t1 - a * m0


def zero_pads(ref, ey):
    shape = ref.shape
    z = jnp.zeros((8, shape[3]), F32)
    for c in range(2):
        def go(x, carry, c=c):
            ref[c, x, 0:8, :] = z
            ref[c, x, 8 + ey : 16 + ey, :] = z
            return carry
        lax.fori_loop(0, shape[1], go, 0)


def fold8(x):
    out = x[0:8]
    for i in range(8, x.shape[0], 8):
        out = out + x[i : i + 8]
    return out


def prefix(x):
    lane = lanes(x.shape)
    step = 1
    while step < x.shape[1]:
        x = x + jnp.where(lane >= step, pltpu.roll(x, step, 1), 0.0)
        step *= 2
    return x


def spread_rhs(g0, g1, cols_ref, pad_ref, out_ref, scalars, grid):
    gx, gy = grid
    n = gx * gy
    lane = lanes((1, 128))
    rows = []
    for g in (g0, g1):
        total = jnp.sum(g, axis=0, keepdims=True)
        rows.append(jnp.where(lane == 0, total, total - pltpu.roll(total, 1, 1)))
    z = []
    for row in rows:
        acc = None
        for q in range(4):
            weight = take(row, lanes((8, 128)) // 32 + 4 * q)[0:1]
            term = cols_ref[:, 128 * q : 128 * (q + 1)] * weight
            acc = term if acc is None else acc + term
        acc = acc + pltpu.roll(acc, 64, 1)
        z.append(acc + pltpu.roll(acc, 32, 1))
    whole = z[0] + turn(z[1])
    margin = (pad_ref.shape[0] - n) // 2
    pad_ref[0:margin, :] = jnp.zeros((margin, 128), F32)
    pad_ref[margin + n : 2 * margin + n, :] = jnp.zeros((margin, 128), F32)
    pad_ref[margin : margin + n, :] = whole
    place = lax.broadcasted_iota(jnp.int32, (n, 128), 0) % gy
    group = lanes((n, 128)) // 32
    outs = [jnp.zeros((n, 128), F32) for _ in range(3)]
    for dx in (-1, 0, 1):
        for dy in (-1, 0, 1):
            k = (dx + 1) * 3 + dy + 1
            start = margin + dx * gy + dy
            piece = pad_ref[start : start + n, :]
            ok = (group == k % 4) & (place + dy >= 0) & (place + dy < gy)
            outs[k // 4] = jnp.where(ok, piece, outs[k // 4])
    outs[2] = outs[2] + jnp.broadcast_to(scalars, (n, 128))
    for r in range(3):
        out_ref[:, 128 * r : 128 * (r + 1)] = outs[r]


def scalar_row(items):
    lane = lanes((1, 128))
    row = jnp.zeros((1, 128), F32)
    for where, acc in items:
        s = jnp.sum(jnp.sum(acc, axis=0, keepdims=True), axis=1, keepdims=True)
        row = jnp.where(lane == where, jnp.broadcast_to(s, (1, 128)), row)
    return row


def second_passes(f, g, u_at, coefs, halo, own, ends, t_ref, s_ref, ey):
    diag, absorb, sre, sim = coefs
    cx, cy = own

    def smooth_pass(x):
        a0, a1 = operate_plane(f, diag, absorb, x, 0, ey)
        u0, u1 = u_at(x, 0, ey)
        e0, e1 = u0 - a0, u1 - a1
        p, q = sre[x], sim[x]
        g[0, x, 8 : 8 + ey, :] = f[0, x, 8 : 8 + ey, :] + (p * e0 - q * e1)
        g[1, x, 8 : 8 + ey, :] = f[1, x, 8 : 8 + ey, :] + (p * e1 + q * e0)

    planes(HALO - halo - 1, HALO + cx + halo + 1, smooth_pass)

    def edge(x):
        a0, a1 = operate_plane(g, diag, absorb, x, 0, ey)
        t_ref[0, x], t_ref[1, x] = a0, a1

    if halo > 0:
        planes(HALO - halo, HALO, edge)
        planes(HALO + cx, HALO + cx + halo, edge)
    y0, y1 = HALO, HALO + cy

    def middle(x, carry):
        g0, g1 = carry
        if halo > 0:
            a0, a1 = operate_plane(g, diag, absorb, x, 0, ey)
            t_ref[0, x], t_ref[1, x] = a0, a1
            a0, a1 = a0[y0:y1], a1[y0:y1]
        else:
            a0, a1 = operate_plane(g, diag, absorb, x, y0, y1)
            t_ref[0, x, y0:y1, :], t_ref[1, x, y0:y1, :] = a0, a1
        u0, u1 = u_at(x, y0, y1)
        s_ref[0, x - HALO] = g[0, x, 8 + y0 : 8 + y1, :]
        s_ref[1, x - HALO] = g[1, x, 8 + y0 : 8 + y1, :]
        index = ends[x - HALO]
        w0 = jnp.take_along_axis(prefix(u0 - a0), index, axis=1, mode="promise_in_bounds")
        w1 = jnp.take_along_axis(prefix(u1 - a1), index, axis=1, mode="promise_in_bounds")
        return g0 + fold8(w0), g1 + fold8(w1)

    zero = jnp.zeros((8, 128), F32)
    return planes(HALO, HALO + cx, middle, (zero, zero))


def start_kernel(grid, own,
                 rhs, wave, layer, agg, ylo, yhi, xlo, xhi, cols,
                 diag, absorb, sre, sim, ids, ends, t_ref, s_ref, out_ref,
                 u, f, g, pad):
    cx, cy = own
    ex, ey = cx + 2 * HALO, cy + 2 * HALO
    zero_pads(f, ey)
    zero_pads(g, ey)

    def fill(x, y0, y1, r0, r1, k, l, a):
        sq = k * k
        depth = l / 3.0
        ab = sq * (pml_strength * depth * depth)
        d = 6.0 - sq
        w = jnp.where(k > 0.0, damping / (d * d + ab * ab), 0.0)
        p, q = d * w, ab * w
        diag[x, y0:y1, :] = d
        absorb[x, y0:y1, :] = ab
        sre[x, y0:y1, :] = p
        sim[x, y0:y1, :] = q
        ids[x, y0:y1, :] = a
        u[0, x, y0:y1, :] = r0
        u[1, x, y0:y1, :] = r1
        f[0, x, 8 + y0 : 8 + y1, :] = p * r0 - q * r1
        f[1, x, 8 + y0 : 8 + y1, :] = p * r1 + q * r0

    def from_buffer(buf, base, y0, y1):
        def go(x):
            i = x - base
            fill(x, y0, y1, buf[0, i], buf[1, i], buf[2, i], buf[3, i], buf[4, i].astype(jnp.int32))
        return go

    planes(0, HALO, from_buffer(xlo, 0, 0, ey))
    planes(HALO + cx, ex, from_buffer(xhi, HALO + cx, 0, ey))
    y0, y1 = HALO, HALO + cy

    def inner(x, acc):
        i = x - HALO
        r0, r1 = rhs[0, i], rhs[1, i]
        from_buffer(ylo, HALO, 0, HALO)(x)
        from_buffer(yhi, HALO, HALO + cy, ey)(x)
        a = agg[i]
        fill(x, y0, y1, r0, r1, wave[i], layer[i].astype(F32), a)
        lane = lanes(a.shape)
        low = jnp.zeros(a.shape, jnp.int32)
        step = a.shape[1] // 2
        while step >= 1:
            probe = low + step
            val = jnp.take_along_axis(a, probe - 1, axis=1, mode="promise_in_bounds")
            low = jnp.where(val <= lane, probe, low)
            step //= 2
        val = jnp.take_along_axis(a, low, axis=1, mode="promise_in_bounds")
        low = jnp.where(val <= lane, low + 1, low)
        ends[i] = jnp.maximum(low - 1, 0)
        return acc + fold8(r0 * r0 + r1 * r1)

    sq = planes(HALO, HALO + cx, inner, jnp.zeros((8, 128), F32))

    def u_at(x, y0, y1):
        return u[0, x, y0:y1, :], u[1, x, y0:y1, :]

    g0, g1 = second_passes(f, g, u_at, (diag, absorb, sre, sim), HALO - 2, own, ends, t_ref, s_ref, ey)
    spread_rhs(g0, g1, cols, pad, out_ref, scalar_row([(40, sq)]), grid)


def step_kernel(j, grid, own, *refs):
    refs = list(refs)
    take_refs = lambda k: [refs.pop(0) for _ in range(k)]
    rcv, diag, absorb, sre, sim, ids, ends, cols, t_in, u_in, s_in = take_refs(11)
    m_old, v_old, z_old, c_old = take_refs(j), take_refs(j), take_refs(j), take_refs(j)
    last = j == ITERS - 1
    m_out = None if last else refs.pop(0)
    v_out, z_out, c_out, h_out = take_refs(4)
    if not last:
        u_out, s_out, t_out = take_refs(3)
    out_ref = refs.pop(0)
    pc = refs.pop(0)
    if not last:
        f, u, pad = take_refs(3)
    cx, cy = own
    ey = cy + 2 * HALO
    halo = HALO - 2 - 2 * j
    y0, y1 = HALO, HALO + cy

    zero_pads(pc, ey)
    if not last:
        zero_pads(f, ey)
    row = jnp.sum(rcv[...], axis=0, keepdims=True)
    scal = row[:, 256:384]
    h_out[...] = scal
    sq = pick(scal, 40)
    hr = [pick(scal, 32 + 2 * i) for i in range(j)]
    hi = [pick(scal, 33 + 2 * i) for i in range(j)]
    for i in range(j):
        sq = sq - (hr[i] * hr[i] + hi[i] * hi[i])
    inv = 1.0 / jnp.sqrt(jnp.maximum(sq, 0.0) + epsilon)
    table = row
    for i in range(j):
        old = c_old[i][...]
        wide = lambda v: jnp.concatenate([v[0:1]] * 3, axis=1)
        table = table - (wide(hr[i]) * old + wide(hi[i]) * turn_rows(old))
    table = table * jnp.concatenate([inv[0:1]] * 3, axis=1)
    c_out[...] = table

    def like(v, rows):
        return jnp.concatenate([v] * (rows // 8), axis=0)

    def combine(new, old, x, rows):
        a0, a1 = new
        for i in range(j):
            b0, b1 = old(i)
            r, q = like(hr[i], rows), like(hi[i], rows)
            a0 = a0 - (r * b0 - q * b1)
            a1 = a1 - (r * b1 + q * b0)
        s = like(inv, rows)
        return a0 * s, a1 * s

    def prolong(dx):
        def go(x):
            for dy, lo, hi_ in ((0, 0, HALO), (1, HALO, HALO + cy), (2, HALO + cy, ey)):
                n = dx * 3 + dy
                src = table[:, 128 * (n // 4) : 128 * (n // 4) + 128]
                index = ids[x, lo:hi_, :] + 32 * (n % 4)
                pc[0, x, 8 + lo : 8 + hi_, :] = take(src, index)
                pc[1, x, 8 + lo : 8 + hi_, :] = take(src, index + AGG)
        return go

    planes(HALO - halo - 1, HALO, prolong(0))
    planes(HALO, HALO + cx, prolong(1))
    planes(HALO + cx, HALO + cx + halo + 1, prolong(2))

    def image_plane(x, lo, hi_):
        a0, a1 = operate_plane(pc, diag, absorb, x, lo, hi_)
        m0, m1 = combine(
            (t_in[0, x, lo:hi_, :], t_in[1, x, lo:hi_, :]),
            lambda i: (m_old[i][0, x, lo:hi_, :], m_old[i][1, x, lo:hi_, :]),
            x, hi_ - lo,
        )
        if not last:
            m_out[0, x, lo:hi_, :], m_out[1, x, lo:hi_, :] = m0, m1
        u0, u1 = m0 + a0, m1 + a1
        if not last:
            p, q = sre[x, lo:hi_, :], sim[x, lo:hi_, :]
            u[0, x, lo:hi_, :], u[1, x, lo:hi_, :] = u0, u1
            f[0, x, 8 + lo : 8 + hi_, :] = p * u0 - q * u1
            f[1, x, 8 + lo : 8 + hi_, :] = p * u1 + q * u0
        return u0, u1

    if halo > 0:
        edge = lambda x: (image_plane(x, 0, ey), None)[1]
        planes(HALO - halo, HALO, edge)
        planes(HALO + cx, HALO + cx + halo, edge)

    def middle(x, acc):
        i = x - HALO
        if halo > 0:
            u0, u1 = image_plane(x, 0, ey)
            u0, u1 = u0[y0:y1], u1[y0:y1]
        else:
            u0, u1 = image_plane(x, y0, y1)
        if not last:
            u_out[0, i], u_out[1, i] = u0, u1
        v0, v1 = combine((u_in[0, i], u_in[1, i]), lambda k: (v_old[k][0, i], v_old[k][1, i]), x, cy)
        v_out[0, i], v_out[1, i] = v0, v1
        z0, z1 = combine((s_in[0, i], s_in[1, i]), lambda k: (z_old[k][0, i], z_old[k][1, i]), x, cy)
        z_out[0, i], z_out[1, i] = z0, z1
        new = []
        for k in range(j + 1):
            b0, b1 = (v0, v1) if k == j else (v_old[k][0, i], v_old[k][1, i])
            new.append(fold8(b0 * u0 + b1 * u1))
            new.append(fold8(b0 * u1 - b1 * u0))
        new.append(fold8(u0 * u0 + u1 * u1))
        return tuple(a + b for a, b in zip(acc, new))

    zero = jnp.zeros((8, 128), F32)
    acc = planes(HALO, HALO + cx, middle, (zero,) * (2 * j + 3))
    items = [(32 + k, acc[k]) for k in range(2 * j + 2)] + [(40, acc[-1])]
    scalars = scalar_row(items)
    if last:
        n = out_ref.shape[0]
        for r in range(2):
            out_ref[:, 128 * r : 128 * r + 128] = jnp.zeros((n, 128), F32)
        out_ref[:, 256:384] = jnp.broadcast_to(scalars, (n, 128))
        return

    def u_at(x, lo, hi_):
        return u[0, x, lo:hi_, :], u[1, x, lo:hi_, :]

    g0, g1 = second_passes(f, pc, u_at, (diag, absorb, sre, sim), halo - 2, own, ends, t_out, s_out, ey)
    spread_rhs(g0, g1, cols, pad, out_ref, scalars, grid)


def cmul(a, b):
    return a[0] * b[0] - a[1] * b[1], a[0] * b[1] + a[1] * b[0]


def finish_kernel(own, *refs):
    rcv, ids = refs[0], refs[1]
    z = refs[2 : 2 + ITERS]
    c = refs[2 + ITERS : 2 + 2 * ITERS]
    rows = refs[2 + 2 * ITERS : 2 + 3 * ITERS]
    sol, hess = refs[2 + 3 * ITERS :]
    cx, cy = own
    final = jnp.sum(rcv[:, 256:384], axis=0, keepdims=True)
    scal = [r[...] for r in rows] + [final]
    beta = jnp.sqrt(pick(scal[0], 40) + epsilon)
    upper = []
    sub = []
    for j in range(ITERS):
        row = scal[j + 1]
        col = [(pick(row, 32 + 2 * i), pick(row, 33 + 2 * i)) for i in range(j + 1)]
        sq = pick(row, 40)
        for a, b in col:
            sq = sq - (a * a + b * b)
        upper.append(col)
        sub.append(jnp.sqrt(jnp.maximum(sq, 0.0) + epsilon))
    r_i = lax.broadcasted_iota(jnp.int32, (8, 128), 0)
    c_i = lanes((8, 128))
    for comp in range(2):
        block = jnp.zeros((8, 128), F32)
        for j in range(ITERS):
            for i in range(j + 1):
                block = jnp.where((r_i == i) & (c_i == j), upper[j][i][comp], block)
            if comp == 0:
                block = jnp.where((r_i == j + 1) & (c_i == j), sub[j], block)
        hess[comp] = block[0 : ITERS + 1, 0:ITERS]
    zero = jnp.zeros((8, 128), F32)
    target = [(beta, zero)]
    rot = []
    tri = []
    for j in range(ITERS):
        col = list(upper[j])
        for i in range(j):
            cr, ci, s = rot[i]
            a, b = col[i], col[i + 1]
            up = cmul((cr, -ci), a)
            dn = cmul((cr, ci), b)
            col[i] = (up[0] + s * b[0], up[1] + s * b[1])
            col[i + 1] = (dn[0] - s * a[0], dn[1] - s * a[1])
        a = col[j]
        big = jnp.sqrt(a[0] * a[0] + a[1] * a[1] + sub[j] * sub[j])
        w = 1.0 / big
        cr, ci, s = a[0] * w, a[1] * w, sub[j] * w
        rot.append((cr, ci, s))
        g = target[j]
        target[j] = cmul((cr, -ci), g)
        target.append((-s * g[0], -s * g[1]))
        col[j] = big
        tri.append(col)
    y = [None] * ITERS
    for j in reversed(range(ITERS)):
        a0, a1 = target[j]
        for k in range(j + 1, ITERS):
            b = cmul(tri[k][j], y[k])
            a0, a1 = a0 - b[0], a1 - b[1]
        w = 1.0 / tri[j][j]
        y[j] = (a0 * w, a1 * w)
    table = jnp.zeros((1, 128), F32)
    for j in range(ITERS):
        old = c[j][:, 128:256]
        table = table + (y[j][0][0:1] * old + y[j][1][0:1] * turn(old))

    def like(v):
        return jnp.concatenate([v] * (cy // 8), axis=0)

    def go(i):
        index = ids[HALO + i, HALO : HALO + cy, :]
        a0, a1 = take(table, index), take(table, index + AGG)
        for j in range(ITERS):
            b = cmul((like(y[j][0]), like(y[j][1])), (z[j][0, i], z[j][1, i]))
            a0, a1 = a0 + b[0], a1 + b[1]
        sol[0, i], sol[1, i] = a0, a1

    planes(0, cx, go)


def shape(*dims, dtype=F32):
    return jax.ShapeDtypeStruct(dims, dtype)


def call(kernel, outs, scratch, args, name, flops=200_000_000):
    vm = pl.BlockSpec(memory_space=pltpu.VMEM)
    return pl.pallas_call(
        kernel,
        out_shape=outs,
        in_specs=[vm] * len(args),
        out_specs=[vm] * len(outs),
        scratch_shapes=scratch,
        compiler_params=pltpu.CompilerParams(vmem_limit_bytes=VLIMIT),
        cost_estimate=pl.CostEstimate(flops=flops, bytes_accessed=1_000_000, transcendentals=0),
        name=name,
    )(*args)


def exchange(x):
    return lax.all_to_all(x, AXES, 0, 0, tiled=True)


def body(right_side, wavenumber, pml_layer, aggregate, coarse_inverse):
    gx, gy = lax.axis_size("gx"), lax.axis_size("gy")
    n = gx * gy
    cx, cy, cz = wavenumber.shape
    own = (cx, cy)
    ex, ey = cx + 2 * HALO, cy + 2 * HALO
    grid = (gx, gy)
    margin = -(-(gy + 1) // 8) * 8

    fields = jnp.concatenate(
        [right_side, wavenumber[None], pml_layer.astype(F32)[None], aggregate.astype(F32)[None]], 0
    )

    def swap(block, axis, dim):
        count = lax.axis_size(axis)
        up = [(i, i + 1) for i in range(count - 1)]
        down = [(b, a) for a, b in up]
        size = block.shape[dim]
        low = lax.ppermute(lax.slice_in_dim(block, size - HALO, size, axis=dim), axis, up)
        high = lax.ppermute(lax.slice_in_dim(block, 0, HALO, axis=dim), axis, down)
        return low, high

    ylo, yhi = swap(fields, "gy", 2)
    inverse = coarse_inverse.reshape(2, AGG, n, AGG).transpose(2, 3, 0, 1).reshape(n, 2 * AGG * AGG)
    cols = exchange(inverse)
    edges = jnp.concatenate([ylo, fields, yhi], axis=2)
    xlo, xhi = swap(edges, "gx", 1)

    ext = shape(ex, ey, cz)
    ext2 = shape(2, ex, ey, cz)
    mine = shape(2, cx, cy, cz)
    chunk = shape(n, 384)
    tab = shape(1, 384)
    padded = pltpu.VMEM((2, ex, ey + 16, cz), F32)
    wide = pltpu.VMEM((2, ex, ey, cz), F32)
    pad = pltpu.VMEM((n + 2 * margin, 128), F32)

    diag, absorb, sre, sim, ids, ends, t, s, send = call(
        functools.partial(start_kernel, grid, own),
        [ext, ext, ext, ext, shape(ex, ey, cz, dtype=jnp.int32), shape(cx, cy, cz, dtype=jnp.int32), ext2, mine, chunk],
        [wide, padded, padded, pad],
        [right_side, wavenumber, pml_layer, aggregate, ylo, yhi, xlo, xhi, cols],
        "start",
    )
    u = right_side
    ms, vs, zs, cs, hs = [], [], [], [], []
    for j in range(ITERS):
        got = exchange(send)
        last = j == ITERS - 1
        args = [got, diag, absorb, sre, sim, ids, ends, cols, t, u, s] + ms + vs + zs + cs
        outs = ([] if last else [ext2]) + [mine, mine, tab, shape(1, 128)]
        scratch = [padded]
        if not last:
            outs += [mine, mine, ext2]
            scratch += [padded, wide, pad]
        outs += [chunk]
        res = list(call(functools.partial(step_kernel, j, grid, own), outs, scratch, args, f"step{j}"))
        if not last:
            ms.append(res.pop(0))
        vs.append(res.pop(0))
        zs.append(res.pop(0))
        cs.append(res.pop(0))
        hs.append(res.pop(0))
        if not last:
            u, s, t = res.pop(0), res.pop(0), res.pop(0)
        send = res.pop(0)
    got = exchange(send)
    sol, hess = call(
        functools.partial(finish_kernel, own),
        [mine, shape(2, ITERS + 1, ITERS)],
        [],
        [got, ids] + zs + cs + hs,
        "finish",
    )
    return sol, hess


def solution(mesh):
    return jax.shard_map(
        body,
        mesh=mesh,
        in_specs=(
            P(None, "gx", "gy", None),
            P("gx", "gy", None),
            P("gx", "gy", None),
            P("gx", "gy", None),
            P(None, ("gx", "gy"), None),
        ),
        out_specs=(P(None, "gx", "gy", None), P()),
        check_vma=False,
    )
```

time: 821 us -> 186 us (0.23); the launches traced: 810 us -> 185 us
  blocking collectives: 406 us -> 59.5 us
  other arithmetic: 135 us -> 2.41 us
  starting transfers between devices: 129 us -> 12.3 us
  Pallas kernels: 0 us -> 92.8 us
  between operations: 54.8 us -> 0.81 us
  matrix products: 39.1 us -> 0 us
  local copies, waits for them, and re-layouts: 22.3 us -> 4.64 us
  waiting for transfers between devices: 23.2 us -> 12.9 us
    psum x9 -> x0, blocking collectives: 406 us -> none  [the longest x4 189 us: coarse_fix(): whole = lax.psum(padded, ('gx', 'gy'))]
    ppermute x48 -> x4, starting transfers between devices: 129 us -> 12.3 us  [the longest x2 9.55 us: swap(): lax.ppermute(lax.slice_in_dim(block, size - HALO, size, axis=dim), axis, up)]
    pallas_call x0 -> x6, Pallas kernels: none -> 92.8 us  [call(): pl.pallas_call(kernel, out_shape=outs, in_specs=[vm] * len(args), out_spe...]
    reduce_sum x57 -> x0, other arithmetic: 91.2 us -> none  [the longest x34 64.5 us: least_squares(): weight = jnp.sum(ortho[position] * vector)]
    all_to_all x0 -> x6, blocking collectives: none -> 59.5 us  [exchange(): return lax.all_to_all(x, AXES, 0, 0, tiled=True)]
    dot_general x48 -> x0, matrix products: 39.1 us -> none  [the longest x16 27.2 us: accumulate(): lax.dot_general(piece, onehot, (((1,), (1,)), ((), ())), precision=lax.Pr...]
    sub x22 -> x0, other arithmetic: 18.5 us -> none  [the longest x10 9.83 us: complex_scale(): scale_re * field[0] - scale_im * field[1]]
    another operation x41 -> x0, other arithmetic: 18.3 us -> none  [the longest x13 13.8 us: body(): local_dots = jnp.stack([inner_local(member, image) for member in basis], 1)]
  transfers between devices with their start and end apart: 48 -> 4, of which waited for: 23 -> 2; matrix products, arithmetic and copies ran while one was open for 1% -> 1% of each run, Pallas kernels for 0% -> 0%
where the time goes in v1:
time: 186 us; the launch traced here: 185 us
  Pallas kernels  92.8 us (50%)
  blocking collectives  59.5 us (32%)
  waiting for transfers between devices  12.9 us (7%)
  starting transfers between devices  12.3 us (7%)
  local copies, waits for them, and re-layouts  4.64 us (2%)
  other arithmetic  2.41 us (1%)
    pallas_call x6, Pallas kernels, call(): pl.pallas_call(kernel, out_shape=outs, in_specs=[vm] * len(args), out_spe...  92.8 us
    all_to_all x6, blocking collectives, exchange(): return lax.all_to_all(x, AXES, 0, 0, tiled=True)  59.5 us
    ppermute x2, starting transfers between devices, swap(): lax.ppermute(lax.slice_in_dim(block, size - HALO, size, axis=dim), axis, up)  9.55 us
    ppermute x2, waiting for transfers between devices, swap(): lax.ppermute(lax.slice_in_dim(block, size - HALO, size, axis=dim), axis, up)  7.18 us
    ppermute x2, waiting for transfers between devices, swap(): high = lax.ppermute(lax.slice_in_dim(block, 0, HALO, axis=dim), axis, down)  5.75 us
  transfers between devices with their start and end apart: 4, of which 2 were waited for; matrix products, arithmetic and copies ran while one was open for 1% of the time, Pallas kernels for 0%

profile of v1, /device:TPU:0, one launch (start us, length us, event | category | flops | bytes accessed | tf_op | source)
XLA Modules:
  0.0 185.3 jit_solution(887684408333582942)
XLA Ops:
  0.6 0.0 copy-start
  0.6 0.0 copy-start.1
  0.7 1.1 convert_bitcast_fusion
  1.8 1.1 pad_maximum_fusion.1
  2.9 1.3 collective-permute-start.1
  4.2 5.5 %collective-permute-start = (f32[5,16,8,128]{3,2,1,0:T(8,128)S(1)}, f32[5,16,8,128]{3,2,1,0:T(8,128)S(1)}, u32[]{:S(2)}, u32[]{:S(2)}) collective-permute-start(f32[5,16,8,128]{3,2,1,0:T(8,128)S(1)} %get-tuple-element.91), channel_id=1, source_target_pairs={{0,1},{1,2},{2,3},{3,4},{4,5},{5,6},{6,7},{8,9},{9,10},{10,11},{11... | collective-permute-start | bytes 983048 | tf_op jit(solution)/shard_map/ppermute | solution.py:510
  9.8 5.8 %collective-permute-done.1.yhi = f32[5,16,8,128]{3,2,1,0:T(8,128)S(1)} collective-permute-done((f32[5,16,8,128]{3,2,1,0:T(8,128)S(1)}, f32[5,16,8,128]{3,2,1,0:T(8,128)S(1)}, u32[]{:S(2)}, u32[]{:S(2)}) %collective-permute-start.1) | collective-permute-done | bytes 327712 | tf_op jit(solution)/shard_map/ppermute | solution.py:511
  15.5 7.2 %collective-permute-done.ylo = f32[5,16,8,128]{3,2,1,0:T(8,128)S(1)} collective-permute-done((f32[5,16,8,128]{3,2,1,0:T(8,128)S(1)}, f32[5,16,8,128]{3,2,1,0:T(8,128)S(1)}, u32[]{:S(2)}, u32[]{:S(2)}) %collective-permute-start) | collective-permute-done | bytes 327712 | tf_op jit(solution)/shard_map/ppermute | solution.py:510
  22.7 0.0 copy-done
  22.7 0.0 copy-done.1
  22.7 0.2 pad_maximum_fusion
  22.9 0.0 copy-start.4
  22.9 1.4 fusion
  24.3 0.0 copy-start.2
  24.3 0.0 copy-start.3
  24.3 1.4 collective-permute-start.3
  25.7 4.0 %collective-permute-start.2 = (f32[5,8,48,128]{3,2,1,0:T(8,128)}, f32[5,8,48,128]{3,2,1,0:T(8,128)}, u32[]{:S(2)}, u32[]{:S(2)}) collective-permute-start(f32[5,8,48,128]{3,2,1,0:T(8,128)} %get-tuple-element.89), channel_id=1, source_target_pairs={{0,8},{8,16},{16,24},{1,9},{9,17},{17,25},{2,10},{10,18},{18,26},{... | collective-permute-start | bytes 2949128 | tf_op jit(solution)/shard_map/ppermute | solution.py:510
  29.7 0.0 copy-done.4
  29.7 0.2 reshape.21
  30.0 0.9 copy.12
  30.9 1.1 copy.13
  32.0 12.0 %all_to_all.66 = f32[32,1,512]{2,1,0:T(1,128)S(1)} all-to-all(f32[32,1,512]{2,1,0:T(1,128)S(1)} %copy.13), channel_id=1, replica_groups=mesh['gx'=4,'gy'=8] {'gx','gy'}, dimensions={0} | all-to-all | bytes 131072 | tf_op jit(solution)/shard_map/all_to_all | solution.py:489
  44.0 0.0 collective-permute-done.3.xhi
  44.0 0.0 collective-permute-done.2.xlo
  44.0 0.0 copy-done.2
  44.0 0.0 copy-done.3
  44.0 27.1 %start.1 = (f32[32,48,128]{2,1,0:T(8,128)S(1)}, f32[32,48,128]{2,1,0:T(8,128)S(1)}, f32[32,48,128]{2,1,0:T(8,128)S(1)}, f32[32,48,128]{2,1,0:T(8,128)S(1)}, s32[...) custom-call(f32[2,16,32,128]{3,2,1,0:T(8,128)S(1)} %copy-done, ...), custom_call_target="tpu_custom_call" | custom-call | flops 200000000 | bytes 1000000 | tf_op jit(solution)/shard_map/start/pallas_call | solution.py:476
  71.1 0.1 copy.14
  71.2 11.7 %all_to_all.67 = f32[32,1,384]{2,1,0:T(1,128)S(1)} all-to-all(f32[32,1,384]{2,1,0:T(1,128)S(1)} %copy.14), channel_id=1, replica_groups=mesh['gx'=4,'gy'=8] {'gx','gy'}, dimensions={0} | all-to-all | bytes 98304 | tf_op jit(solution)/shard_map/all_to_all | solution.py:489
  82.9 21.0 %step0.1 = (f32[2,32,48,128]{3,2,1,0:T(8,128)S(1)}, f32[2,16,32,128]{3,2,1,0:T(8,128)S(1)}, f32[2,16,32,128]{3,2,1,0:T(8,128)S(1)}, f32[1,384]{1,0:T(1,128)S(1)}...) custom-call(f32[32,384]{1,0:T(8,128)S(1)} %bitcast.37, ...), custom_call_target="tpu_custom_call" | custom-call | flops 200000000 | bytes 1000000 | tf_op jit(solution)/shard_map/step0/pallas_call | solution.py:476
  104.0 0.1 copy.15
  104.0 8.9 %all_to_all.68 = f32[32,1,384]{2,1,0:T(1,128)S(1)} all-to-all(f32[32,1,384]{2,1,0:T(1,128)S(1)} %copy.15), channel_id=1, replica_groups=mesh['gx'=4,'gy'=8] {'gx','gy'}, dimensions={0} | all-to-all | bytes 98304 | tf_op jit(solution)/shard_map/all_to_all | solution.py:489
  113.0 19.5 %step1.1 = (f32[2,32,48,128]{3,2,1,0:T(8,128)S(1)}, f32[2,16,32,128]{3,2,1,0:T(8,128)S(1)}, f32[2,16,32,128]{3,2,1,0:T(8,128)S(1)}, f32[1,384]{1,0:T(1,128)S(1)}...) custom-call(f32[32,384]{1,0:T(8,128)S(1)} %bitcast.38, ...), custom_call_target="tpu_custom_call" | custom-call | flops 200000000 | bytes 1000000 | tf_op jit(solution)/shard_map/step1/pallas_call | solution.py:476
  132.5 0.1 copy.16
  132.6 8.9 %all_to_all.69 = f32[32,1,384]{2,1,0:T(1,128)S(1)} all-to-all(f32[32,1,384]{2,1,0:T(1,128)S(1)} %copy.16), channel_id=1, replica_groups=mesh['gx'=4,'gy'=8] {'gx','gy'}, dimensions={0} | all-to-all | bytes 98304 | tf_op jit(solution)/shard_map/all_to_all | solution.py:489
  141.5 18.0 %step2.1 = (f32[2,32,48,128]{3,2,1,0:T(8,128)S(1)}, f32[2,16,32,128]{3,2,1,0:T(8,128)S(1)}, f32[2,16,32,128]{3,2,1,0:T(8,128)S(1)}, f32[1,384]{1,0:T(1,128)S(1)}...) custom-call(f32[32,384]{1,0:T(8,128)S(1)} %bitcast.39, ...), custom_call_target="tpu_custom_call" | custom-call | flops 200000000 | bytes 1000000 | tf_op jit(solution)/shard_map/step2/pallas_call | solution.py:476
  159.5 0.1 copy.17
  159.5 8.9 %all_to_all.70 = f32[32,1,384]{2,1,0:T(1,128)S(1)} all-to-all(f32[32,1,384]{2,1,0:T(1,128)S(1)} %copy.17), channel_id=1, replica_groups=mesh['gx'=4,'gy'=8] {'gx','gy'}, dimensions={0} | all-to-all | bytes 98304 | tf_op jit(solution)/shard_map/all_to_all | solution.py:489
  168.5 4.7 %step3.1 = (f32[2,16,32,128]{3,2,1,0:T(8,128)}, f32[2,16,32,128]{3,2,1,0:T(8,128)S(1)}, f32[1,384]{1,0:T(1,128)S(1)}, f32[1,128]{1,0:T(1,128)S(1)}, f32[32,384]{1,0:T(8,128)S(1)}) custom-call(f32[32,384]{1,0:T(8,128)S(1)} %bitcast.41, f32[32,48,128]{2,1,0:T(8,128)S(1)} %get-tuple-element.43.refs_1_, f32[32,48,128]{2,1,0:T(8,128)S(1)} %get-tuple-element.44.refs_2_, ...), custom_call_target="tpu_custom_call" | custom-call | flops 200000000 | bytes 1000000 | tf_op jit(solution)/shard_map/step3/pallas_call | solution.py:476
  173.1 0.1 copy.18
  173.2 8.9 %all_to_all.71 = f32[32,1,384]{2,1,0:T(1,128)S(1)} all-to-all(f32[32,1,384]{2,1,0:T(1,128)S(1)} %copy.18), channel_id=1, replica_groups=mesh['gx'=4,'gy'=8] {'gx','gy'}, dimensions={0} | all-to-all | bytes 98304 | tf_op jit(solution)/shard_map/all_to_all | solution.py:489
  182.1 2.5 %finish.1 = (f32[2,16,32,128]{3,2,1,0:T(8,128)}, f32[2,5,4]{2,1,0:T(8,128)S(1)}) custom-call(f32[32,384]{1,0:T(8,128)S(1)} %bitcast.40, s32[32,48,128]{2,1,0:T(8,128)S(1)} %get-tuple-element.47.refs_5_.refs_1_, f32[2,16,32,128]{3,2,1,0:T(8,128)S(1)} %get-tuple-element.57.refs_13_.refs_15_.refs_17_.refs_2_, ...), custom_call_target="tpu_custom_call" | custom-call | flops 200000000 | bytes 1000000 | tf_op jit(solution)/shard_map/finish/pallas_call | solution.py:476
  184.7 0.7 copy.19
  (6 shorter events, 0.0 us)
Async XLA Ops:
  0.6 22.1 %copy-start = (f32[2,16,32,128]{3,2,1,0:T(8,128)S(1)}, f32[2,16,32,128]{3,2,1,0:T(8,128)}, u32[]{:S(2)}) copy-start(f32[2,16,32,128]{3,2,1,0:T(8,128)} %refs_9_.1) | copy-start | bytes 1572868
  0.6 22.1 %copy-start.1 = (f32[16,32,128]{2,1,0:T(8,128)S(1)}, f32[16,32,128]{2,1,0:T(8,128)}, u32[]{:S(2)}) copy-start(f32[16,32,128]{2,1,0:T(8,128)} %wave.1) | copy-start | bytes 786436
  2.9 12.6 %collective-permute-start.1 = (f32[5,16,8,128]{3,2,1,0:T(8,128)S(1)}, f32[5,16,8,128]{3,2,1,0:T(8,128)S(1)}, u32[]{:S(2)}, u32[]{:S(2)}) collective-permute-start(f32[5,16,8,128]{3,2,1,0:T(8,128)S(1)} %get-tuple-element.90), channel_id=1, source_target_pairs={{1,0},{2,1},{3,2},{4,3},{5,4},{6,5},{7,6},{9,8},{10,9},{11,10},{12... | collective-permute-start | bytes 983048 | tf_op jit(solution)/shard_map/ppermute | solution.py:511
  4.2 18.5 %collective-permute-start = (f32[5,16,8,128]{3,2,1,0:T(8,128)S(1)}, f32[5,16,8,128]{3,2,1,0:T(8,128)S(1)}, u32[]{:S(2)}, u32[]{:S(2)}) collective-permute-start(f32[5,16,8,128]{3,2,1,0:T(8,128)S(1)} %get-tuple-element.91), channel_id=1, source_target_pairs={{0,1},{1,2},{2,3},{3,4},{4,5},{5,6},{6,7},{8,9},{9,10},{10,11},{11... | collective-permute-start | bytes 983048 | tf_op jit(solution)/shard_map/ppermute | solution.py:510
  22.9 6.9 %copy-start.4 = (f32[2,16,512]{2,1,0:T(8,128)S(1)}, f32[2,16,512]{2,1,0:T(8,128)}, u32[]{:S(2)}) copy-start(f32[2,16,512]{2,1,0:T(8,128)} %param.9) | copy-start | bytes 196612
  24.3 19.7 %copy-start.2 = (s32[16,32,128]{2,1,0:T(8,128)S(1)}, s32[16,32,128]{2,1,0:T(8,128)}, u32[]{:S(2)}) copy-start(s32[16,32,128]{2,1,0:T(8,128)} %layer.1) | copy-start | bytes 786436
  24.3 19.7 %copy-start.3 = (s32[16,32,128]{2,1,0:T(8,128)S(1)}, s32[16,32,128]{2,1,0:T(8,128)}, u32[]{:S(2)}) copy-start(s32[16,32,128]{2,1,0:T(8,128)} %agg.1) | copy-start | bytes 786436
  24.3 19.6 %collective-permute-start.3 = (f32[5,8,48,128]{3,2,1,0:T(8,128)}, f32[5,8,48,128]{3,2,1,0:T(8,128)S(1)}, u32[]{:S(2)}, u32[]{:S(2)}) collective-permute-start(f32[5,8,48,128]{3,2,1,0:T(8,128)} %get-tuple-element.88), channel_id=1, source_target_pairs={{8,0},{16,8},{24,16},{9,1},{17,9},{25,17},{10,2},{18,10},{26,18},{... | collective-permute-start | bytes 2949128 | tf_op jit(solution)/shard_map/ppermute | solution.py:511
  25.7 18.2 %collective-permute-start.2 = (f32[5,8,48,128]{3,2,1,0:T(8,128)}, f32[5,8,48,128]{3,2,1,0:T(8,128)}, u32[]{:S(2)}, u32[]{:S(2)}) collective-permute-start(f32[5,8,48,128]{3,2,1,0:T(8,128)} %get-tuple-element.89), channel_id=1, source_target_pairs={{0,8},{8,16},{16,24},{1,9},{9,17},{17,25},{2,10},{10,18},{18,26},{... | collective-permute-start | bytes 2949128 | tf_op jit(solution)/shard_map/ppermute | solution.py:510

commit v2 on v1

v2 whole, which is shorter than its diff:
```python
import functools

import jax
import jax.numpy as jnp
from jax import lax
from jax.experimental import pallas as pl
from jax.experimental.pallas import tpu as pltpu
from jax.sharding import PartitionSpec as P


ITERS = 4
HALO = 2 * ITERS
NEAR = 2
AXES = ("gx", "gy")
AGG = 16
damping = 0.8
pml_strength = 3.0
epsilon = 1e-06
F32 = jnp.float32
VLIMIT = 16 * 1024 * 1024


def lanes(shape):
    return lax.broadcasted_iota(jnp.int32, shape, len(shape) - 1)


def turn(x):
    odd = (lanes(x.shape) // AGG) % 2 == 1
    return jnp.where(odd, pltpu.roll(x, AGG, 1), -pltpu.roll(x, x.shape[1] - AGG, 1))


def turn_rows(x):
    parts = [turn(x[:, i : i + 128]) for i in range(0, x.shape[1], 128)]
    return jnp.concatenate(parts, axis=1)


def pick(row, lane):
    return jnp.broadcast_to(row[:, lane : lane + 1], (8, 128))


def take(table, index):
    rows = index.shape[0]
    src = jnp.broadcast_to(table, (rows, 128))
    return jnp.take_along_axis(src, index, axis=1, mode="promise_in_bounds")


def planes(lo, hi, fn, carry=None, width=8):
    count = hi - lo
    step = max(d for d in range(1, count + 1) if count % d == 0 and d <= width + width // 2)
    if step * 2 < width and count > width:
        step = width
    whole = count // step * step

    def go(i, c):
        for k in range(step):
            x = lo + i * step + k
            if carry is None:
                fn(x)
            else:
                c = fn(x, c)
        return c

    c = 0 if carry is None else carry
    if whole // step == 1:
        c = go(0, c)
    else:
        c = lax.fori_loop(0, whole // step, go, c)
    for x in range(lo + whole, hi):
        if carry is None:
            fn(x)
        else:
            c = fn(x, c)
    return c


def stencil(ref, c, x, y0, y1):
    mid = ref[c, x, 8 + y0 : 8 + y1, :]
    total = (
        ref[c, x - 1, 8 + y0 : 8 + y1, :]
        + ref[c, x + 1, 8 + y0 : 8 + y1, :]
        + ref[c, x, 7 + y0 : 7 + y1, :]
        + ref[c, x, 9 + y0 : 9 + y1, :]
    )
    lane = lanes(mid.shape)
    last = mid.shape[-1] - 1
    total = total + jnp.where(lane == 0, 0.0, pltpu.roll(mid, 1, 1))
    total = total + jnp.where(lane == last, 0.0, pltpu.roll(mid, last, 1))
    return mid, total


def operate_plane(ref, k, coefs, y0, y1):
    refs, i = coefs
    d = refs[0][i, y0:y1, :]
    a = refs[1][i, y0:y1, :]
    m0, t0 = stencil(ref, 0, k, y0, y1)
    m1, t1 = stencil(ref, 1, k, y0, y1)
    return d * m0 - t0 + a * m1, d * m1 - t1 - a * m0


def fold8(x):
    out = x[0:8]
    for i in range(8, x.shape[0], 8):
        out = out + x[i : i + 8]
    return out


def keep_split(ref, c, i, x):
    top = x.astype(jnp.bfloat16)
    ref[c, i, :, 0:128] = top
    ref[c, i, :, 128:256] = (x - top.astype(F32)).astype(jnp.bfloat16)


def restrict(split, ends, own):
    cx, cy = own
    r = lax.broadcasted_iota(jnp.int32, (256, 128), 0) % 128
    ones = jnp.where(r <= lanes((256, 128)), 1.0, 0.0).astype(jnp.bfloat16)
    per = 4
    out = []
    for c in range(2):
        acc = jnp.zeros((8, 128), F32)
        for i in range(0, cx, per):
            block = split[c, i : i + per].reshape(cy * per, 256)
            sums = jnp.dot(block, ones, preferred_element_type=F32)
            for k in range(per):
                part = sums[cy * k : cy * (k + 1)]
                acc = acc + fold8(jnp.take_along_axis(part, ends[i + k], axis=1, mode="promise_in_bounds"))
        out.append(acc)
    return out


def spread_rhs(g0, g1, cols_ref, pad_ref, out_ref, scalars, grid):
    gx, gy = grid
    n = gx * gy
    lane = lanes((1, 128))
    rows = []
    for g in (g0, g1):
        total = jnp.sum(g, axis=0, keepdims=True)
        rows.append(jnp.where(lane == 0, total, total - pltpu.roll(total, 1, 1)))
    z = []
    for row in rows:
        acc = None
        for q in range(4):
            weight = take(row, lanes((8, 128)) // 32 + 4 * q)[0:1]
            term = cols_ref[pl.ds(q, n, stride=4), :] * weight
            acc = term if acc is None else acc + term
        acc = acc + pltpu.roll(acc, 64, 1)
        z.append(acc + pltpu.roll(acc, 32, 1))
    whole = z[0] + turn(z[1])
    margin = (pad_ref.shape[0] - n) // 2
    pad_ref[0:margin, :] = jnp.zeros((margin, 128), F32)
    pad_ref[margin + n : 2 * margin + n, :] = jnp.zeros((margin, 128), F32)
    pad_ref[margin : margin + n, :] = whole
    place = lax.broadcasted_iota(jnp.int32, (n, 128), 0) % gy
    group = lanes((n, 128)) // 32
    outs = [jnp.zeros((n, 128), F32) for _ in range(3)]
    for dx in (-1, 0, 1):
        for dy in (-1, 0, 1):
            k = (dx + 1) * 3 + dy + 1
            start = margin + dx * gy + dy
            piece = pad_ref[start : start + n, :]
            ok = (group == k % 4) & (place + dy >= 0) & (place + dy < gy)
            outs[k // 4] = jnp.where(ok, piece, outs[k // 4])
    outs[2] = outs[2] + jnp.broadcast_to(scalars, (n, 128))
    for r in range(3):
        out_ref[:, 128 * r : 128 * (r + 1)] = outs[r]


def scalar_row(items):
    lane = lanes((1, 128))
    row = jnp.zeros((1, 128), F32)
    for where, acc in items:
        s = jnp.sum(jnp.sum(acc, axis=0, keepdims=True), axis=1, keepdims=True)
        row = jnp.where(lane == where, jnp.broadcast_to(s, (1, 128)), row)
    return row


def smooth_plane(f, g, u, k, coefs, y0, y1):
    a0, a1 = operate_plane(f, k, coefs, y0, y1)
    e0, e1 = u[0, k, y0:y1, :] - a0, u[1, k, y0:y1, :] - a1
    refs, i = coefs
    p, q = refs[2][i, y0:y1, :], refs[3][i, y0:y1, :]
    g[0, k, 8 + y0 : 8 + y1, :] = f[0, k, 8 + y0 : 8 + y1, :] + (p * e0 - q * e1)
    g[1, k, 8 + y0 : 8 + y1, :] = f[1, k, 8 + y0 : 8 + y1, :] + (p * e1 + q * e0)


def pairs(lo, hi, size, fn, low, high):
    if hi > lo:
        def go(x):
            fn(x, low(x))
            y = size - 1 - x
            fn(y, high(y))

        planes(lo, hi, go, width=4)


def centre(f, g, u, t, t_rim, places, halo, s, edge, split, ends, own, rows, t_rows):
    mine, low, high = places
    cx, cy = own
    size = cx + 2 * HALO
    y0, y1 = HALO, HALO + cy
    r0, r1 = t_rows
    pairs(HALO - halo + 1, HALO, size, lambda k, c: smooth_plane(f, g, u, k, c, *rows), low, high)
    planes(HALO, HALO + cx, lambda x: smooth_plane(f, g, u, x, mine(x), *rows))

    def outer(k, c):
        a0, a1 = operate_plane(g, k, c, r0, r1)
        t_rim[0, c[1], r0:r1, :], t_rim[1, c[1], r0:r1, :] = a0, a1

    pairs(HALO - halo + 2, HALO, size, outer, low, high)

    def middle(x):
        i = x - HALO
        a0, a1 = operate_plane(g, x, mine(x), r0, r1)
        t[0, i, r0:r1, :], t[1, i, r0:r1, :] = a0, a1
        lo = y0 - r0
        s[0, i] = g[0, x, 8 + y0 : 8 + y1, :]
        s[1, i] = g[1, x, 8 + y0 : 8 + y1, :]
        keep_split(split, 0, i, u[0, x, y0:y1, :] - a0[lo : lo + cy])
        keep_split(split, 1, i, u[1, x, y0:y1, :] - a1[lo : lo + cy])

    planes(HALO, HALO + cx, middle)
    if edge is not None:
        for c in range(2):
            for k, x in enumerate((HALO, HALO + cx - 1)):
                edge[0, c, k] = f[c, x]
                edge[1, c, k] = g[c, x]
    return restrict(split, ends, own)


def rim_pair(lo, hi, fn):
    if hi > lo:
        def go(x):
            fn(x, x)
            y = lo + hi - 1 - x
            fn(2 * HALO + 1 - y, 2 * HALO - 1 - y)

        planes(lo, hi, go, width=4)


def fringe(f, g, u, t, rim, edge, halo, rows):
    for c in range(2):
        for k, x in enumerate((HALO, HALO + 1)):
            f[c, x] = edge[0, c, k]
            g[c, x] = edge[1, c, k]
    rim_pair(HALO - halo + 1, HALO, lambda k, i: smooth_plane(f, g, u, k, (rim, i), *rows))
    y0, y1 = rows

    def last(k, i):
        a0, a1 = operate_plane(g, k, (rim, i), y0, y1)
        t[0, i, y0:y1, :], t[1, i, y0:y1, :] = a0, a1

    rim_pair(HALO - halo + 2, HALO, last)


def fill(store, u, f, k, y0, y1, r0, r1, wave, layer, a):
    sq = wave * wave
    depth = layer / 3.0
    ab = sq * (pml_strength * depth * depth)
    d = 6.0 - sq
    w = jnp.where(wave > 0.0, damping / (d * d + ab * ab), 0.0)
    p, q = d * w, ab * w
    refs, i = store
    refs[0][i, y0:y1, :] = d
    refs[1][i, y0:y1, :] = ab
    refs[2][i, y0:y1, :] = p
    refs[3][i, y0:y1, :] = q
    refs[4][i, y0:y1, :] = a
    u[0, k, y0:y1, :] = r0
    u[1, k, y0:y1, :] = r1
    f[0, k, 8 + y0 : 8 + y1, :] = p * r0 - q * r1
    f[1, k, 8 + y0 : 8 + y1, :] = p * r1 + q * r0


def fill_from(store, u, f, k, buf, b, y0, y1):
    fill(store, u, f, k, y0, y1, buf[0, b], buf[1, b], buf[2, b], buf[3, b], buf[4, b].astype(jnp.int32))


def start_kernel(grid, own,
                 rhs, wave, layer, agg, ylo, yhi, xlo, xhi, cols,
                 diag, absorb, sre, sim, ids, ends, t, s, edge, out_ref,
                 n0, n1, n2, n3, n4, u, f, g, split, pad):
    cx, cy = own
    ey = cy + 2 * HALO
    refs, near = (diag, absorb, sre, sim, ids), (n0, n1, n2, n3, n4)
    mine = lambda x: (refs, x - HALO)
    low = lambda x: (near, x - HALO + NEAR)
    high = lambda x: (near, x - HALO - cx + NEAR)
    for i in range(NEAR):
        x = HALO - NEAR + i
        fill_from(low(x), u, f, x, xlo, i, 0, ey)
        x = HALO + cx + i
        fill_from(high(x), u, f, x, xhi, i, 0, ey)

    def inner(x, acc):
        i = x - HALO
        r0, r1 = rhs[0, i], rhs[1, i]
        fill_from(mine(x), u, f, x, ylo, i, 0, HALO)
        fill_from(mine(x), u, f, x, yhi, i, HALO + cy, ey)
        fill(mine(x), u, f, x, HALO, HALO + cy, r0, r1, wave[i], layer[i].astype(F32), agg[i])
        return acc + fold8(r0 * r0 + r1 * r1)

    sq = planes(HALO, HALO + cx, inner, jnp.zeros((8, 128), F32))

    def find(i):
        a = agg[i]
        lane = lanes(a.shape)
        low = jnp.zeros(a.shape, jnp.int32)
        step = a.shape[1] // 2
        while step >= 1:
            probe = low + step
            val = jnp.take_along_axis(a, probe - 1, axis=1, mode="promise_in_bounds")
            low = jnp.where(val <= lane, probe, low)
            step //= 2
        val = jnp.take_along_axis(a, low, axis=1, mode="promise_in_bounds")
        low = jnp.where(val <= lane, low + 1, low)
        ends[i] = jnp.maximum(low - 1, 0)

    planes(0, cx, find)
    g0, g1 = centre(f, g, u, t, None, (mine, low, high), 2, s, edge, split, ends, own, (0, ey), (0, ey))
    spread_rhs(g0, g1, cols, pad, out_ref, scalar_row([(40, sq)]), grid)


def start_fringe_kernel(own, got, xlo, xhi, wlo, whi, edge,
                        diag, absorb, sre, sim, ids, t, u, f, g):
    _, cy = own
    ey = cy + 2 * HALO
    rim = (diag, absorb, sre, sim, ids)
    far = HALO - NEAR

    def go(i):
        fill_from((rim, i), u, f, i, wlo, i, 0, ey)
        fill_from((rim, HALO + NEAR + i), u, f, HALO + 2 + NEAR + i, whi, i, 0, ey)

    planes(0, far, go, width=4)
    for i in range(NEAR):
        fill_from((rim, far + i), u, f, far + i, xlo, i, 0, ey)
        fill_from((rim, HALO + i), u, f, HALO + 2 + i, xhi, i, 0, ey)
    fringe(f, g, u, t, rim, edge, HALO, (0, ey))


def read_scalars(scal, j):
    hr = [pick(scal, 32 + 2 * i) for i in range(j)]
    hi = [pick(scal, 33 + 2 * i) for i in range(j)]
    sq = pick(scal, 40)
    for i in range(j):
        sq = sq - (hr[i] * hr[i] + hi[i] * hi[i])
    return hr, hi, 1.0 / jnp.sqrt(jnp.maximum(sq, 0.0) + epsilon)


def like(v, rows):
    return jnp.concatenate([v] * (rows // 8), axis=0)


def combine(scalars, new, old):
    hr, hi, inv = scalars
    a0, a1 = new
    rows = a0.shape[0]
    for i in range(len(hr)):
        b0, b1 = old(i)
        r, q = like(hr[i], rows), like(hi[i], rows)
        a0 = a0 - (r * b0 - q * b1)
        a1 = a1 - (r * b1 + q * b0)
    s = like(inv, rows)
    return a0 * s, a1 * s


def prolong_plane(pc, k, ids, i, table, own, dx):
    cy = own[1]
    ey = cy + 2 * HALO
    for dy, lo, hi in ((0, 0, HALO), (1, HALO, HALO + cy), (2, HALO + cy, ey)):
        n = dx * 3 + dy
        src = table[:, 128 * (n // 4) : 128 * (n // 4) + 128]
        index = ids[i, lo:hi, :] + 32 * (n % 4)
        pc[0, k, 8 + lo : 8 + hi, :] = take(src, index)
        pc[1, k, 8 + lo : 8 + hi, :] = take(src, index + AGG)


def image_plane(pc, k, coefs, t_in, m_old, scalars, lo, hi):
    i = coefs[1]
    a0, a1 = operate_plane(pc, k, coefs, lo, hi)
    m = combine(
        scalars,
        (t_in[0, i, lo:hi, :], t_in[1, i, lo:hi, :]),
        lambda n: (m_old[n][0, i, lo:hi, :], m_old[n][1, i, lo:hi, :]),
    )
    return m, (m[0] + a0, m[1] + a1)


def image_store(pc, u, f, k, coefs, t_in, m_old, scalars, m_out, lo, hi):
    m, (u0, u1) = image_plane(pc, k, coefs, t_in, m_old, scalars, lo, hi)
    refs, i = coefs
    if m_out is not None:
        m_out[0, i, lo:hi, :], m_out[1, i, lo:hi, :] = m
    p, q = refs[2][i, lo:hi, :], refs[3][i, lo:hi, :]
    u[0, k, lo:hi, :], u[1, k, lo:hi, :] = u0, u1
    f[0, k, 8 + lo : 8 + hi, :] = p * u0 - q * u1
    f[1, k, 8 + lo : 8 + hi, :] = p * u1 + q * u0
    return u0, u1


def y_rows(j, cy):
    halo = HALO - 2 - 2 * j
    if halo > 4:
        return 0, cy + 2 * HALO
    if halo > 0:
        return HALO - 4, HALO + cy + 4
    return HALO, HALO + cy


def step_kernel(j, grid, own, *refs):
    refs = list(refs)
    take_refs = lambda k: [refs.pop(0) for _ in range(k)]
    last = j == ITERS - 1
    rcv = refs.pop(0)
    home, rim = take_refs(5), take_refs(5)
    ends, cols, t_own, t_rim, u_in = take_refs(5)
    m_own, m_rim = take_refs(j), take_refs(0 if last else j)
    v_old, c_old = take_refs(j), take_refs(j)
    v_out, c_out, h_out, out_ref = take_refs(4)
    if not last:
        m_out, t, u_out, s_out = take_refs(4)
    mr_out = tr_out = None
    if j < ITERS - 2:
        mr_out, tr_out = take_refs(2)
    pc = refs.pop(0)
    if not last:
        u, f, split, pad = take_refs(4)
    cx, cy = own
    mine = lambda x: (home, x - HALO)
    low = lambda x: (rim, x)
    high = lambda x: (rim, x - cx)
    y0, y1 = HALO, HALO + cy
    rows = y_rows(j, cy)
    halo = HALO - 2 - 2 * j
    size = cx + 2 * HALO

    row = jnp.sum(rcv[...], axis=0, keepdims=True)
    scal = row[:, 256:384]
    h_out[...] = scal
    scalars = read_scalars(scal, j)
    hr, hi, inv = scalars
    wide = lambda v: jnp.concatenate([v[0:1]] * 3, axis=1)
    table = row
    for i in range(j):
        old = c_old[i][...]
        table = table - (wide(hr[i]) * old + wide(hi[i]) * turn_rows(old))
    table = table * wide(inv)
    c_out[...] = table

    def outside(x):
        prolong_plane(pc, x, rim[4], x, table, own, 0)
        y = 2 * HALO - 1 - x
        prolong_plane(pc, y + cx, rim[4], y, table, own, 2)

    planes(HALO - halo - 1, HALO, outside, width=4)
    planes(HALO, HALO + cx, lambda x: prolong_plane(pc, x, home[4], x - HALO, table, own, 1))

    def outer(k, c):
        image_store(pc, u, f, k, c, t_rim, m_rim, scalars, mr_out, *rows)

    pairs(HALO - halo, HALO, size, outer, low, high)

    def middle(x, acc):
        i = x - HALO
        if last:
            u0, u1 = image_plane(pc, x, mine(x), t_own, m_own, scalars, y0, y1)[1]
        else:
            u0, u1 = image_store(pc, u, f, x, mine(x), t_own, m_own, scalars, m_out, *rows)
            lo = y0 - rows[0]
            u0, u1 = u0[lo : lo + cy], u1[lo : lo + cy]
            u_out[0, i], u_out[1, i] = u0, u1
        v0, v1 = combine(scalars, (u_in[0, i], u_in[1, i]), lambda k: (v_old[k][0, i], v_old[k][1, i]))
        v_out[0, i], v_out[1, i] = v0, v1
        new = []
        for k in range(j + 1):
            b0, b1 = (v0, v1) if k == j else (v_old[k][0, i], v_old[k][1, i])
            new.append(fold8(b0 * u0 + b1 * u1))
            new.append(fold8(b0 * u1 - b1 * u0))
        new.append(fold8(u0 * u0 + u1 * u1))
        return tuple(a + b for a, b in zip(acc, new))

    zero = jnp.zeros((8, 128), F32)
    acc = planes(HALO, HALO + cx, middle, (zero,) * (2 * j + 3))
    items = [(32 + k, acc[k]) for k in range(2 * j + 2)] + [(40, acc[-1])]
    dots = scalar_row(items)
    if last:
        n = out_ref.shape[0]
        for r in range(2):
            out_ref[:, 128 * r : 128 * r + 128] = jnp.zeros((n, 128), F32)
        out_ref[:, 256:384] = jnp.broadcast_to(dots, (n, 128))
        return
    t_rows = rows if j < ITERS - 2 else (y0, y1)
    g0, g1 = centre(f, pc, u, t, tr_out, (mine, low, high), halo, s_out, None, split, ends, own, rows, t_rows)
    spread_rhs(g0, g1, cols, pad, out_ref, dots, grid)


def pack_kernel(rhs, wave, layer, agg, low, high, ints, sems):
    cy = wave.shape[1]
    copies = []
    for k, (out, y) in enumerate(((low, 0), (high, cy - HALO))):
        rows = pl.ds(y, HALO)
        for i, (src, dst) in enumerate((
            (rhs.at[:, :, rows, :], out.at[0:2]),
            (wave.at[:, rows, :], out.at[2]),
            (layer.at[:, rows, :], ints.at[2 * k]),
            (agg.at[:, rows, :], ints.at[2 * k + 1]),
        )):
            copies.append(pltpu.make_async_copy(src, dst, sems.at[4 * k + i]))
    for copy in copies:
        copy.start()
    for copy in copies:
        copy.wait()
    for k, out in enumerate((low, high)):
        out[3] = ints[2 * k].astype(F32)
        out[4] = ints[2 * k + 1].astype(F32)


def slab_kernel(rhs, wave, layer, agg, ylo, yhi, near_low, near_high, far_low, far_high):
    cx, cy = wave.shape[:2]
    y0, y1 = HALO, HALO + cy
    for out, lo, hi in (
        (near_low, 0, NEAR), (near_high, cx - NEAR, cx), (far_low, NEAR, HALO), (far_high, cx - HALO, cx - NEAR),
    ):
        out[:, :, 0:y0, :] = ylo[:, lo:hi]
        out[:, :, y1 : y1 + HALO, :] = yhi[:, lo:hi]
        out[0:2, :, y0:y1, :] = rhs[:, lo:hi]
        out[2, :, y0:y1, :] = wave[lo:hi]
        out[3, :, y0:y1, :] = layer[lo:hi].astype(F32)
        out[4, :, y0:y1, :] = agg[lo:hi].astype(F32)


def columns_kernel(inverse, out, turned):
    turned[:, 0:32] = inverse[...].T
    group = lanes(out.shape) // 32
    total = jnp.zeros(out.shape, F32)
    for r in range(4):
        part = turned[pl.ds(r, out.shape[0], stride=4), :]
        part = jnp.where(group == 0, part, 0.0)
        total = total + (part if r == 0 else pltpu.roll(part, 32 * r, 1))
    out[...] = total


def cmul(a, b):
    return a[0] * b[0] - a[1] * b[1], a[0] * b[1] + a[1] * b[0]


def finish_kernel(own, *refs):
    rcv, ids = refs[0], refs[1]
    z = refs[2 : 2 + ITERS]
    c = refs[2 + ITERS : 2 + 2 * ITERS]
    rows = refs[2 + 2 * ITERS : 2 + 3 * ITERS]
    sol, hess = refs[2 + 3 * ITERS :]
    cx, cy = own
    final = jnp.sum(rcv[:, 256:384], axis=0, keepdims=True)
    scal = [r[...] for r in rows] + [final]
    beta = jnp.sqrt(pick(scal[0], 40) + epsilon)
    upper = []
    sub = []
    for j in range(ITERS):
        row = scal[j + 1]
        col = [(pick(row, 32 + 2 * i), pick(row, 33 + 2 * i)) for i in range(j + 1)]
        sq = pick(row, 40)
        for a, b in col:
            sq = sq - (a * a + b * b)
        upper.append(col)
        sub.append(jnp.sqrt(jnp.maximum(sq, 0.0) + epsilon))
    r_i = lax.broadcasted_iota(jnp.int32, (8, 128), 0)
    c_i = lanes((8, 128))
    for comp in range(2):
        block = jnp.zeros((8, 128), F32)
        for j in range(ITERS):
            for i in range(j + 1):
                block = jnp.where((r_i == i) & (c_i == j), upper[j][i][comp], block)
            if comp == 0:
                block = jnp.where((r_i == j + 1) & (c_i == j), sub[j], block)
        hess[comp] = block[0 : ITERS + 1, 0:ITERS]
    zero = jnp.zeros((8, 128), F32)
    target = [(beta, zero)]
    rot = []
    tri = []
    for j in range(ITERS):
        col = list(upper[j])
        for i in range(j):
            cr, ci, s = rot[i]
            a, b = col[i], col[i + 1]
            up = cmul((cr, -ci), a)
            dn = cmul((cr, ci), b)
            col[i] = (up[0] + s * b[0], up[1] + s * b[1])
            col[i + 1] = (dn[0] - s * a[0], dn[1] - s * a[1])
        a = col[j]
        big = jnp.sqrt(a[0] * a[0] + a[1] * a[1] + sub[j] * sub[j])
        w = 1.0 / big
        cr, ci, s = a[0] * w, a[1] * w, sub[j] * w
        rot.append((cr, ci, s))
        g = target[j]
        target[j] = cmul((cr, -ci), g)
        target.append((-s * g[0], -s * g[1]))
        col[j] = big
        tri.append(col)
    y = [None] * ITERS
    for j in reversed(range(ITERS)):
        a0, a1 = target[j]
        for k in range(j + 1, ITERS):
            b = cmul(tri[k][j], y[k])
            a0, a1 = a0 - b[0], a1 - b[1]
        w = 1.0 / tri[j][j]
        y[j] = (a0 * w, a1 * w)
    table = jnp.zeros((1, 128), F32)
    for j in range(ITERS):
        old = c[j][:, 128:256]
        table = table + (y[j][0][0:1] * old + y[j][1][0:1] * turn(old))

    gamma = list(y)
    for j in reversed(range(ITERS)):
        w = 1.0 / (sub[j - 1] if j > 0 else beta)
        gamma[j] = (gamma[j][0] * w, gamma[j][1] * w)
        for i in range(j):
            b = cmul(upper[j - 1][i], gamma[j])
            gamma[i] = (gamma[i][0] - b[0], gamma[i][1] - b[1])

    def go(i):
        index = ids[i, HALO : HALO + cy, :]
        a0, a1 = take(table, index), take(table, index + AGG)
        for j in range(ITERS):
            b = cmul((like(gamma[j][0], cy), like(gamma[j][1], cy)), (z[j][0, i], z[j][1, i]))
            a0, a1 = a0 + b[0], a1 + b[1]
        sol[0, i], sol[1, i] = a0, a1

    planes(0, cx, go)


def shape(*dims, dtype=F32):
    return jax.ShapeDtypeStruct(dims, dtype)


def call(kernel, outs, scratch, args, flops=100_000_000, space=pltpu.VMEM):
    vm = pl.BlockSpec(memory_space=pltpu.VMEM)
    return pl.pallas_call(
        kernel,
        out_shape=outs,
        in_specs=[pl.BlockSpec(memory_space=space)] * len(args),
        out_specs=[vm] * len(outs),
        scratch_shapes=scratch,
        compiler_params=pltpu.CompilerParams(vmem_limit_bytes=VLIMIT),
        cost_estimate=pl.CostEstimate(flops=flops, bytes_accessed=1_000_000, transcendentals=0),
    )(*args)


def exchange(x):
    return lax.all_to_all(x, AXES, 0, 0, tiled=True)


def program(right_side, wavenumber, pml_layer, aggregate, coarse_inverse):
    gx, gy = lax.axis_size("gx"), lax.axis_size("gy")
    n = gx * gy
    cx, cy, cz = wavenumber.shape
    own = (cx, cy)
    ex, ey = cx + 2 * HALO, cy + 2 * HALO
    grid = (gx, gy)
    margin = -(-(gy + 1) // 8) * 8

    def swap(low, high, axis):
        count = lax.axis_size(axis)
        up = [(i, i + 1) for i in range(count - 1)]
        down = [(b, a) for a, b in up]
        low_in = lax.ppermute(high, axis, up)
        high_in = lax.ppermute(low, axis, down)
        return low_in, high_in

    strip = shape(5, cx, HALO, cz)
    low, high = call(
        pack_kernel, [strip, strip],
        [pltpu.VMEM((4, cx, HALO, cz), jnp.int32), pltpu.SemaphoreType.DMA((8,))],
        [pltpu.with_memory_space_constraint(x, pltpu.HBM) for x in (right_side, wavenumber, pml_layer, aggregate)],
        space=pltpu.HBM,
    )
    ylo, yhi = swap(low, high, "gy")
    (inverse,) = call(
        columns_kernel, [shape(4 * n, 128)], [pltpu.VMEM((AGG * n, 128), F32)],
        [coarse_inverse.reshape(2 * AGG, AGG * n)],
    )
    cols = exchange(inverse)
    right_side, wavenumber, pml_layer, aggregate, ylo, yhi, cols = lax.optimization_barrier(
        (right_side, wavenumber, pml_layer, aggregate, ylo, yhi, cols)
    )
    near, far = shape(5, NEAR, ey, cz), shape(5, HALO - NEAR, ey, cz)
    near_low, near_high, far_low, far_high = call(
        slab_kernel, [near, near, far, far], [],
        [right_side, wavenumber, pml_layer, aggregate, ylo, yhi],
    )
    xlo, xhi = swap(near_low, near_high, "gx")
    wlo, whi = swap(far_low, far_high, "gx")

    I32 = jnp.int32
    home = [shape(cx, ey, cz)] * 4 + [shape(cx, ey, cz, dtype=I32)]
    rim = [shape(2 * HALO, ey, cz)] * 4 + [shape(2 * HALO, ey, cz, dtype=I32)]
    home2, rim2 = shape(2, cx, ey, cz), shape(2, 2 * HALO, ey, cz)
    mine = shape(2, cx, cy, cz)
    chunk = shape(n, 384)
    edges = shape(2, 2, 2, ey + 16, cz)
    vmem = lambda *dims, dtype=F32: pltpu.VMEM(dims, dtype)
    tall = vmem(2, ex, ey + 16, cz)
    flat = vmem(2, ex, ey, cz)
    short_tall = vmem(2, 2 * HALO + 2, ey + 16, cz)
    short_flat = vmem(2, 2 * HALO + 2, ey, cz)
    pad = vmem(n + 2 * margin, 128)
    split = vmem(2, cx, cy, 256, dtype=jnp.bfloat16)
    near = [vmem(2 * NEAR, ey, cz)] * 4 + [vmem(2 * NEAR, ey, cz, dtype=I32)]

    *own_coefs, ends, t_own, s, edge, send = call(
        functools.partial(start_kernel, grid, own),
        home + [shape(cx, cy, cz, dtype=I32), home2, mine, edges, chunk],
        near + [flat, tall, tall, split, pad],
        [right_side, wavenumber, pml_layer, aggregate, ylo, yhi, xlo, xhi, cols],
    )
    got = exchange(send)
    *rim_coefs, t_rim = call(
        functools.partial(start_fringe_kernel, own),
        rim + [rim2],
        [short_flat, short_tall, short_tall],
        [got, xlo, xhi, wlo, whi, edge],
    )
    u = right_side
    ms, mrs, vs, ss, cs, hs = [], [], [], [s], [], []
    for j in range(ITERS):
        last = j == ITERS - 1
        args = [got] + own_coefs + rim_coefs + [ends, cols, t_own, t_rim, u] + ms + ([] if last else mrs) + vs + cs
        outs = [mine, shape(1, 384), shape(1, 128), chunk]
        scratch = [tall]
        if not last:
            outs += [home2, home2, mine, mine]
            if j < ITERS - 2:
                outs += [rim2, rim2]
            scratch += [flat, tall, split, pad]
        v, c, h, send, *rest = call(functools.partial(step_kernel, j, grid, own), outs, scratch, args)
        got = exchange(send)
        if not last:
            m, t_own, u, s = rest[:4]
            ms.append(m)
            ss.append(s)
            if j < ITERS - 2:
                mrs.append(rest[4])
                t_rim = rest[5]
        vs.append(v)
        cs.append(c)
        hs.append(h)
    sol, hess = call(
        functools.partial(finish_kernel, own),
        [mine, shape(2, ITERS + 1, ITERS)],
        [],
        [got, own_coefs[4]] + ss + cs + hs,
    )
    return sol, hess


def solution(mesh):
    return jax.shard_map(
        program,
        mesh=mesh,
        in_specs=(
            P(None, "gx", "gy", None),
            P("gx", "gy", None),
            P("gx", "gy", None),
            P("gx", "gy", None),
            P(None, ("gx", "gy"), None),
        ),
        out_specs=(P(None, "gx", "gy", None), P()),
        check_vma=False,
    )
```

time: 186 us -> 114 us (0.61)
  Pallas kernels: 92.8 us -> 25.5 us
  waiting for transfers between devices: 12.9 us -> 3.33 us
  blocking collectives: 59.5 us -> 69 us
  local copies, waits for them, and re-layouts: 4.64 us -> 0.99 us
  other arithmetic: 2.41 us -> 0 us
  starting transfers between devices: 12.3 us -> 14.2 us
    pallas_call x6 -> x10, Pallas kernels: 92.8 us -> 25.5 us  [call(): pl.pallas_call(kernel, out_shape=outs, in_specs=[pl.BlockSpec(memory_spac...]
    ppermute x4 -> x6, waiting for transfers between devices: 12.9 us -> 3.33 us  [the longest x3 3.33 us: swap(): high_in = lax.ppermute(low, axis, down)]
    all_to_all x6, blocking collectives: 59.5 us -> 69 us  [exchange(): return lax.all_to_all(x, AXES, 0, 0, tiled=True)]
    ppermute x4 -> x6, starting transfers between devices: 12.3 us -> 14.2 us  [the longest x3 10.3 us: swap(): low_in = lax.ppermute(high, axis, up)]
  transfers between devices with their start and end apart: 4 -> 6, of which waited for: 2 -> 1; matrix products, arithmetic and copies ran while one was open for 1% -> 0% of each run, Pallas kernels for 0% -> 4%
where the time goes in v2:
time: 114 us
  blocking collectives  69 us (61%)
  Pallas kernels  25.5 us (22%)
  starting transfers between devices  14.2 us (12%)
  waiting for transfers between devices  3.33 us (3%)
    all_to_all x6, blocking collectives, exchange(): return lax.all_to_all(x, AXES, 0, 0, tiled=True)  69 us
    pallas_call x10, Pallas kernels, call(): pl.pallas_call(kernel, out_shape=outs, in_specs=[pl.BlockSpec(memory_spac...  25.5 us
    ppermute x3, starting transfers between devices, swap(): low_in = lax.ppermute(high, axis, up)  10.3 us
    ppermute x3, starting transfers between devices, swap(): high_in = lax.ppermute(low, axis, down)  3.88 us
    ppermute x3, waiting for transfers between devices, swap(): high_in = lax.ppermute(low, axis, down)  3.33 us
  transfers between devices with their start and end apart: 6, of which 1 were waited for; matrix products, arithmetic and copies ran while one was open for 0% of the time, Pallas kernels for 4%

profile of v2, /device:TPU:0, one launch (start us, length us, event | category | flops | bytes accessed | tf_op | source)
XLA Modules:
  0.0 113.9 jit_solution(16564176173376713831)
XLA Ops:
  0.6 0.0 copy-start.4
  0.6 0.0 copy-start
  0.7 0.0 copy-start.2
  0.7 0.0 copy-start.3
  0.7 1.3 %shard_map.68 = (f32[5,16,8,128]{3,2,1,0:T(8,128)S(1)}, f32[5,16,8,128]{3,2,1,0:T(8,128)S(1)}) custom-call(f32[2,16,32,128]{3,2,1,0:T(8,128)} %refs_15_, f32[16,32,128]{2,1,0:T(8,128)} %wave.3, s32[16,32,128]{2,1,0:T(8,128)} %layer.3, s32[16,32,128]{2,1,0:T(8,128)} %agg.3), custom_call_target="tpu_custom_call" | custom-call | flops 100000000 | bytes 1000000 | tf_op jit(solution)/shard_map/pallas_call | solution.py:638
  2.0 0.0 copy-start.1
  2.0 5.1 %collective-permute-start = (f32[5,16,8,128]{3,2,1,0:T(8,128)S(1)}, f32[5,16,8,128]{3,2,1,0:T(8,128)S(1)}, u32[]{:S(2)}, u32[]{:S(2)}) collective-permute-start(f32[5,16,8,128]{3,2,1,0:T(8,128)S(1)} %get-tuple-element.62), channel_id=1, source_target_pairs={{0,1},{1,2},{2,3},{3,4},{4,5},{5,6},{6,7},{8,9},{9,10},{10,11},{11... | collective-permute-start | bytes 983048 | tf_op jit(solution)/shard_map/ppermute | solution.py:666
  7.0 1.3 %collective-permute-start.1 = (f32[5,16,8,128]{3,2,1,0:T(8,128)S(1)}, f32[5,16,8,128]{3,2,1,0:T(8,128)S(1)}, u32[]{:S(2)}, u32[]{:S(2)}) collective-permute-start(f32[5,16,8,128]{3,2,1,0:T(8,128)S(1)} %get-tuple-element.63), channel_id=1, source_target_pairs={{1,0},{2,1},{3,2},{4,3},{5,4},{6,5},{7,6},{9,8},{10,9},{11,10},{12... | collective-permute-start | bytes 983048 | tf_op jit(solution)/shard_map/ppermute | solution.py:667
  8.3 0.0 copy-done.4
  8.4 0.3 shard_map.69
  8.6 14.3 %all_to_all.67 = f32[32,4,128]{2,1,0:T(4,128)S(1)} all-to-all(f32[32,4,128]{2,1,0:T(4,128)S(1)} %bitcast.34), channel_id=1, replica_groups=mesh['gx'=4,'gy'=8] {'gx','gy'}, dimensions={0} | all-to-all | bytes 131072 | tf_op jit(solution)/shard_map/all_to_all | solution.py:650
  23.0 0.0 collective-permute-done.ylo
  23.0 0.0 collective-permute-done.1.yhi
  23.0 0.0 copy-done
  23.0 0.0 copy-done.2
  23.0 0.0 copy-done.3
  23.0 0.0 copy-done.1
  23.0 0.1 shard_map.70
  23.1 2.1 %collective-permute-start.4 = (f32[5,6,48,128]{3,2,1,0:T(8,128)S(1)}, f32[5,6,48,128]{3,2,1,0:T(8,128)S(1)}, u32[]{:S(2)}, u32[]{:S(2)}) collective-permute-start(f32[5,6,48,128]{3,2,1,0:T(8,128)S(1)} %get-tuple-element.79), channel_id=1, source_target_pairs={{0,8},{8,16},{16,24},{1,9},{9,17},{17,25},{2,10},{10,18},{18,26},{... | collective-permute-start | bytes 2211848 | tf_op jit(solution)/shard_map/ppermute | solution.py:666
  25.2 1.3 %collective-permute-start.5 = (f32[5,6,48,128]{3,2,1,0:T(8,128)S(1)}, f32[5,6,48,128]{3,2,1,0:T(8,128)S(1)}, u32[]{:S(2)}, u32[]{:S(2)}) collective-permute-start(f32[5,6,48,128]{3,2,1,0:T(8,128)S(1)} %get-tuple-element.80), channel_id=1, source_target_pairs={{8,0},{16,8},{24,16},{9,1},{17,9},{25,17},{10,2},{18,10},{26,18},{... | collective-permute-start | bytes 2211848 | tf_op jit(solution)/shard_map/ppermute | solution.py:667
  26.5 3.2 %collective-permute-start.2 = (f32[5,2,48,128]{3,2,1,0:T(8,128)S(1)}, f32[5,2,48,128]{3,2,1,0:T(8,128)S(1)}, u32[]{:S(2)}, u32[]{:S(2)}) collective-permute-start(f32[5,2,48,128]{3,2,1,0:T(8,128)S(1)} %get-tuple-element.70), channel_id=1, source_target_pairs={{0,8},{8,16},{16,24},{1,9},{9,17},{17,25},{2,10},{10,18},{18,26},{... | collective-permute-start | bytes 737288 | tf_op jit(solution)/shard_map/ppermute | solution.py:666
  29.7 1.3 %collective-permute-start.3 = (f32[5,2,48,128]{3,2,1,0:T(8,128)S(1)}, f32[5,2,48,128]{3,2,1,0:T(8,128)S(1)}, u32[]{:S(2)}, u32[]{:S(2)}) collective-permute-start(f32[5,2,48,128]{3,2,1,0:T(8,128)S(1)} %get-tuple-element.71), channel_id=1, source_target_pairs={{8,0},{16,8},{24,16},{9,1},{17,9},{25,17},{10,2},{18,10},{26,18},{... | collective-permute-start | bytes 737288 | tf_op jit(solution)/shard_map/ppermute | solution.py:667
  31.0 0.0 collective-permute-done.2.xlo
  31.0 3.3 %collective-permute-done.3.xhi = f32[5,2,48,128]{3,2,1,0:T(8,128)S(1)} collective-permute-done((f32[5,2,48,128]{3,2,1,0:T(8,128)S(1)}, f32[5,2,48,128]{3,2,1,0:T(8,128)S(1)}, u32[]{:S(2)}, u32[]{:S(2)}) %collective-permute-start.3) | collective-permute-done | bytes 245792 | tf_op jit(solution)/shard_map/ppermute | solution.py:667
  34.3 4.2 %shard_map.71 = (f32[16,48,128]{2,1,0:T(8,128)S(1)}, f32[16,48,128]{2,1,0:T(8,128)S(1)}, f32[16,48,128]{2,1,0:T(8,128)S(1)}, f32[16,48,128]{2,1,0:T(8,128)S(1)},...) custom-call(f32[2,16,32,128]{3,2,1,0:T(8,128)S(1)} %copy-done, ...), custom_call_target="tpu_custom_call" | custom-call | flops 100000000 | bytes 1000000 | tf_op jit(solution)/shard_map/pallas_call | solution.py:638
  38.6 0.1 copy.8
  38.6 18.9 %all_to_all.68 = f32[32,1,384]{2,1,0:T(1,128)S(1)} all-to-all(f32[32,1,384]{2,1,0:T(1,128)S(1)} %copy.8), channel_id=1, replica_groups=mesh['gx'=4,'gy'=8] {'gx','gy'}, dimensions={0} | all-to-all | bytes 98304 | tf_op jit(solution)/shard_map/all_to_all | solution.py:650
  57.6 0.0 collective-permute-done.4.wlo
  57.6 0.0 collective-permute-done.5.whi
  57.6 1.0 shard_map.72
  58.6 5.2 %shard_map.73 = (f32[2,16,32,128]{3,2,1,0:T(8,128)S(1)}, f32[1,384]{1,0:T(1,128)S(1)}, f32[1,128]{1,0:T(1,128)S(1)}, f32[32,384]{1,0:T(8,128)S(1)}, f32[2,16,48,...) custom-call(f32[32,384]{1,0:T(8,128)S(1)} %bitcast.29, ...), custom_call_target="tpu_custom_call" | custom-call | flops 100000000 | bytes 1000000 | tf_op jit(solution)/shard_map/pallas_call | solution.py:638
  63.8 0.1 copy.9
  63.9 8.9 %all_to_all.69 = f32[32,1,384]{2,1,0:T(1,128)S(1)} all-to-all(f32[32,1,384]{2,1,0:T(1,128)S(1)} %copy.9), channel_id=1, replica_groups=mesh['gx'=4,'gy'=8] {'gx','gy'}, dimensions={0} | all-to-all | bytes 98304 | tf_op jit(solution)/shard_map/all_to_all | solution.py:650
  72.8 4.7 %shard_map.74 = (f32[2,16,32,128]{3,2,1,0:T(8,128)S(1)}, f32[1,384]{1,0:T(1,128)S(1)}, f32[1,128]{1,0:T(1,128)S(1)}, f32[32,384]{1,0:T(8,128)S(1)}, f32[2,16,48,...) custom-call(f32[32,384]{1,0:T(8,128)S(1)} %bitcast.31, ...), custom_call_target="tpu_custom_call" | custom-call | flops 100000000 | bytes 1000000 | tf_op jit(solution)/shard_map/pallas_call | solution.py:638
  77.5 0.1 copy.10
  77.6 8.9 %all_to_all.70 = f32[32,1,384]{2,1,0:T(1,128)S(1)} all-to-all(f32[32,1,384]{2,1,0:T(1,128)S(1)} %copy.10), channel_id=1, replica_groups=mesh['gx'=4,'gy'=8] {'gx','gy'}, dimensions={0} | all-to-all | bytes 98304 | tf_op jit(solution)/shard_map/all_to_all | solution.py:650
  86.5 4.4 %shard_map.75 = (f32[2,16,32,128]{3,2,1,0:T(8,128)S(1)}, f32[1,384]{1,0:T(1,128)S(1)}, f32[1,128]{1,0:T(1,128)S(1)}, f32[32,384]{1,0:T(8,128)S(1)}, f32[2,16,48,...) custom-call(f32[32,384]{1,0:T(8,128)S(1)} %bitcast.32, ...), custom_call_target="tpu_custom_call" | custom-call | flops 100000000 | bytes 1000000 | tf_op jit(solution)/shard_map/pallas_call | solution.py:638
  90.9 0.1 copy.11
  91.0 8.9 %all_to_all.71 = f32[32,1,384]{2,1,0:T(1,128)S(1)} all-to-all(f32[32,1,384]{2,1,0:T(1,128)S(1)} %copy.11), channel_id=1, replica_groups=mesh['gx'=4,'gy'=8] {'gx','gy'}, dimensions={0} | all-to-all | bytes 98304 | tf_op jit(solution)/shard_map/all_to_all | solution.py:650
  99.9 2.8 %shard_map.76 = (f32[2,16,32,128]{3,2,1,0:T(8,128)}, f32[1,384]{1,0:T(1,128)S(1)}, f32[1,128]{1,0:T(1,128)S(1)}, f32[32,384]{1,0:T(8,128)S(1)}) custom-call(f32[32,384]{1,0:T(8,128)S(1)} %bitcast.30, f32[16,48,128]{2,1,0:T(8,128)S(1)} %get-tuple-element.74.refs_1_, f32[16,48,128]{2,1,0:T(8,128)S(1)} %get-tuple-element.75.refs_2_, ...), custom_call_target="tpu_custom_call" | custom-call | flops 100000000 | bytes 1000000 | tf_op jit(solution)/shard_map/pallas_call | solution.py:638
  102.7 0.1 copy.12
  102.8 8.9 %all_to_all.72 = f32[32,1,384]{2,1,0:T(1,128)S(1)} all-to-all(f32[32,1,384]{2,1,0:T(1,128)S(1)} %copy.12), channel_id=1, replica_groups=mesh['gx'=4,'gy'=8] {'gx','gy'}, dimensions={0} | all-to-all | bytes 98304 | tf_op jit(solution)/shard_map/all_to_all | solution.py:650
  111.7 1.5 %shard_map.77 = (f32[2,16,32,128]{3,2,1,0:T(8,128)}, f32[2,5,4]{2,1,0:T(8,128)S(1)}) custom-call(f32[32,384]{1,0:T(8,128)S(1)} %bitcast.33, s32[16,48,128]{2,1,0:T(8,128)S(1)} %get-tuple-element.78.refs_5_.refs_1_, f32[2,16,32,128]{3,2,1,0:T(8,128)S(1)} %get-tuple-element.113.refs_2_, f32[2,16,32,128]{3,2,1,0:T(8,128)S(1)} %get-tuple-element.114.refs_3_, ...), custom_call_target="tpu_custom_call" | custom-call | flops 100000000 | bytes 1000000 | tf_op jit(solution)/shard_map/pallas_call | solution.py:638
  113.2 0.7 copy.13
  (5 shorter events, 0.0 us)
Async XLA Ops:
  0.6 7.7 %copy-start.4 = (f32[2,16,512]{2,1,0:T(8,128)S(1)}, f32[2,16,512]{2,1,0:T(8,128)}, u32[]{:S(2)}) copy-start(f32[2,16,512]{2,1,0:T(8,128)} %param.9) | copy-start | bytes 196612
  0.6 22.3 %copy-start = (f32[2,16,32,128]{3,2,1,0:T(8,128)S(1)}, f32[2,16,32,128]{3,2,1,0:T(8,128)}, u32[]{:S(2)}) copy-start(f32[2,16,32,128]{3,2,1,0:T(8,128)} %refs_15_) | copy-start | bytes 1572868
  0.7 22.3 %copy-start.2 = (s32[16,32,128]{2,1,0:T(8,128)S(1)}, s32[16,32,128]{2,1,0:T(8,128)}, u32[]{:S(2)}) copy-start(s32[16,32,128]{2,1,0:T(8,128)} %layer.3) | copy-start | bytes 786436
  0.7 22.3 %copy-start.3 = (s32[16,32,128]{2,1,0:T(8,128)S(1)}, s32[16,32,128]{2,1,0:T(8,128)}, u32[]{:S(2)}) copy-start(s32[16,32,128]{2,1,0:T(8,128)} %agg.3) | copy-start | bytes 786436
  2.0 21.0 %copy-start.1 = (f32[16,32,128]{2,1,0:T(8,128)S(1)}, f32[16,32,128]{2,1,0:T(8,128)}, u32[]{:S(2)}) copy-start(f32[16,32,128]{2,1,0:T(8,128)} %wave.3) | copy-start | bytes 786436
  2.0 21.0 %collective-permute-start = (f32[5,16,8,128]{3,2,1,0:T(8,128)S(1)}, f32[5,16,8,128]{3,2,1,0:T(8,128)S(1)}, u32[]{:S(2)}, u32[]{:S(2)}) collective-permute-start(f32[5,16,8,128]{3,2,1,0:T(8,128)S(1)} %get-tuple-element.62), channel_id=1, source_target_pairs={{0,1},{1,2},{2,3},{3,4},{4,5},{5,6},{6,7},{8,9},{9,10},{10,11},{11... | collective-permute-start | bytes 983048 | tf_op jit(solution)/shard_map/ppermute | solution.py:666
  7.0 15.9 %collective-permute-start.1 = (f32[5,16,8,128]{3,2,1,0:T(8,128)S(1)}, f32[5,16,8,128]{3,2,1,0:T(8,128)S(1)}, u32[]{:S(2)}, u32[]{:S(2)}) collective-permute-start(f32[5,16,8,128]{3,2,1,0:T(8,128)S(1)} %get-tuple-element.63), channel_id=1, source_target_pairs={{1,0},{2,1},{3,2},{4,3},{5,4},{6,5},{7,6},{9,8},{10,9},{11,10},{12... | collective-permute-start | bytes 983048 | tf_op jit(solution)/shard_map/ppermute | solution.py:667
  23.1 34.5 %collective-permute-start.4 = (f32[5,6,48,128]{3,2,1,0:T(8,128)S(1)}, f32[5,6,48,128]{3,2,1,0:T(8,128)S(1)}, u32[]{:S(2)}, u32[]{:S(2)}) collective-permute-start(f32[5,6,48,128]{3,2,1,0:T(8,128)S(1)} %get-tuple-element.79), channel_id=1, source_target_pairs={{0,8},{8,16},{16,24},{1,9},{9,17},{17,25},{2,10},{10,18},{18,26},{... | collective-permute-start | bytes 2211848 | tf_op jit(solution)/shard_map/ppermute | solution.py:666
  25.2 32.4 %collective-permute-start.5 = (f32[5,6,48,128]{3,2,1,0:T(8,128)S(1)}, f32[5,6,48,128]{3,2,1,0:T(8,128)S(1)}, u32[]{:S(2)}, u32[]{:S(2)}) collective-permute-start(f32[5,6,48,128]{3,2,1,0:T(8,128)S(1)} %get-tuple-element.80), channel_id=1, source_target_pairs={{8,0},{16,8},{24,16},{9,1},{17,9},{25,17},{10,2},{18,10},{26,18},{... | collective-permute-start | bytes 2211848 | tf_op jit(solution)/shard_map/ppermute | solution.py:667
  26.5 4.5 %collective-permute-start.2 = (f32[5,2,48,128]{3,2,1,0:T(8,128)S(1)}, f32[5,2,48,128]{3,2,1,0:T(8,128)S(1)}, u32[]{:S(2)}, u32[]{:S(2)}) collective-permute-start(f32[5,2,48,128]{3,2,1,0:T(8,128)S(1)} %get-tuple-element.70), channel_id=1, source_target_pairs={{0,8},{8,16},{16,24},{1,9},{9,17},{17,25},{2,10},{10,18},{18,26},{... | collective-permute-start | bytes 737288 | tf_op jit(solution)/shard_map/ppermute | solution.py:666
  29.7 4.6 %collective-permute-start.3 = (f32[5,2,48,128]{3,2,1,0:T(8,128)S(1)}, f32[5,2,48,128]{3,2,1,0:T(8,128)S(1)}, u32[]{:S(2)}, u32[]{:S(2)}) collective-permute-start(f32[5,2,48,128]{3,2,1,0:T(8,128)S(1)} %get-tuple-element.71), channel_id=1, source_target_pairs={{8,0},{16,8},{24,16},{9,1},{17,9},{25,17},{10,2},{18,10},{26,18},{... | collective-permute-start | bytes 737288 | tf_op jit(solution)/shard_map/ppermute | solution.py:667

commit v3 on v2

--- a/solution.py
+++ b/solution.py
@@ -10,7 +10,6 @@
 
 ITERS = 4
 HALO = 2 * ITERS
-NEAR = 2
 AXES = ("gx", "gy")
 AGG = 16
 damping = 0.8
@@ -114,7 +113,7 @@
     cx, cy = own
     r = lax.broadcasted_iota(jnp.int32, (256, 128), 0) % 128
     ones = jnp.where(r <= lanes((256, 128)), 1.0, 0.0).astype(jnp.bfloat16)
-    per = 4
+    per = 16
     out = []
     for c in range(2):
         acc = jnp.zeros((8, 128), F32)
@@ -131,21 +130,18 @@
 def spread_rhs(g0, g1, cols_ref, pad_ref, out_ref, scalars, grid):
     gx, gy = grid
     n = gx * gy
-    lane = lanes((1, 128))
-    rows = []
-    for g in (g0, g1):
-        total = jnp.sum(g, axis=0, keepdims=True)
-        rows.append(jnp.where(lane == 0, total, total - pltpu.roll(total, 1, 1)))
-    z = []
-    for row in rows:
-        acc = None
+    lane = lanes((8, 128))
+    acc = None
+    for c, g in enumerate((g0, g1)):
+        total = jnp.broadcast_to(jnp.sum(g, axis=0, keepdims=True), (8, 128))
         for q in range(4):
-            weight = take(row, lanes((8, 128)) // 32 + 4 * q)[0:1]
-            term = cols_ref[pl.ds(q, n, stride=4), :] * weight
+            source = lane // 32 + 4 * q
+            below = jnp.take_along_axis(total, jnp.maximum(source - 1, 0), axis=1, mode="promise_in_bounds")
+            weight = jnp.take_along_axis(total, source, axis=1, mode="promise_in_bounds")
+            weight = weight - jnp.where(source == 0, 0.0, below)
+            term = cols_ref[pl.ds((c * 4 + q) * n, n), :] * weight[0:1]
             acc = term if acc is None else acc + term
-        acc = acc + pltpu.roll(acc, 64, 1)
-        z.append(acc + pltpu.roll(acc, 32, 1))
-    whole = z[0] + turn(z[1])
+    whole = (acc + pltpu.roll(acc, 64, 1)) + (pltpu.roll(acc, 32, 1) + pltpu.roll(acc, 96, 1))
     margin = (pad_ref.shape[0] - n) // 2
     pad_ref[0:margin, :] = jnp.zeros((margin, 128), F32)
     pad_ref[margin + n : 2 * margin + n, :] = jnp.zeros((margin, 128), F32)
@@ -193,7 +189,7 @@
         planes(lo, hi, go, width=4)
 
 
-def centre(f, g, u, t, t_rim, places, halo, s, edge, split, ends, own, rows, t_rows):
+def centre(f, g, u, t, t_rim, places, halo, s, split, ends, own, rows, t_rows):
     mine, low, high = places
     cx, cy = own
     size = cx + 2 * HALO
@@ -219,87 +215,37 @@
         keep_split(split, 1, i, u[1, x, y0:y1, :] - a1[lo : lo + cy])
 
     planes(HALO, HALO + cx, middle)
-    if edge is not None:
-        for c in range(2):
-            for k, x in enumerate((HALO, HALO + cx - 1)):
-                edge[0, c, k] = f[c, x]
-                edge[1, c, k] = g[c, x]
     return restrict(split, ends, own)
 
 
-def rim_pair(lo, hi, fn):
-    if hi > lo:
-        def go(x):
-            fn(x, x)
-            y = lo + hi - 1 - x
-            fn(2 * HALO + 1 - y, 2 * HALO - 1 - y)
-
-        planes(lo, hi, go, width=4)
-
-
-def fringe(f, g, u, t, rim, edge, halo, rows):
-    for c in range(2):
-        for k, x in enumerate((HALO, HALO + 1)):
-            f[c, x] = edge[0, c, k]
-            g[c, x] = edge[1, c, k]
-    rim_pair(HALO - halo + 1, HALO, lambda k, i: smooth_plane(f, g, u, k, (rim, i), *rows))
-    y0, y1 = rows
-
-    def last(k, i):
-        a0, a1 = operate_plane(g, k, (rim, i), y0, y1)
-        t[0, i, y0:y1, :], t[1, i, y0:y1, :] = a0, a1
-
-    rim_pair(HALO - halo + 2, HALO, last)
-
-
-def fill(store, u, f, k, y0, y1, r0, r1, wave, layer, a):
+def fill(store, y0, y1, wave, layer, a):
     sq = wave * wave
-    depth = layer / 3.0
-    ab = sq * (pml_strength * depth * depth)
+    ab = sq * (layer * layer * (pml_strength / 9.0))
     d = 6.0 - sq
-    w = jnp.where(wave > 0.0, damping / (d * d + ab * ab), 0.0)
-    p, q = d * w, ab * w
+    w = jnp.where(wave > 0.0, damping * pl.reciprocal(d * d + ab * ab), 0.0)
     refs, i = store
     refs[0][i, y0:y1, :] = d
     refs[1][i, y0:y1, :] = ab
-    refs[2][i, y0:y1, :] = p
-    refs[3][i, y0:y1, :] = q
+    refs[2][i, y0:y1, :] = d * w
+    refs[3][i, y0:y1, :] = ab * w
     refs[4][i, y0:y1, :] = a
-    u[0, k, y0:y1, :] = r0
-    u[1, k, y0:y1, :] = r1
-    f[0, k, 8 + y0 : 8 + y1, :] = p * r0 - q * r1
-    f[1, k, 8 + y0 : 8 + y1, :] = p * r1 + q * r0
-
-
-def fill_from(store, u, f, k, buf, b, y0, y1):
-    fill(store, u, f, k, y0, y1, buf[0, b], buf[1, b], buf[2, b], buf[3, b], buf[4, b].astype(jnp.int32))
-
-
-def start_kernel(grid, own,
-                 rhs, wave, layer, agg, ylo, yhi, xlo, xhi, cols,
-                 diag, absorb, sre, sim, ids, ends, t, s, edge, out_ref,
-                 n0, n1, n2, n3, n4, u, f, g, split, pad):
+
+
+def own_kernel(own, rhs, wave, layer, agg, ylo, yhi, diag, absorb, sre, sim, ids, ends, sq_out):
     cx, cy = own
     ey = cy + 2 * HALO
-    refs, near = (diag, absorb, sre, sim, ids), (n0, n1, n2, n3, n4)
-    mine = lambda x: (refs, x - HALO)
-    low = lambda x: (near, x - HALO + NEAR)
-    high = lambda x: (near, x - HALO - cx + NEAR)
-    for i in range(NEAR):
-        x = HALO - NEAR + i
-        fill_from(low(x), u, f, x, xlo, i, 0, ey)
-        x = HALO + cx + i
-        fill_from(high(x), u, f, x, xhi, i, 0, ey)
-
-    def inner(x, acc):
-        i = x - HALO
+    home = (diag, absorb, sre, sim, ids)
+
+    def inner(i, acc):
+        store = (home, i)
+        fill(store, 0, HALO, ylo[2, i], ylo[3, i], ylo[4, i].astype(jnp.int32))
+        fill(store, HALO + cy, ey, yhi[2, i], yhi[3, i], yhi[4, i].astype(jnp.int32))
+        fill(store, HALO, HALO + cy, wave[i], layer[i].astype(F32), agg[i])
         r0, r1 = rhs[0, i], rhs[1, i]
-        fill_from(mine(x), u, f, x, ylo, i, 0, HALO)
-        fill_from(mine(x), u, f, x, yhi, i, HALO + cy, ey)
-        fill(mine(x), u, f, x, HALO, HALO + cy, r0, r1, wave[i], layer[i].astype(F32), agg[i])
         return acc + fold8(r0 * r0 + r1 * r1)
 
-    sq = planes(HALO, HALO + cx, inner, jnp.zeros((8, 128), F32))
+    sq = planes(0, cx, inner, jnp.zeros((8, 128), F32))
+    sq_out[...] = scalar_row([(40, sq)])
 
     def find(i):
         a = agg[i]
@@ -316,35 +262,69 @@
         ends[i] = jnp.maximum(low - 1, 0)
 
     planes(0, cx, find)
-    g0, g1 = centre(f, g, u, t, None, (mine, low, high), 2, s, edge, split, ends, own, (0, ey), (0, ey))
-    spread_rhs(g0, g1, cols, pad, out_ref, scalar_row([(40, sq)]), grid)
-
-
-def start_fringe_kernel(own, got, xlo, xhi, wlo, whi, edge,
-                        diag, absorb, sre, sim, ids, t, u, f, g):
-    _, cy = own
+
+
+def start_kernel(grid, own, *refs):
+    rhs, ylo, yhi, xlo, xhi, clo, chi, cols, ends, sq = refs[:10]
+    home, rim = refs[10:15], refs[15:20]
+    t, t_rim, s, out_ref, u, f, g, split, pad = refs[20:]
+    cx, cy = own
     ey = cy + 2 * HALO
-    rim = (diag, absorb, sre, sim, ids)
-    far = HALO - NEAR
-
-    def go(i):
-        fill_from((rim, i), u, f, i, wlo, i, 0, ey)
-        fill_from((rim, HALO + NEAR + i), u, f, HALO + 2 + NEAR + i, whi, i, 0, ey)
-
-    planes(0, far, go, width=4)
-    for i in range(NEAR):
-        fill_from((rim, far + i), u, f, far + i, xlo, i, 0, ey)
-        fill_from((rim, HALO + i), u, f, HALO + 2 + i, xhi, i, 0, ey)
-    fringe(f, g, u, t, rim, edge, HALO, (0, ey))
-
-
-def read_scalars(scal, j):
-    hr = [pick(scal, 32 + 2 * i) for i in range(j)]
-    hi = [pick(scal, 33 + 2 * i) for i in range(j)]
-    sq = pick(scal, 40)
+    y0, y1 = HALO, HALO + cy
+    mine = lambda x: (home, x - HALO)
+    low = lambda x: (rim, x)
+    high = lambda x: (rim, x - cx)
+
+    def first(place, k, lo, hi, r0, r1):
+        refs, i = place
+        p, q = refs[2][i, lo:hi, :], refs[3][i, lo:hi, :]
+        u[0, k, lo:hi, :] = r0
+        u[1, k, lo:hi, :] = r1
+        f[0, k, 8 + lo : 8 + hi, :] = p * r0 - q * r1
+        f[1, k, 8 + lo : 8 + hi, :] = p * r1 + q * r0
+
+    for k in range(HALO):
+        for buf, corner, i, x in ((xlo, clo, HALO - 1 - k, HALO - 1 - k), (xhi, chi, k, HALO + cx + k)):
+            place = low(x) if x < HALO else high(x)
+            below, above = corner_plane(corner, k)
+            for src, lo, hi in ((below, 0, y0), (buf[:, i], y0, y1), (above, y1, ey)):
+                fill(place, lo, hi, src[2], src[3], src[4].astype(jnp.int32))
+                first(place, x, lo, hi, src[0], src[1])
+
+    def inner(x):
+        i = x - HALO
+        first(mine(x), x, 0, y0, ylo[0, i], ylo[1, i])
+        first(mine(x), x, y0, y1, rhs[0, i], rhs[1, i])
+        first(mine(x), x, y1, ey, yhi[0, i], yhi[1, i])
+
+    planes(HALO, HALO + cx, inner)
+    g0, g1 = centre(f, g, u, t, t_rim, (mine, low, high), HALO, s, split, ends, own, (0, ey), (0, ey))
+    spread_rhs(g0, g1, cols, pad, out_ref, sq[...], grid)
+
+
+def read_scalars(raw, olds, j):
+    h = []
     for i in range(j):
-        sq = sq - (hr[i] * hr[i] + hi[i] * hi[i])
-    return hr, hi, 1.0 / jnp.sqrt(jnp.maximum(sq, 0.0) + epsilon)
+        a0, a1 = pick(raw, 32 + 2 * i), pick(raw, 33 + 2 * i)
+        for k in range(i):
+            b0, b1 = pick(olds[i], 32 + 2 * k), pick(olds[i], 33 + 2 * k)
+            a0, a1 = a0 - (b0 * h[k][0] + b1 * h[k][1]), a1 - (b0 * h[k][1] - b1 * h[k][0])
+        inv = pick(olds[i], 41)
+        h.append((a0 * inv, a1 * inv))
+    sq = pick(raw, 40)
+    for a0, a1 in h:
+        sq = sq - (a0 * a0 + a1 * a1)
+    length = jnp.sqrt(jnp.maximum(sq, 0.0) + epsilon)
+    return h, length
+
+
+def write_scalars(out, h, length, inv):
+    lane = lanes((1, 128))
+    row = jnp.where(lane == 40, length[0:1], inv[0:1])
+    for k, pair in enumerate(h):
+        for c in range(2):
+            row = jnp.where(lane == 32 + 2 * k + c, pair[c][0:1], row)
+    out[...] = row
 
 
 def like(v, rows):
@@ -352,23 +332,44 @@
 
 
 def combine(scalars, new, old):
-    hr, hi, inv = scalars
+    h, inv = scalars
     a0, a1 = new
     rows = a0.shape[0]
-    for i in range(len(hr)):
+    for i in range(len(h)):
         b0, b1 = old(i)
-        r, q = like(hr[i], rows), like(hi[i], rows)
+        r, q = like(h[i][0], rows), like(h[i][1], rows)
         a0 = a0 - (r * b0 - q * b1)
         a1 = a1 - (r * b1 + q * b0)
     s = like(inv, rows)
     return a0 * s, a1 * s
 
 
-def prolong_plane(pc, k, ids, i, table, own, dx):
+def splats(row, first):
+    return [pick(row, first + k) for k in range(AGG)]
+
+
+def marks(index):
+    return [(index & 1) == 1, (index & 3) >= 2, (index & 7) >= 4, index >= 8]
+
+
+def choose(values, bits):
+    rows = bits[0].shape[0]
+    level = [like(v, rows) for v in values]
+    for bit in bits:
+        level = [jnp.where(bit, level[k + 1], level[k]) for k in range(0, len(level), 2)]
+    return level[0]
+
+
+def prolong_plane(pc, k, ids, i, table, own, dx, values=None):
     cy = own[1]
     ey = cy + 2 * HALO
     for dy, lo, hi in ((0, 0, HALO), (1, HALO, HALO + cy), (2, HALO + cy, ey)):
         n = dx * 3 + dy
+        if values is not None and dy == 1:
+            bits = marks(ids[i, lo:hi, :])
+            for c in range(2):
+                pc[c, k, 8 + lo : 8 + hi, :] = choose(values[c], bits)
+            continue
         src = table[:, 128 * (n // 4) : 128 * (n // 4) + 128]
         index = ids[i, lo:hi, :] + 32 * (n % 4)
         pc[0, k, 8 + lo : 8 + hi, :] = take(src, index)
@@ -413,10 +414,10 @@
     last = j == ITERS - 1
     rcv = refs.pop(0)
     home, rim = take_refs(5), take_refs(5)
-    ends, cols, t_own, t_rim, u_in = take_refs(5)
+    ends, cols, t_own, t_rim = take_refs(4)
     m_own, m_rim = take_refs(j), take_refs(0 if last else j)
-    v_old, c_old = take_refs(j), take_refs(j)
-    v_out, c_out, h_out, out_ref = take_refs(4)
+    u_in, c_old, h_old = take_refs(j + 1), take_refs(j), take_refs(j)
+    c_out, h_out, out_ref = take_refs(3)
     if not last:
         m_out, t, u_out, s_out = take_refs(4)
     mr_out = tr_out = None
@@ -435,15 +436,15 @@
     size = cx + 2 * HALO
 
     row = jnp.sum(rcv[...], axis=0, keepdims=True)
-    scal = row[:, 256:384]
-    h_out[...] = scal
-    scalars = read_scalars(scal, j)
-    hr, hi, inv = scalars
+    h, length = read_scalars(row[:, 256:384], [r[...] for r in h_old], j)
+    inv = 1.0 / length
+    write_scalars(h_out, h, length, inv)
+    scalars = h, inv
     wide = lambda v: jnp.concatenate([v[0:1]] * 3, axis=1)
     table = row
     for i in range(j):
         old = c_old[i][...]
-        table = table - (wide(hr[i]) * old + wide(hi[i]) * turn_rows(old))
+        table = table - (wide(h[i][0]) * old + wide(h[i][1]) * turn_rows(old))
     table = table * wide(inv)
     c_out[...] = table
 
@@ -453,7 +454,8 @@
         prolong_plane(pc, y + cx, rim[4], y, table, own, 2)
 
     planes(HALO - halo - 1, HALO, outside, width=4)
-    planes(HALO, HALO + cx, lambda x: prolong_plane(pc, x, home[4], x - HALO, table, own, 1))
+    values = [splats(table[:, 128:256], AGG * c) for c in range(2)]
+    planes(HALO, HALO + cx, lambda x: prolong_plane(pc, x, home[4], x - HALO, table, own, 1, values))
 
     def outer(k, c):
         image_store(pc, u, f, k, c, t_rim, m_rim, scalars, mr_out, *rows)
@@ -469,11 +471,9 @@
             lo = y0 - rows[0]
             u0, u1 = u0[lo : lo + cy], u1[lo : lo + cy]
             u_out[0, i], u_out[1, i] = u0, u1
-        v0, v1 = combine(scalars, (u_in[0, i], u_in[1, i]), lambda k: (v_old[k][0, i], v_old[k][1, i]))
-        v_out[0, i], v_out[1, i] = v0, v1
         new = []
         for k in range(j + 1):
-            b0, b1 = (v0, v1) if k == j else (v_old[k][0, i], v_old[k][1, i])
+            b0, b1 = u_in[k][0, i], u_in[k][1, i]
             new.append(fold8(b0 * u0 + b1 * u1))
             new.append(fold8(b0 * u1 - b1 * u0))
         new.append(fold8(u0 * u0 + u1 * u1))
@@ -490,43 +490,58 @@
         out_ref[:, 256:384] = jnp.broadcast_to(dots, (n, 128))
         return
     t_rows = rows if j < ITERS - 2 else (y0, y1)
-    g0, g1 = centre(f, pc, u, t, tr_out, (mine, low, high), halo, s_out, None, split, ends, own, rows, t_rows)
+    g0, g1 = centre(f, pc, u, t, tr_out, (mine, low, high), halo, s_out, split, ends, own, rows, t_rows)
     spread_rhs(g0, g1, cols, pad, out_ref, dots, grid)
 
 
-def pack_kernel(rhs, wave, layer, agg, low, high, ints, sems):
-    cy = wave.shape[1]
+def pack_kernel(rhs, wave, layer, agg, ylow, yhigh, xlow, xhigh, yint, xint, sems):
+    cx, cy = wave.shape[:2]
+    every = slice(None)
+    cuts = (
+        (ylow, yint, 0, every, pl.ds(0, HALO)),
+        (yhigh, yint, 2, every, pl.ds(cy - HALO, HALO)),
+        (xlow, xint, 0, pl.ds(0, HALO), every),
+        (xhigh, xint, 2, pl.ds(cx - HALO, HALO), every),
+    )
     copies = []
-    for k, (out, y) in enumerate(((low, 0), (high, cy - HALO))):
-        rows = pl.ds(y, HALO)
+    for k, (out, ints, slot, xs, ys) in enumerate(cuts):
         for i, (src, dst) in enumerate((
-            (rhs.at[:, :, rows, :], out.at[0:2]),
-            (wave.at[:, rows, :], out.at[2]),
-            (layer.at[:, rows, :], ints.at[2 * k]),
-            (agg.at[:, rows, :], ints.at[2 * k + 1]),
+            (rhs.at[:, xs, ys, :], out.at[0:2]),
+            (wave.at[xs, ys, :], out.at[2]),
+            (layer.at[xs, ys, :], ints.at[slot]),
+            (agg.at[xs, ys, :], ints.at[slot + 1]),
         )):
             copies.append(pltpu.make_async_copy(src, dst, sems.at[4 * k + i]))
     for copy in copies:
         copy.start()
     for copy in copies:
         copy.wait()
-    for k, out in enumerate((low, high)):
-        out[3] = ints[2 * k].astype(F32)
-        out[4] = ints[2 * k + 1].astype(F32)
-
-
-def slab_kernel(rhs, wave, layer, agg, ylo, yhi, near_low, near_high, far_low, far_high):
-    cx, cy = wave.shape[:2]
-    y0, y1 = HALO, HALO + cy
-    for out, lo, hi in (
-        (near_low, 0, NEAR), (near_high, cx - NEAR, cx), (far_low, NEAR, HALO), (far_high, cx - HALO, cx - NEAR),
-    ):
-        out[:, :, 0:y0, :] = ylo[:, lo:hi]
-        out[:, :, y1 : y1 + HALO, :] = yhi[:, lo:hi]
-        out[0:2, :, y0:y1, :] = rhs[:, lo:hi]
-        out[2, :, y0:y1, :] = wave[lo:hi]
-        out[3, :, y0:y1, :] = layer[lo:hi].astype(F32)
-        out[4, :, y0:y1, :] = agg[lo:hi].astype(F32)
+    for out, ints, slot, _, _ in cuts:
+        out[3] = ints[slot].astype(F32)
+        out[4] = ints[slot + 1].astype(F32)
+
+
+def corner_kernel(ylo, yhi, low, high):
+    cx = ylo.shape[1]
+    row = lax.broadcasted_iota(jnp.int32, (5, HALO, ylo.shape[3]), 1)
+    for out, plane in ((low, lambda k: k), (high, lambda k: cx - 1 - k)):
+        for p in range(HALO // 2):
+            a, b = plane(p), plane(HALO - 2 - p)
+            out[:, p, 0:HALO, :] = jnp.where(row > p, ylo[:, a], pltpu.roll(ylo[:, b], p + 1, 1))
+            out[:, p, HALO : 2 * HALO, :] = jnp.where(
+                row < HALO - 1 - p, yhi[:, a], pltpu.roll(yhi[:, b], HALO - 1 - p, 1)
+            )
+
+
+def corner_plane(buf, k):
+    if k == HALO - 1:
+        zero = jnp.zeros((5, HALO, buf.shape[3]), F32)
+        return zero, zero
+    p = min(k, HALO - 2 - k)
+    below, above = buf[:, p, 0:HALO, :], buf[:, p, HALO : 2 * HALO, :]
+    if k != p:
+        below, above = pltpu.roll(below, HALO - 1 - p, 1), pltpu.roll(above, p + 1, 1)
+    return below, above
 
 
 def columns_kernel(inverse, out, turned):
@@ -540,6 +555,14 @@
     out[...] = total
 
 
+def arrange_kernel(got, out):
+    n = got.shape[0] // 4
+    for q in range(4):
+        rows = got[pl.ds(q, n, stride=4), :]
+        out[q * n : (q + 1) * n, :] = rows
+        out[(4 + q) * n : (5 + q) * n, :] = turn(rows)
+
+
 def cmul(a, b):
     return a[0] * b[0] - a[1] * b[1], a[0] * b[1] + a[1] * b[0]
 
@@ -552,28 +575,25 @@
     sol, hess = refs[2 + 3 * ITERS :]
     cx, cy = own
     final = jnp.sum(rcv[:, 256:384], axis=0, keepdims=True)
-    scal = [r[...] for r in rows] + [final]
-    beta = jnp.sqrt(pick(scal[0], 40) + epsilon)
-    upper = []
-    sub = []
-    for j in range(ITERS):
-        row = scal[j + 1]
-        col = [(pick(row, 32 + 2 * i), pick(row, 33 + 2 * i)) for i in range(j + 1)]
-        sq = pick(row, 40)
-        for a, b in col:
-            sq = sq - (a * a + b * b)
-        upper.append(col)
-        sub.append(jnp.sqrt(jnp.maximum(sq, 0.0) + epsilon))
+    scal = [r[...] for r in rows]
+    beta = pick(scal[0], 40)
+    upper, sub = [], []
+    for j in range(1, ITERS):
+        upper.append([(pick(scal[j], 32 + 2 * i), pick(scal[j], 33 + 2 * i)) for i in range(j)])
+        sub.append(pick(scal[j], 40))
+    h, length = read_scalars(final, scal, ITERS)
+    upper.append(h)
+    sub.append(length)
     r_i = lax.broadcasted_iota(jnp.int32, (8, 128), 0)
     c_i = lanes((8, 128))
     for comp in range(2):
         block = jnp.zeros((8, 128), F32)
         for j in range(ITERS):
             for i in range(j + 1):
-                block = jnp.where((r_i == i) & (c_i == j), upper[j][i][comp], block)
+                block = jnp.where((r_i == j) & (c_i == i), upper[j][i][comp], block)
             if comp == 0:
-                block = jnp.where((r_i == j + 1) & (c_i == j), sub[j], block)
-        hess[comp] = block[0 : ITERS + 1, 0:ITERS]
+                block = jnp.where((r_i == j) & (c_i == j + 1), sub[j], block)
+        hess[comp] = block[0:ITERS, 0 : ITERS + 1]
     zero = jnp.zeros((8, 128), F32)
     target = [(beta, zero)]
     rot = []
@@ -618,9 +638,11 @@
             b = cmul(upper[j - 1][i], gamma[j])
             gamma[i] = (gamma[i][0] - b[0], gamma[i][1] - b[1])
 
+    values = splats(table, AGG)
+
     def go(i):
         index = ids[i, HALO : HALO + cy, :]
-        a0, a1 = take(table, index), take(table, index + AGG)
+        a0, a1 = take(table, index), choose(values, marks(index))
         for j in range(ITERS):
             b = cmul((like(gamma[j][0], cy), like(gamma[j][1], cy)), (z[j][0, i], z[j][1, i]))
             a0, a1 = a0 + b[0], a1 + b[1]
@@ -667,14 +689,15 @@
         high_in = lax.ppermute(low, axis, down)
         return low_in, high_in
 
-    strip = shape(5, cx, HALO, cz)
-    low, high = call(
-        pack_kernel, [strip, strip],
-        [pltpu.VMEM((4, cx, HALO, cz), jnp.int32), pltpu.SemaphoreType.DMA((8,))],
+    strip, slab = shape(5, cx, HALO, cz), shape(5, HALO, cy, cz)
+    ylow, yhigh, xlow, xhigh = call(
+        pack_kernel, [strip, strip, slab, slab],
+        [pltpu.VMEM((4, cx, HALO, cz), jnp.int32), pltpu.VMEM((4, HALO, cy, cz), jnp.int32), pltpu.SemaphoreType.DMA((16,))],
         [pltpu.with_memory_space_constraint(x, pltpu.HBM) for x in (right_side, wavenumber, pml_layer, aggregate)],
         space=pltpu.HBM,
     )
-    ylo, yhi = swap(low, high, "gy")
+    ylo, yhi = swap(ylow, yhigh, "gy")
+    xlo, xhi = swap(xlow, xhigh, "gx")
     (inverse,) = call(
         columns_kernel, [shape(4 * n, 128)], [pltpu.VMEM((AGG * n, 128), F32)],
         [coarse_inverse.reshape(2 * AGG, AGG * n)],
@@ -683,74 +706,66 @@
     right_side, wavenumber, pml_layer, aggregate, ylo, yhi, cols = lax.optimization_barrier(
         (right_side, wavenumber, pml_layer, aggregate, ylo, yhi, cols)
     )
-    near, far = shape(5, NEAR, ey, cz), shape(5, HALO - NEAR, ey, cz)
-    near_low, near_high, far_low, far_high = call(
-        slab_kernel, [near, near, far, far], [],
-        [right_side, wavenumber, pml_layer, aggregate, ylo, yhi],
-    )
-    xlo, xhi = swap(near_low, near_high, "gx")
-    wlo, whi = swap(far_low, far_high, "gx")
-
+    corner = shape(5, HALO // 2, 2 * HALO, cz)
+    clow, chigh = call(corner_kernel, [corner, corner], [], [ylo, yhi])
+    clo, chi = swap(clow, chigh, "gx")
+    (cols,) = call(arrange_kernel, [shape(8 * n, 128)], [], [cols])
     I32 = jnp.int32
     home = [shape(cx, ey, cz)] * 4 + [shape(cx, ey, cz, dtype=I32)]
     rim = [shape(2 * HALO, ey, cz)] * 4 + [shape(2 * HALO, ey, cz, dtype=I32)]
     home2, rim2 = shape(2, cx, ey, cz), shape(2, 2 * HALO, ey, cz)
     mine = shape(2, cx, cy, cz)
     chunk = shape(n, 384)
-    edges = shape(2, 2, 2, ey + 16, cz)
     vmem = lambda *dims, dtype=F32: pltpu.VMEM(dims, dtype)
     tall = vmem(2, ex, ey + 16, cz)
     flat = vmem(2, ex, ey, cz)
-    short_tall = vmem(2, 2 * HALO + 2, ey + 16, cz)
-    short_flat = vmem(2, 2 * HALO + 2, ey, cz)
     pad = vmem(n + 2 * margin, 128)
     split = vmem(2, cx, cy, 256, dtype=jnp.bfloat16)
-    near = [vmem(2 * NEAR, ey, cz)] * 4 + [vmem(2 * NEAR, ey, cz, dtype=I32)]
-
-    *own_coefs, ends, t_own, s, edge, send = call(
+
+    *own_coefs, ends, sq = call(
+        functools.partial(own_kernel, own),
+        home + [shape(cx, cy, cz, dtype=I32), shape(1, 128)], [],
+        [right_side, wavenumber, pml_layer, aggregate, ylo, yhi],
+    )
+    res = call(
         functools.partial(start_kernel, grid, own),
-        home + [shape(cx, cy, cz, dtype=I32), home2, mine, edges, chunk],
-        near + [flat, tall, tall, split, pad],
-        [right_side, wavenumber, pml_layer, aggregate, ylo, yhi, xlo, xhi, cols],
-    )
+        rim + [home2, rim2, mine, chunk],
+        [flat, tall, tall, split, pad],
+        [right_side, ylo, yhi, xlo, xhi, clo, chi, cols, ends, sq] + own_coefs,
+    )
+    rim_coefs = list(res[:5])
+    t_own, t_rim, s, send = res[5:]
     got = exchange(send)
-    *rim_coefs, t_rim = call(
-        functools.partial(start_fringe_kernel, own),
-        rim + [rim2],
-        [short_flat, short_tall, short_tall],
-        [got, xlo, xhi, wlo, whi, edge],
-    )
-    u = right_side
-    ms, mrs, vs, ss, cs, hs = [], [], [], [s], [], []
+    ms, mrs, us, ss, cs, hs = [], [], [right_side], [s], [], []
     for j in range(ITERS):
         last = j == ITERS - 1
-        args = [got] + own_coefs + rim_coefs + [ends, cols, t_own, t_rim, u] + ms + ([] if last else mrs) + vs + cs
-        outs = [mine, shape(1, 384), shape(1, 128), chunk]
+        args = [got] + own_coefs + rim_coefs + [ends, cols, t_own, t_rim] + ms + ([] if last else mrs) + us + cs + hs
+        outs = [shape(1, 384), shape(1, 128), chunk]
         scratch = [tall]
         if not last:
             outs += [home2, home2, mine, mine]
             if j < ITERS - 2:
                 outs += [rim2, rim2]
             scratch += [flat, tall, split, pad]
-        v, c, h, send, *rest = call(functools.partial(step_kernel, j, grid, own), outs, scratch, args)
+        c, h, send, *rest = call(functools.partial(step_kernel, j, grid, own), outs, scratch, args)
         got = exchange(send)
         if not last:
             m, t_own, u, s = rest[:4]
+            us.append(u)
             ms.append(m)
             ss.append(s)
             if j < ITERS - 2:
                 mrs.append(rest[4])
                 t_rim = rest[5]
-        vs.append(v)
         cs.append(c)
         hs.append(h)
     sol, hess = call(
         functools.partial(finish_kernel, own),
-        [mine, shape(2, ITERS + 1, ITERS)],
+        [mine, shape(2, ITERS, ITERS + 1)],
         [],
         [got, own_coefs[4]] + ss + cs + hs,
     )
-    return sol, hess
+    return sol, jnp.swapaxes(hess, 1, 2)
 
 
 def solution(mesh):

time: 114 us -> 107 us (0.939)
  waiting for transfers between devices: 3.33 us -> 0.15 us
  blocking collectives: 69 us -> 67.4 us
  starting transfers between devices: 14.2 us -> 12.7 us
    ppermute x3, waiting for transfers between devices: 3.33 us -> 0.15 us  [swap(): high_in = lax.ppermute(low, axis, down)]
    all_to_all x6, blocking collectives: 69 us -> 67.4 us  [exchange(): return lax.all_to_all(x, AXES, 0, 0, tiled=True)]
    ppermute x3, starting transfers between devices: 10.3 us -> 8.86 us  [swap(): low_in = lax.ppermute(high, axis, up)]
    pallas_call x10 -> x11, Pallas kernels: 25.5 us -> 24.9 us  [call(): pl.pallas_call(kernel, out_shape=outs, in_specs=[pl.BlockSpec(memory_spac...]
  transfers between devices with their start and end apart: 6 -> 6, of which waited for: 1 -> 1; matrix products, arithmetic and copies ran while one was open for 0% -> 0% of each run, Pallas kernels for 4% -> 2%
where the time goes in v3:
time: 107 us; the launch traced here: 106 us
  blocking collectives  67.4 us (63%)
  Pallas kernels  24.9 us (23%)
  starting transfers between devices  12.7 us (12%)
    all_to_all x6, blocking collectives, exchange(): return lax.all_to_all(x, AXES, 0, 0, tiled=True)  67.4 us
    pallas_call x11, Pallas kernels, call(): pl.pallas_call(kernel, out_shape=outs, in_specs=[pl.BlockSpec(memory_spac...  24.9 us
    ppermute x3, starting transfers between devices, swap(): low_in = lax.ppermute(high, axis, up)  8.86 us
    ppermute x3, starting transfers between devices, swap(): high_in = lax.ppermute(low, axis, down)  3.88 us
  transfers between devices with their start and end apart: 6, of which 1 were waited for; matrix products, arithmetic and copies ran while one was open for 0% of the time, Pallas kernels for 2%

profile of v3, /device:TPU:0, one launch (start us, length us, event | category | flops | bytes accessed | tf_op | source)
XLA Modules:
  0.0 106.4 jit_solution(2314355869802642810)
XLA Ops:
  0.6 0.0 copy-start.4
  0.6 1.8 %shard_map.68 = (f32[5,16,8,128]{3,2,1,0:T(8,128)S(1)}, f32[5,16,8,128]{3,2,1,0:T(8,128)S(1)}, f32[5,8,32,128]{3,2,1,0:T(8,128)S(1)}, f32[5,8,32,128]{3,2,1,0:T(8,128)S(1)}) custom-call(f32[2,16,32,128]{3,2,1,0:T(8,128)} %refs_18_, f32[16,32,128]{2,1,0:T(8,128)} %wave.2, s32[16,32,128]{2,1,0:T(8,128)} %layer.2, s32[16,32,128]{2,1,0:T(8,128)} %agg.2), custom_call_target="tpu_custom_call" | custom-call | flops 100000000 | bytes 1000000 | tf_op jit(solution)/shard_map/pallas_call | solution.py:660
  2.4 2.4 %collective-permute-start.2 = (f32[5,8,32,128]{3,2,1,0:T(8,128)S(1)}, f32[5,8,32,128]{3,2,1,0:T(8,128)S(1)}, u32[]{:S(2)}, u32[]{:S(2)}) collective-permute-start(f32[5,8,32,128]{3,2,1,0:T(8,128)S(1)} %get-tuple-element.66), channel_id=1, source_target_pairs={{0,8},{8,16},{16,24},{1,9},{9,17},{17,25},{2,10},{10,18},{18,26},{... | collective-permute-start | bytes 1966088 | tf_op jit(solution)/shard_map/ppermute | solution.py:688
  4.9 1.3 %collective-permute-start.3 = (f32[5,8,32,128]{3,2,1,0:T(8,128)S(1)}, f32[5,8,32,128]{3,2,1,0:T(8,128)S(1)}, u32[]{:S(2)}, u32[]{:S(2)}) collective-permute-start(f32[5,8,32,128]{3,2,1,0:T(8,128)S(1)} %get-tuple-element.67), channel_id=1, source_target_pairs={{8,0},{16,8},{24,16},{9,1},{17,9},{25,17},{10,2},{18,10},{26,18},{... | collective-permute-start | bytes 1966088 | tf_op jit(solution)/shard_map/ppermute | solution.py:689
  6.2 4.3 %collective-permute-start = (f32[5,16,8,128]{3,2,1,0:T(8,128)S(1)}, f32[5,16,8,128]{3,2,1,0:T(8,128)S(1)}, u32[]{:S(2)}, u32[]{:S(2)}) collective-permute-start(f32[5,16,8,128]{3,2,1,0:T(8,128)S(1)} %get-tuple-element.61), channel_id=1, source_target_pairs={{0,1},{1,2},{2,3},{3,4},{4,5},{5,6},{6,7},{8,9},{9,10},{10,11},{11... | collective-permute-start | bytes 983048 | tf_op jit(solution)/shard_map/ppermute | solution.py:688
  10.4 1.3 %collective-permute-start.1 = (f32[5,16,8,128]{3,2,1,0:T(8,128)S(1)}, f32[5,16,8,128]{3,2,1,0:T(8,128)S(1)}, u32[]{:S(2)}, u32[]{:S(2)}) collective-permute-start(f32[5,16,8,128]{3,2,1,0:T(8,128)S(1)} %get-tuple-element.62), channel_id=1, source_target_pairs={{1,0},{2,1},{3,2},{4,3},{5,4},{6,5},{7,6},{9,8},{10,9},{11,10},{12... | collective-permute-start | bytes 983048 | tf_op jit(solution)/shard_map/ppermute | solution.py:689
  11.7 0.0 copy-done.4
  11.8 0.0 copy-start.3
  11.8 0.3 shard_map.69
  12.0 0.0 copy-start.2
  12.0 16.5 %all_to_all.67 = f32[32,4,128]{2,1,0:T(4,128)S(1)} all-to-all(f32[32,4,128]{2,1,0:T(4,128)S(1)} %bitcast.30), channel_id=1, replica_groups=mesh['gx'=4,'gy'=8] {'gx','gy'}, dimensions={0} | all-to-all | bytes 131072 | tf_op jit(solution)/shard_map/all_to_all | solution.py:672
  28.6 0.0 copy-start
  28.6 0.0 collective-permute-done.ylo.refs_1_
  28.6 0.0 collective-permute-done.1.yhi.refs_2_
  28.6 0.0 copy-start.1
  28.7 2.2 %collective-permute-start.4 = (f32[5,4,16,128]{3,2,1,0:T(8,128)S(1)}, f32[5,4,16,128]{3,2,1,0:T(8,128)S(1)}, u32[]{:S(2)}, u32[]{:S(2)}) collective-permute-start(f32[5,4,16,128]{3,2,1,0:T(8,128)S(1)} %get-tuple-element.68), channel_id=1, source_target_pairs={{0,8},{8,16},{16,24},{1,9},{9,17},{17,25},{2,10},{10,18},{18,26},{... | collective-permute-start | bytes 491528 | tf_op jit(solution)/shard_map/ppermute | solution.py:688
  30.8 1.3 %collective-permute-start.5 = (f32[5,4,16,128]{3,2,1,0:T(8,128)S(1)}, f32[5,4,16,128]{3,2,1,0:T(8,128)S(1)}, u32[]{:S(2)}, u32[]{:S(2)}) collective-permute-start(f32[5,4,16,128]{3,2,1,0:T(8,128)S(1)} %get-tuple-element.69), channel_id=1, source_target_pairs={{8,0},{16,8},{24,16},{9,1},{17,9},{25,17},{10,2},{18,10},{26,18},{... | collective-permute-start | bytes 491528 | tf_op jit(solution)/shard_map/ppermute | solution.py:689
  32.1 0.1 shard_map.71.refs_7_.refs_12_
  32.2 0.0 copy-done.3
  32.2 0.0 copy-done.2
  32.3 0.0 copy-done
  32.3 0.0 copy-done.1
  32.3 1.9 %shard_map.72 = (f32[16,48,128]{2,1,0:T(8,128)S(1)}, f32[16,48,128]{2,1,0:T(8,128)S(1)}, f32[16,48,128]{2,1,0:T(8,128)S(1)}, f32[16,48,128]{2,1,0:T(8,128)S(1)},...) custom-call(f32[2,16,32,128]{3,2,1,0:T(8,128)S(1)} %copy-done, ...), custom_call_target="tpu_custom_call" | custom-call | flops 100000000 | bytes 1000000 | tf_op jit(solution)/shard_map/pallas_call | solution.py:660
  34.2 0.0 collective-permute-done.4.refs_5_
  34.2 0.1 collective-permute-done.5.refs_6_
  34.3 0.0 collective-permute-done.2.refs_3_
  34.3 0.0 collective-permute-done.3.refs_4_
  34.3 3.3 %shard_map.73 = (f32[16,48,128]{2,1,0:T(8,128)S(1)}, f32[16,48,128]{2,1,0:T(8,128)S(1)}, f32[16,48,128]{2,1,0:T(8,128)S(1)}, f32[16,48,128]{2,1,0:T(8,128)S(1)},...) custom-call(f32[2,16,32,128]{3,2,1,0:T(8,128)S(1)} %copy-done, ...), custom_call_target="tpu_custom_call" | custom-call | flops 100000000 | bytes 1000000 | tf_op jit(solution)/shard_map/pallas_call | solution.py:660
  37.6 0.1 copy.7
  37.7 15.1 %all_to_all.68 = f32[32,1,384]{2,1,0:T(1,128)S(1)} all-to-all(f32[32,1,384]{2,1,0:T(1,128)S(1)} %copy.7), channel_id=1, replica_groups=mesh['gx'=4,'gy'=8] {'gx','gy'}, dimensions={0} | all-to-all | bytes 98304 | tf_op jit(solution)/shard_map/all_to_all | solution.py:672
  52.8 5.2 %shard_map.74 = (f32[1,384]{1,0:T(1,128)S(1)}, f32[1,128]{1,0:T(1,128)S(1)}, f32[32,384]{1,0:T(8,128)S(1)}, f32[2,16,48,128]{3,2,1,0:T(8,128)S(1)}, f32[2,16,48,...) custom-call(f32[32,384]{1,0:T(8,128)S(1)} %bitcast.25, ...), custom_call_target="tpu_custom_call" | custom-call | flops 100000000 | bytes 1000000 | tf_op jit(solution)/shard_map/pallas_call | solution.py:660
  58.0 0.1 copy.8
  58.0 8.9 %all_to_all.69 = f32[32,1,384]{2,1,0:T(1,128)S(1)} all-to-all(f32[32,1,384]{2,1,0:T(1,128)S(1)} %copy.8), channel_id=1, replica_groups=mesh['gx'=4,'gy'=8] {'gx','gy'}, dimensions={0} | all-to-all | bytes 98304 | tf_op jit(solution)/shard_map/all_to_all | solution.py:672
  67.0 4.6 %shard_map.75 = (f32[1,384]{1,0:T(1,128)S(1)}, f32[1,128]{1,0:T(1,128)S(1)}, f32[32,384]{1,0:T(8,128)S(1)}, f32[2,16,48,128]{3,2,1,0:T(8,128)S(1)}, f32[2,16,48,...) custom-call(f32[32,384]{1,0:T(8,128)S(1)} %bitcast.26, ...), custom_call_target="tpu_custom_call" | custom-call | flops 100000000 | bytes 1000000 | tf_op jit(solution)/shard_map/pallas_call | solution.py:660
  71.5 0.1 copy.9
  71.6 8.9 %all_to_all.70 = f32[32,1,384]{2,1,0:T(1,128)S(1)} all-to-all(f32[32,1,384]{2,1,0:T(1,128)S(1)} %copy.9), channel_id=1, replica_groups=mesh['gx'=4,'gy'=8] {'gx','gy'}, dimensions={0} | all-to-all | bytes 98304 | tf_op jit(solution)/shard_map/all_to_all | solution.py:672
  80.5 4.2 %shard_map.76 = (f32[1,384]{1,0:T(1,128)S(1)}, f32[1,128]{1,0:T(1,128)S(1)}, f32[32,384]{1,0:T(8,128)S(1)}, f32[2,16,48,128]{3,2,1,0:T(8,128)S(1)}, f32[2,16,48,...) custom-call(f32[32,384]{1,0:T(8,128)S(1)} %bitcast.27, ...), custom_call_target="tpu_custom_call" | custom-call | flops 100000000 | bytes 1000000 | tf_op jit(solution)/shard_map/pallas_call | solution.py:660
  84.8 0.1 copy.10
  84.9 8.9 %all_to_all.71 = f32[32,1,384]{2,1,0:T(1,128)S(1)} all-to-all(f32[32,1,384]{2,1,0:T(1,128)S(1)} %copy.10), channel_id=1, replica_groups=mesh['gx'=4,'gy'=8] {'gx','gy'}, dimensions={0} | all-to-all | bytes 98304 | tf_op jit(solution)/shard_map/all_to_all | solution.py:672
  93.8 2.0 %shard_map.77 = (f32[1,384]{1,0:T(1,128)S(1)}, f32[1,128]{1,0:T(1,128)S(1)}, f32[32,384]{1,0:T(8,128)S(1)}) custom-call(f32[32,384]{1,0:T(8,128)S(1)} %bitcast.24, f32[16,48,128]{2,1,0:T(8,128)S(1)} %get-tuple-element.76.refs_10_.refs_1_, f32[16,48,128]{2,1,0:T(8,128)S(1)} %get-tuple-element.77.refs_11_.refs_2_, ...), custom_call_target="tpu_custom_call" | custom-call | flops 100000000 | bytes 1000000 | tf_op jit(solution)/shard_map/pallas_call | solution.py:660
  95.8 0.1 copy.11
  95.8 8.9 %all_to_all.72 = f32[32,1,384]{2,1,0:T(1,128)S(1)} all-to-all(f32[32,1,384]{2,1,0:T(1,128)S(1)} %copy.11), channel_id=1, replica_groups=mesh['gx'=4,'gy'=8] {'gx','gy'}, dimensions={0} | all-to-all | bytes 98304 | tf_op jit(solution)/shard_map/all_to_all | solution.py:672
  104.8 1.6 %shard_map.78 = (f32[2,16,32,128]{3,2,1,0:T(8,128)}, f32[2,4,5]{2,1,0:T(4,128)}) custom-call(f32[32,384]{1,0:T(8,128)S(1)} %bitcast.28, s32[16,48,128]{2,1,0:T(8,128)S(1)} %get-tuple-element.80.refs_14_.refs_5_.refs_1_, f32[2,16,32,128]{3,2,1,0:T(8,128)S(1)} %get-tuple-element.112.refs_2_, f32[2,16,32,128]{3,2,1,0:T(8,128)S(1)} %get-tuple-element.113.refs_3_, ...), custom_call_target="tpu_custom_call" | custom-call | flops 100000000 | bytes 1000000 | tf_op jit(solution)/shard_map/pallas_call | solution.py:660
  (6 shorter events, 0.1 us)
Async XLA Ops:
  0.6 11.1 %copy-start.4 = (f32[2,16,512]{2,1,0:T(8,128)S(1)}, f32[2,16,512]{2,1,0:T(8,128)}, u32[]{:S(2)}) copy-start(f32[2,16,512]{2,1,0:T(8,128)} %param.9) | copy-start | bytes 196612
  2.4 31.9 %collective-permute-start.2 = (f32[5,8,32,128]{3,2,1,0:T(8,128)S(1)}, f32[5,8,32,128]{3,2,1,0:T(8,128)S(1)}, u32[]{:S(2)}, u32[]{:S(2)}) collective-permute-start(f32[5,8,32,128]{3,2,1,0:T(8,128)S(1)} %get-tuple-element.66), channel_id=1, source_target_pairs={{0,8},{8,16},{16,24},{1,9},{9,17},{17,25},{2,10},{10,18},{18,26},{... | collective-permute-start | bytes 1966088 | tf_op jit(solution)/shard_map/ppermute | solution.py:688
  4.9 29.4 %collective-permute-start.3 = (f32[5,8,32,128]{3,2,1,0:T(8,128)S(1)}, f32[5,8,32,128]{3,2,1,0:T(8,128)S(1)}, u32[]{:S(2)}, u32[]{:S(2)}) collective-permute-start(f32[5,8,32,128]{3,2,1,0:T(8,128)S(1)} %get-tuple-element.67), channel_id=1, source_target_pairs={{8,0},{16,8},{24,16},{9,1},{17,9},{25,17},{10,2},{18,10},{26,18},{... | collective-permute-start | bytes 1966088 | tf_op jit(solution)/shard_map/ppermute | solution.py:689
  6.2 22.4 %collective-permute-start = (f32[5,16,8,128]{3,2,1,0:T(8,128)S(1)}, f32[5,16,8,128]{3,2,1,0:T(8,128)S(1)}, u32[]{:S(2)}, u32[]{:S(2)}) collective-permute-start(f32[5,16,8,128]{3,2,1,0:T(8,128)S(1)} %get-tuple-element.61), channel_id=1, source_target_pairs={{0,1},{1,2},{2,3},{3,4},{4,5},{5,6},{6,7},{8,9},{9,10},{10,11},{11... | collective-permute-start | bytes 983048 | tf_op jit(solution)/shard_map/ppermute | solution.py:688
  10.4 18.2 %collective-permute-start.1 = (f32[5,16,8,128]{3,2,1,0:T(8,128)S(1)}, f32[5,16,8,128]{3,2,1,0:T(8,128)S(1)}, u32[]{:S(2)}, u32[]{:S(2)}) collective-permute-start(f32[5,16,8,128]{3,2,1,0:T(8,128)S(1)} %get-tuple-element.62), channel_id=1, source_target_pairs={{1,0},{2,1},{3,2},{4,3},{5,4},{6,5},{7,6},{9,8},{10,9},{11,10},{12... | collective-permute-start | bytes 983048 | tf_op jit(solution)/shard_map/ppermute | solution.py:689
  11.8 20.5 %copy-start.3 = (s32[16,32,128]{2,1,0:T(8,128)S(1)}, s32[16,32,128]{2,1,0:T(8,128)}, u32[]{:S(2)}) copy-start(s32[16,32,128]{2,1,0:T(8,128)} %agg.2) | copy-start | bytes 786436
  12.0 20.2 %copy-start.2 = (s32[16,32,128]{2,1,0:T(8,128)S(1)}, s32[16,32,128]{2,1,0:T(8,128)}, u32[]{:S(2)}) copy-start(s32[16,32,128]{2,1,0:T(8,128)} %layer.2) | copy-start | bytes 786436
  28.6 3.7 %copy-start = (f32[2,16,32,128]{3,2,1,0:T(8,128)S(1)}, f32[2,16,32,128]{3,2,1,0:T(8,128)}, u32[]{:S(2)}) copy-start(f32[2,16,32,128]{3,2,1,0:T(8,128)} %refs_18_) | copy-start | bytes 1572868
  28.6 3.6 %copy-start.1 = (f32[16,32,128]{2,1,0:T(8,128)S(1)}, f32[16,32,128]{2,1,0:T(8,128)}, u32[]{:S(2)}) copy-start(f32[16,32,128]{2,1,0:T(8,128)} %wave.2) | copy-start | bytes 786436
  28.7 5.5 %collective-permute-start.4 = (f32[5,4,16,128]{3,2,1,0:T(8,128)S(1)}, f32[5,4,16,128]{3,2,1,0:T(8,128)S(1)}, u32[]{:S(2)}, u32[]{:S(2)}) collective-permute-start(f32[5,4,16,128]{3,2,1,0:T(8,128)S(1)} %get-tuple-element.68), channel_id=1, source_target_pairs={{0,8},{8,16},{16,24},{1,9},{9,17},{17,25},{2,10},{10,18},{18,26},{... | collective-permute-start | bytes 491528 | tf_op jit(solution)/shard_map/ppermute | solution.py:688
  30.8 3.5 %collective-permute-start.5 = (f32[5,4,16,128]{3,2,1,0:T(8,128)S(1)}, f32[5,4,16,128]{3,2,1,0:T(8,128)S(1)}, u32[]{:S(2)}, u32[]{:S(2)}) collective-permute-start(f32[5,4,16,128]{3,2,1,0:T(8,128)S(1)} %get-tuple-element.69), channel_id=1, source_target_pairs={{8,0},{16,8},{24,16},{9,1},{17,9},{25,17},{10,2},{18,10},{26,18},{... | collective-permute-start | bytes 491528 | tf_op jit(solution)/shard_map/ppermute | solution.py:689

commit v4 on v3

--- a/solution.py
+++ b/solution.py
@@ -10,6 +10,7 @@
 
 ITERS = 4
 HALO = 2 * ITERS
+GROUP = 4
 AXES = ("gx", "gy")
 AGG = 16
 damping = 0.8
@@ -43,7 +44,7 @@
     return jnp.take_along_axis(src, index, axis=1, mode="promise_in_bounds")
 
 
-def planes(lo, hi, fn, carry=None, width=8):
+def planes(lo, hi, fn, carry=None, width=16):
     count = hi - lo
     step = max(d for d in range(1, count + 1) if count % d == 0 and d <= width + width // 2)
     if step * 2 < width and count > width:
@@ -74,17 +75,11 @@
 
 def stencil(ref, c, x, y0, y1):
     mid = ref[c, x, 8 + y0 : 8 + y1, :]
-    total = (
-        ref[c, x - 1, 8 + y0 : 8 + y1, :]
-        + ref[c, x + 1, 8 + y0 : 8 + y1, :]
-        + ref[c, x, 7 + y0 : 7 + y1, :]
-        + ref[c, x, 9 + y0 : 9 + y1, :]
-    )
     lane = lanes(mid.shape)
     last = mid.shape[-1] - 1
-    total = total + jnp.where(lane == 0, 0.0, pltpu.roll(mid, 1, 1))
-    total = total + jnp.where(lane == last, 0.0, pltpu.roll(mid, last, 1))
-    return mid, total
+    total = jnp.where(lane == 0, 0.0, pltpu.roll(mid, 1, 1)) + jnp.where(lane == last, 0.0, pltpu.roll(mid, last, 1))
+    total = total + (ref[c, x - 1, 8 + y0 : 8 + y1, :] + ref[c, x + 1, 8 + y0 : 8 + y1, :])
+    return mid, total + (ref[c, x, 7 + y0 : 7 + y1, :] + ref[c, x, 9 + y0 : 9 + y1, :])
 
 
 def operate_plane(ref, k, coefs, y0, y1):
@@ -103,28 +98,28 @@
     return out
 
 
-def keep_split(ref, c, i, x):
+def halves(x):
     top = x.astype(jnp.bfloat16)
-    ref[c, i, :, 0:128] = top
-    ref[c, i, :, 128:256] = (x - top.astype(F32)).astype(jnp.bfloat16)
-
-
-def restrict(split, ends, own):
-    cx, cy = own
+    return jnp.concatenate([top, (x - top.astype(F32)).astype(jnp.bfloat16)], axis=1)
+
+
+def below_ones():
     r = lax.broadcasted_iota(jnp.int32, (256, 128), 0) % 128
-    ones = jnp.where(r <= lanes((256, 128)), 1.0, 0.0).astype(jnp.bfloat16)
-    per = 16
-    out = []
-    for c in range(2):
-        acc = jnp.zeros((8, 128), F32)
-        for i in range(0, cx, per):
-            block = split[c, i : i + per].reshape(cy * per, 256)
-            sums = jnp.dot(block, ones, preferred_element_type=F32)
-            for k in range(per):
-                part = sums[cy * k : cy * (k + 1)]
-                acc = acc + fold8(jnp.take_along_axis(part, ends[i + k], axis=1, mode="promise_in_bounds"))
-        out.append(acc)
-    return out
+    return jnp.where(r <= lanes((256, 128)), 1.0, 0.0).astype(jnp.bfloat16)
+
+
+def restrict(parts, ends, i, ones, acc):
+    cy = parts[0][0].shape[0]
+    sums = jnp.dot(
+        jnp.concatenate([p for pair in parts for p in pair], axis=0), ones, preferred_element_type=F32
+    )
+    acc = list(acc)
+    for k in range(len(parts)):
+        index = ends[i + k]
+        for c in range(2):
+            part = sums[cy * (2 * k + c) : cy * (2 * k + c + 1)]
+            acc[c] = acc[c] + fold8(jnp.take_along_axis(part, index, axis=1, mode="promise_in_bounds"))
+    return tuple(acc)
 
 
 def spread_rhs(g0, g1, cols_ref, pad_ref, out_ref, scalars, grid):
@@ -179,43 +174,59 @@
     g[1, k, 8 + y0 : 8 + y1, :] = f[1, k, 8 + y0 : 8 + y1, :] + (p * e1 + q * e0)
 
 
-def pairs(lo, hi, size, fn, low, high):
-    if hi > lo:
-        def go(x):
-            fn(x, low(x))
-            y = size - 1 - x
-            fn(y, high(y))
-
-        planes(lo, hi, go, width=4)
-
-
-def centre(f, g, u, t, t_rim, places, halo, s, split, ends, own, rows, t_rows):
+def window(halo, cy):
+    if halo > 4:
+        return 0, cy + 2 * HALO
+    if halo > 0:
+        return HALO - 4, HALO + cy + 4
+    return HALO, HALO + cy
+
+
+def pairs(lo, size, fn, low, high):
+    for x in range(lo, HALO):
+        y = size - 1 - x
+        fn(x, low(x), HALO - x)
+        fn(y, high(y), HALO - x)
+
+
+def centre(f, g, u, t, t_rim, places, halo, s, ends, own, rows, t_rows):
     mine, low, high = places
     cx, cy = own
     size = cx + 2 * HALO
     y0, y1 = HALO, HALO + cy
     r0, r1 = t_rows
-    pairs(HALO - halo + 1, HALO, size, lambda k, c: smooth_plane(f, g, u, k, c, *rows), low, high)
+    pairs(
+        HALO - halo + 1, size,
+        lambda k, c, far: smooth_plane(f, g, u, k, c, *window(halo - 1 - far, cy)), low, high,
+    )
     planes(HALO, HALO + cx, lambda x: smooth_plane(f, g, u, x, mine(x), *rows))
 
-    def outer(k, c):
-        a0, a1 = operate_plane(g, k, c, r0, r1)
-        t_rim[0, c[1], r0:r1, :], t_rim[1, c[1], r0:r1, :] = a0, a1
-
-    pairs(HALO - halo + 2, HALO, size, outer, low, high)
-
-    def middle(x):
-        i = x - HALO
-        a0, a1 = operate_plane(g, x, mine(x), r0, r1)
-        t[0, i, r0:r1, :], t[1, i, r0:r1, :] = a0, a1
-        lo = y0 - r0
-        s[0, i] = g[0, x, 8 + y0 : 8 + y1, :]
-        s[1, i] = g[1, x, 8 + y0 : 8 + y1, :]
-        keep_split(split, 0, i, u[0, x, y0:y1, :] - a0[lo : lo + cy])
-        keep_split(split, 1, i, u[1, x, y0:y1, :] - a1[lo : lo + cy])
-
-    planes(HALO, HALO + cx, middle)
-    return restrict(split, ends, own)
+    def outer(k, c, far):
+        q0, q1 = window(halo - 2 - far, cy)
+        a0, a1 = operate_plane(g, k, c, q0, q1)
+        t_rim[0, c[1], q0:q1, :], t_rim[1, c[1], q0:q1, :] = a0, a1
+
+    pairs(HALO - halo + 2, size, outer, low, high)
+
+    ones = below_ones()
+
+    def middle(b, acc):
+        parts = []
+        for k in range(GROUP):
+            i = b * GROUP + k
+            x = HALO + i
+            a0, a1 = operate_plane(g, x, mine(x), r0, r1)
+            t[0, i, r0:r1, :], t[1, i, r0:r1, :] = a0, a1
+            lo = y0 - r0
+            s[0, i] = g[0, x, 8 + y0 : 8 + y1, :]
+            s[1, i] = g[1, x, 8 + y0 : 8 + y1, :]
+            parts.append((
+                halves(u[0, x, y0:y1, :] - a0[lo : lo + cy]), halves(u[1, x, y0:y1, :] - a1[lo : lo + cy])
+            ))
+        return restrict(parts, ends, b * GROUP, ones, acc)
+
+    zero = jnp.zeros((8, 128), F32)
+    return planes(0, cx // GROUP, middle, (zero, zero), width=16 // GROUP)
 
 
 def fill(store, y0, y1, wave, layer, a):
@@ -244,7 +255,7 @@
         r0, r1 = rhs[0, i], rhs[1, i]
         return acc + fold8(r0 * r0 + r1 * r1)
 
-    sq = planes(0, cx, inner, jnp.zeros((8, 128), F32))
+    sq = planes(0, cx, inner, jnp.zeros((8, 128), F32), width=8)
     sq_out[...] = scalar_row([(40, sq)])
 
     def find(i):
@@ -261,13 +272,13 @@
         low = jnp.where(val <= lane, low + 1, low)
         ends[i] = jnp.maximum(low - 1, 0)
 
-    planes(0, cx, find)
+    planes(0, cx, find, width=8)
 
 
 def start_kernel(grid, own, *refs):
     rhs, ylo, yhi, xlo, xhi, clo, chi, cols, ends, sq = refs[:10]
     home, rim = refs[10:15], refs[15:20]
-    t, t_rim, s, out_ref, u, f, g, split, pad = refs[20:]
+    t, t_rim, s, out_ref, u, f, g, pad = refs[20:]
     cx, cy = own
     ey = cy + 2 * HALO
     y0, y1 = HALO, HALO + cy
@@ -298,7 +309,7 @@
         first(mine(x), x, y1, ey, yhi[0, i], yhi[1, i])
 
     planes(HALO, HALO + cx, inner)
-    g0, g1 = centre(f, g, u, t, t_rim, (mine, low, high), HALO, s, split, ends, own, (0, ey), (0, ey))
+    g0, g1 = centre(f, g, u, t, t_rim, (mine, low, high), HALO, s, ends, own, (0, ey), (0, ey))
     spread_rhs(g0, g1, cols, pad, out_ref, sq[...], grid)
 
 
@@ -360,11 +371,13 @@
     return level[0]
 
 
-def prolong_plane(pc, k, ids, i, table, own, dx, values=None):
+def prolong_plane(pc, k, ids, i, table, own, dx, values=None, wide_y=True):
     cy = own[1]
     ey = cy + 2 * HALO
     for dy, lo, hi in ((0, 0, HALO), (1, HALO, HALO + cy), (2, HALO + cy, ey)):
         n = dx * 3 + dy
+        if dy != 1 and not wide_y:
+            continue
         if values is not None and dy == 1:
             bits = marks(ids[i, lo:hi, :])
             for c in range(2):
@@ -397,15 +410,6 @@
     f[0, k, 8 + lo : 8 + hi, :] = p * u0 - q * u1
     f[1, k, 8 + lo : 8 + hi, :] = p * u1 + q * u0
     return u0, u1
-
-
-def y_rows(j, cy):
-    halo = HALO - 2 - 2 * j
-    if halo > 4:
-        return 0, cy + 2 * HALO
-    if halo > 0:
-        return HALO - 4, HALO + cy + 4
-    return HALO, HALO + cy
 
 
 def step_kernel(j, grid, own, *refs):
@@ -425,14 +429,14 @@
         mr_out, tr_out = take_refs(2)
     pc = refs.pop(0)
     if not last:
-        u, f, split, pad = take_refs(4)
+        u, f, pad = take_refs(3)
     cx, cy = own
     mine = lambda x: (home, x - HALO)
     low = lambda x: (rim, x)
     high = lambda x: (rim, x - cx)
     y0, y1 = HALO, HALO + cy
-    rows = y_rows(j, cy)
     halo = HALO - 2 - 2 * j
+    rows = window(halo, cy)
     size = cx + 2 * HALO
 
     row = jnp.sum(rcv[...], axis=0, keepdims=True)
@@ -448,19 +452,18 @@
     table = table * wide(inv)
     c_out[...] = table
 
-    def outside(x):
-        prolong_plane(pc, x, rim[4], x, table, own, 0)
+    for x in range(HALO - halo - 1, HALO):
         y = 2 * HALO - 1 - x
-        prolong_plane(pc, y + cx, rim[4], y, table, own, 2)
-
-    planes(HALO - halo - 1, HALO, outside, width=4)
+        wide_y = halo + 1 - (HALO - x) > 0
+        prolong_plane(pc, x, rim[4], x, table, own, 0, wide_y=wide_y)
+        prolong_plane(pc, y + cx, rim[4], y, table, own, 2, wide_y=wide_y)
     values = [splats(table[:, 128:256], AGG * c) for c in range(2)]
     planes(HALO, HALO + cx, lambda x: prolong_plane(pc, x, home[4], x - HALO, table, own, 1, values))
 
-    def outer(k, c):
-        image_store(pc, u, f, k, c, t_rim, m_rim, scalars, mr_out, *rows)
-
-    pairs(HALO - halo, HALO, size, outer, low, high)
+    def outer(k, c, far):
+        image_store(pc, u, f, k, c, t_rim, m_rim, scalars, mr_out, *window(halo - far, cy))
+
+    pairs(HALO - halo, size, outer, low, high)
 
     def middle(x, acc):
         i = x - HALO
@@ -490,7 +493,7 @@
         out_ref[:, 256:384] = jnp.broadcast_to(dots, (n, 128))
         return
     t_rows = rows if j < ITERS - 2 else (y0, y1)
-    g0, g1 = centre(f, pc, u, t, tr_out, (mine, low, high), halo, s_out, split, ends, own, rows, t_rows)
+    g0, g1 = centre(f, pc, u, t, tr_out, (mine, low, high), halo, s_out, ends, own, rows, t_rows)
     spread_rhs(g0, g1, cols, pad, out_ref, dots, grid)
 
 
@@ -656,12 +659,11 @@
 
 
 def call(kernel, outs, scratch, args, flops=100_000_000, space=pltpu.VMEM):
-    vm = pl.BlockSpec(memory_space=pltpu.VMEM)
     return pl.pallas_call(
         kernel,
         out_shape=outs,
         in_specs=[pl.BlockSpec(memory_space=space)] * len(args),
-        out_specs=[vm] * len(outs),
+        out_specs=[pl.BlockSpec(memory_space=pltpu.VMEM)] * len(outs),
         scratch_shapes=scratch,
         compiler_params=pltpu.CompilerParams(vmem_limit_bytes=VLIMIT),
         cost_estimate=pl.CostEstimate(flops=flops, bytes_accessed=1_000_000, transcendentals=0),
@@ -720,7 +722,6 @@
     tall = vmem(2, ex, ey + 16, cz)
     flat = vmem(2, ex, ey, cz)
     pad = vmem(n + 2 * margin, 128)
-    split = vmem(2, cx, cy, 256, dtype=jnp.bfloat16)
 
     *own_coefs, ends, sq = call(
         functools.partial(own_kernel, own),
@@ -730,7 +731,7 @@
     res = call(
         functools.partial(start_kernel, grid, own),
         rim + [home2, rim2, mine, chunk],
-        [flat, tall, tall, split, pad],
+        [flat, tall, tall, pad],
         [right_side, ylo, yhi, xlo, xhi, clo, chi, cols, ends, sq] + own_coefs,
     )
     rim_coefs = list(res[:5])
@@ -746,7 +747,7 @@
             outs += [home2, home2, mine, mine]
             if j < ITERS - 2:
                 outs += [rim2, rim2]
-            scratch += [flat, tall, split, pad]
+            scratch += [flat, tall, pad]
         c, h, send, *rest = call(functools.partial(step_kernel, j, grid, own), outs, scratch, args)
         got = exchange(send)
         if not last:

time: 107 us -> 105 us (0.981)
  Pallas kernels: 24.9 us -> 22.8 us
    pallas_call x11, Pallas kernels: 24.9 us -> 22.8 us  [call(): pl.pallas_call(kernel, out_shape=outs, in_specs=[pl.BlockSpec(memory_spac...]
where the time goes in v4:
time: 105 us; the launch traced here: 104 us
  blocking collectives  67.4 us (64%)
  Pallas kernels  22.8 us (22%)
  starting transfers between devices  12.7 us (12%)
    all_to_all x6, blocking collectives, exchange(): return lax.all_to_all(x, AXES, 0, 0, tiled=True)  67.4 us
    pallas_call x11, Pallas kernels, call(): pl.pallas_call(kernel, out_shape=outs, in_specs=[pl.BlockSpec(memory_spac...  22.8 us
    ppermute x3, starting transfers between devices, swap(): low_in = lax.ppermute(high, axis, up)  8.86 us
    ppermute x3, starting transfers between devices, swap(): high_in = lax.ppermute(low, axis, down)  3.88 us
  transfers between devices with their start and end apart: 6, of which 1 were waited for; matrix products, arithmetic and copies ran while one was open for 0% of the time, Pallas kernels for 2%

profile of v4, /device:TPU:0, one launch (start us, length us, event | category | flops | bytes accessed | tf_op | source)
XLA Modules:
  0.0 104.2 jit_solution(10034678107013435260)
XLA Ops:
  0.6 0.0 copy-start.4
  0.6 1.8 %shard_map.68 = (f32[5,16,8,128]{3,2,1,0:T(8,128)S(1)}, f32[5,16,8,128]{3,2,1,0:T(8,128)S(1)}, f32[5,8,32,128]{3,2,1,0:T(8,128)S(1)}, f32[5,8,32,128]{3,2,1,0:T(8,128)S(1)}) custom-call(f32[2,16,32,128]{3,2,1,0:T(8,128)} %refs_18_, f32[16,32,128]{2,1,0:T(8,128)} %wave.2, s32[16,32,128]{2,1,0:T(8,128)} %layer.2, s32[16,32,128]{2,1,0:T(8,128)} %agg.2), custom_call_target="tpu_custom_call" | custom-call | flops 100000000 | bytes 1000000 | tf_op jit(solution)/shard_map/pallas_call | solution.py:662
  2.4 2.4 %collective-permute-start.2 = (f32[5,8,32,128]{3,2,1,0:T(8,128)S(1)}, f32[5,8,32,128]{3,2,1,0:T(8,128)S(1)}, u32[]{:S(2)}, u32[]{:S(2)}) collective-permute-start(f32[5,8,32,128]{3,2,1,0:T(8,128)S(1)} %get-tuple-element.66), channel_id=1, source_target_pairs={{0,8},{8,16},{16,24},{1,9},{9,17},{17,25},{2,10},{10,18},{18,26},{... | collective-permute-start | bytes 1966088 | tf_op jit(solution)/shard_map/ppermute | solution.py:690
  4.9 1.3 %collective-permute-start.3 = (f32[5,8,32,128]{3,2,1,0:T(8,128)S(1)}, f32[5,8,32,128]{3,2,1,0:T(8,128)S(1)}, u32[]{:S(2)}, u32[]{:S(2)}) collective-permute-start(f32[5,8,32,128]{3,2,1,0:T(8,128)S(1)} %get-tuple-element.67), channel_id=1, source_target_pairs={{8,0},{16,8},{24,16},{9,1},{17,9},{25,17},{10,2},{18,10},{26,18},{... | collective-permute-start | bytes 1966088 | tf_op jit(solution)/shard_map/ppermute | solution.py:691
  6.2 4.3 %collective-permute-start = (f32[5,16,8,128]{3,2,1,0:T(8,128)S(1)}, f32[5,16,8,128]{3,2,1,0:T(8,128)S(1)}, u32[]{:S(2)}, u32[]{:S(2)}) collective-permute-start(f32[5,16,8,128]{3,2,1,0:T(8,128)S(1)} %get-tuple-element.61), channel_id=1, source_target_pairs={{0,1},{1,2},{2,3},{3,4},{4,5},{5,6},{6,7},{8,9},{9,10},{10,11},{11... | collective-permute-start | bytes 983048 | tf_op jit(solution)/shard_map/ppermute | solution.py:690
  10.4 1.3 %collective-permute-start.1 = (f32[5,16,8,128]{3,2,1,0:T(8,128)S(1)}, f32[5,16,8,128]{3,2,1,0:T(8,128)S(1)}, u32[]{:S(2)}, u32[]{:S(2)}) collective-permute-start(f32[5,16,8,128]{3,2,1,0:T(8,128)S(1)} %get-tuple-element.62), channel_id=1, source_target_pairs={{1,0},{2,1},{3,2},{4,3},{5,4},{6,5},{7,6},{9,8},{10,9},{11,10},{12... | collective-permute-start | bytes 983048 | tf_op jit(solution)/shard_map/ppermute | solution.py:691
  11.7 0.0 copy-done.4
  11.8 0.0 copy-start.3
  11.8 0.3 shard_map.69
  12.0 0.0 copy-start.2
  12.0 16.5 %all_to_all.67 = f32[32,4,128]{2,1,0:T(4,128)S(1)} all-to-all(f32[32,4,128]{2,1,0:T(4,128)S(1)} %bitcast.30), channel_id=1, replica_groups=mesh['gx'=4,'gy'=8] {'gx','gy'}, dimensions={0} | all-to-all | bytes 131072 | tf_op jit(solution)/shard_map/all_to_all | solution.py:674
  28.6 0.0 copy-start
  28.6 0.0 collective-permute-done.ylo.refs_1_
  28.6 0.0 collective-permute-done.1.yhi.refs_2_
  28.6 0.0 copy-start.1
  28.7 2.2 %collective-permute-start.4 = (f32[5,4,16,128]{3,2,1,0:T(8,128)S(1)}, f32[5,4,16,128]{3,2,1,0:T(8,128)S(1)}, u32[]{:S(2)}, u32[]{:S(2)}) collective-permute-start(f32[5,4,16,128]{3,2,1,0:T(8,128)S(1)} %get-tuple-element.68), channel_id=1, source_target_pairs={{0,8},{8,16},{16,24},{1,9},{9,17},{17,25},{2,10},{10,18},{18,26},{... | collective-permute-start | bytes 491528 | tf_op jit(solution)/shard_map/ppermute | solution.py:690
  30.8 1.3 %collective-permute-start.5 = (f32[5,4,16,128]{3,2,1,0:T(8,128)S(1)}, f32[5,4,16,128]{3,2,1,0:T(8,128)S(1)}, u32[]{:S(2)}, u32[]{:S(2)}) collective-permute-start(f32[5,4,16,128]{3,2,1,0:T(8,128)S(1)} %get-tuple-element.69), channel_id=1, source_target_pairs={{8,0},{16,8},{24,16},{9,1},{17,9},{25,17},{10,2},{18,10},{26,18},{... | collective-permute-start | bytes 491528 | tf_op jit(solution)/shard_map/ppermute | solution.py:691
  32.1 0.1 shard_map.71.refs_7_.refs_12_
  32.2 0.0 copy-done.3
  32.2 0.0 copy-done.2
  32.3 0.0 copy-done
  32.3 0.0 copy-done.1
  32.3 1.9 %shard_map.72 = (f32[16,48,128]{2,1,0:T(8,128)S(1)}, f32[16,48,128]{2,1,0:T(8,128)S(1)}, f32[16,48,128]{2,1,0:T(8,128)S(1)}, f32[16,48,128]{2,1,0:T(8,128)S(1)},...) custom-call(f32[2,16,32,128]{3,2,1,0:T(8,128)S(1)} %copy-done, ...), custom_call_target="tpu_custom_call" | custom-call | flops 100000000 | bytes 1000000 | tf_op jit(solution)/shard_map/pallas_call | solution.py:662
  34.2 0.0 collective-permute-done.4.refs_5_
  34.2 0.1 collective-permute-done.5.refs_6_
  34.3 0.0 collective-permute-done.2.refs_3_
  34.3 0.0 collective-permute-done.3.refs_4_
  34.3 3.0 %shard_map.73 = (f32[16,48,128]{2,1,0:T(8,128)S(1)}, f32[16,48,128]{2,1,0:T(8,128)S(1)}, f32[16,48,128]{2,1,0:T(8,128)S(1)}, f32[16,48,128]{2,1,0:T(8,128)S(1)},...) custom-call(f32[2,16,32,128]{3,2,1,0:T(8,128)S(1)} %copy-done, ...), custom_call_target="tpu_custom_call" | custom-call | flops 100000000 | bytes 1000000 | tf_op jit(solution)/shard_map/pallas_call | solution.py:662
  37.3 0.1 copy.7
  37.4 15.1 %all_to_all.68 = f32[32,1,384]{2,1,0:T(1,128)S(1)} all-to-all(f32[32,1,384]{2,1,0:T(1,128)S(1)} %copy.7), channel_id=1, replica_groups=mesh['gx'=4,'gy'=8] {'gx','gy'}, dimensions={0} | all-to-all | bytes 98304 | tf_op jit(solution)/shard_map/all_to_all | solution.py:674
  52.5 4.5 %shard_map.74 = (f32[1,384]{1,0:T(1,128)S(1)}, f32[1,128]{1,0:T(1,128)S(1)}, f32[32,384]{1,0:T(8,128)S(1)}, f32[2,16,48,128]{3,2,1,0:T(8,128)S(1)}, f32[2,16,48,...) custom-call(f32[32,384]{1,0:T(8,128)S(1)} %bitcast.25, ...), custom_call_target="tpu_custom_call" | custom-call | flops 100000000 | bytes 1000000 | tf_op jit(solution)/shard_map/pallas_call | solution.py:662
  57.0 0.1 copy.8
  57.0 8.9 %all_to_all.69 = f32[32,1,384]{2,1,0:T(1,128)S(1)} all-to-all(f32[32,1,384]{2,1,0:T(1,128)S(1)} %copy.8), channel_id=1, replica_groups=mesh['gx'=4,'gy'=8] {'gx','gy'}, dimensions={0} | all-to-all | bytes 98304 | tf_op jit(solution)/shard_map/all_to_all | solution.py:674
  66.0 4.1 %shard_map.75 = (f32[1,384]{1,0:T(1,128)S(1)}, f32[1,128]{1,0:T(1,128)S(1)}, f32[32,384]{1,0:T(8,128)S(1)}, f32[2,16,48,128]{3,2,1,0:T(8,128)S(1)}, f32[2,16,48,...) custom-call(f32[32,384]{1,0:T(8,128)S(1)} %bitcast.26, ...), custom_call_target="tpu_custom_call" | custom-call | flops 100000000 | bytes 1000000 | tf_op jit(solution)/shard_map/pallas_call | solution.py:662
  70.1 0.1 copy.9
  70.1 8.9 %all_to_all.70 = f32[32,1,384]{2,1,0:T(1,128)S(1)} all-to-all(f32[32,1,384]{2,1,0:T(1,128)S(1)} %copy.9), channel_id=1, replica_groups=mesh['gx'=4,'gy'=8] {'gx','gy'}, dimensions={0} | all-to-all | bytes 98304 | tf_op jit(solution)/shard_map/all_to_all | solution.py:674
  79.1 4.0 %shard_map.76 = (f32[1,384]{1,0:T(1,128)S(1)}, f32[1,128]{1,0:T(1,128)S(1)}, f32[32,384]{1,0:T(8,128)S(1)}, f32[2,16,48,128]{3,2,1,0:T(8,128)S(1)}, f32[2,16,48,...) custom-call(f32[32,384]{1,0:T(8,128)S(1)} %bitcast.27, ...), custom_call_target="tpu_custom_call" | custom-call | flops 100000000 | bytes 1000000 | tf_op jit(solution)/shard_map/pallas_call | solution.py:662
  83.0 0.1 copy.10
  83.1 8.9 %all_to_all.71 = f32[32,1,384]{2,1,0:T(1,128)S(1)} all-to-all(f32[32,1,384]{2,1,0:T(1,128)S(1)} %copy.10), channel_id=1, replica_groups=mesh['gx'=4,'gy'=8] {'gx','gy'}, dimensions={0} | all-to-all | bytes 98304 | tf_op jit(solution)/shard_map/all_to_all | solution.py:674
  92.0 1.7 %shard_map.77 = (f32[1,384]{1,0:T(1,128)S(1)}, f32[1,128]{1,0:T(1,128)S(1)}, f32[32,384]{1,0:T(8,128)S(1)}) custom-call(f32[32,384]{1,0:T(8,128)S(1)} %bitcast.24, f32[16,48,128]{2,1,0:T(8,128)S(1)} %get-tuple-element.76.refs_10_.refs_1_, f32[16,48,128]{2,1,0:T(8,128)S(1)} %get-tuple-element.77.refs_11_.refs_2_, ...), custom_call_target="tpu_custom_call" | custom-call | flops 100000000 | bytes 1000000 | tf_op jit(solution)/shard_map/pallas_call | solution.py:662
  93.7 0.1 copy.11
  93.8 8.9 %all_to_all.72 = f32[32,1,384]{2,1,0:T(1,128)S(1)} all-to-all(f32[32,1,384]{2,1,0:T(1,128)S(1)} %copy.11), channel_id=1, replica_groups=mesh['gx'=4,'gy'=8] {'gx','gy'}, dimensions={0} | all-to-all | bytes 98304 | tf_op jit(solution)/shard_map/all_to_all | solution.py:674
  102.7 1.5 %shard_map.78 = (f32[2,16,32,128]{3,2,1,0:T(8,128)}, f32[2,4,5]{2,1,0:T(4,128)}) custom-call(f32[32,384]{1,0:T(8,128)S(1)} %bitcast.28, s32[16,48,128]{2,1,0:T(8,128)S(1)} %get-tuple-element.80.refs_14_.refs_5_.refs_1_, f32[2,16,32,128]{3,2,1,0:T(8,128)S(1)} %get-tuple-element.112.refs_2_, f32[2,16,32,128]{3,2,1,0:T(8,128)S(1)} %get-tuple-element.113.refs_3_, ...), custom_call_target="tpu_custom_call" | custom-call | flops 100000000 | bytes 1000000 | tf_op jit(solution)/shard_map/pallas_call | solution.py:662
  (6 shorter events, 0.1 us)
Async XLA Ops:
  0.6 11.1 %copy-start.4 = (f32[2,16,512]{2,1,0:T(8,128)S(1)}, f32[2,16,512]{2,1,0:T(8,128)}, u32[]{:S(2)}) copy-start(f32[2,16,512]{2,1,0:T(8,128)} %param.9) | copy-start | bytes 196612
  2.4 31.9 %collective-permute-start.2 = (f32[5,8,32,128]{3,2,1,0:T(8,128)S(1)}, f32[5,8,32,128]{3,2,1,0:T(8,128)S(1)}, u32[]{:S(2)}, u32[]{:S(2)}) collective-permute-start(f32[5,8,32,128]{3,2,1,0:T(8,128)S(1)} %get-tuple-element.66), channel_id=1, source_target_pairs={{0,8},{8,16},{16,24},{1,9},{9,17},{17,25},{2,10},{10,18},{18,26},{... | collective-permute-start | bytes 1966088 | tf_op jit(solution)/shard_map/ppermute | solution.py:690
  4.9 29.4 %collective-permute-start.3 = (f32[5,8,32,128]{3,2,1,0:T(8,128)S(1)}, f32[5,8,32,128]{3,2,1,0:T(8,128)S(1)}, u32[]{:S(2)}, u32[]{:S(2)}) collective-permute-start(f32[5,8,32,128]{3,2,1,0:T(8,128)S(1)} %get-tuple-element.67), channel_id=1, source_target_pairs={{8,0},{16,8},{24,16},{9,1},{17,9},{25,17},{10,2},{18,10},{26,18},{... | collective-permute-start | bytes 1966088 | tf_op jit(solution)/shard_map/ppermute | solution.py:691
  6.2 22.4 %collective-permute-start = (f32[5,16,8,128]{3,2,1,0:T(8,128)S(1)}, f32[5,16,8,128]{3,2,1,0:T(8,128)S(1)}, u32[]{:S(2)}, u32[]{:S(2)}) collective-permute-start(f32[5,16,8,128]{3,2,1,0:T(8,128)S(1)} %get-tuple-element.61), channel_id=1, source_target_pairs={{0,1},{1,2},{2,3},{3,4},{4,5},{5,6},{6,7},{8,9},{9,10},{10,11},{11... | collective-permute-start | bytes 983048 | tf_op jit(solution)/shard_map/ppermute | solution.py:690
  10.4 18.2 %collective-permute-start.1 = (f32[5,16,8,128]{3,2,1,0:T(8,128)S(1)}, f32[5,16,8,128]{3,2,1,0:T(8,128)S(1)}, u32[]{:S(2)}, u32[]{:S(2)}) collective-permute-start(f32[5,16,8,128]{3,2,1,0:T(8,128)S(1)} %get-tuple-element.62), channel_id=1, source_target_pairs={{1,0},{2,1},{3,2},{4,3},{5,4},{6,5},{7,6},{9,8},{10,9},{11,10},{12... | collective-permute-start | bytes 983048 | tf_op jit(solution)/shard_map/ppermute | solution.py:691
  11.8 20.5 %copy-start.3 = (s32[16,32,128]{2,1,0:T(8,128)S(1)}, s32[16,32,128]{2,1,0:T(8,128)}, u32[]{:S(2)}) copy-start(s32[16,32,128]{2,1,0:T(8,128)} %agg.2) | copy-start | bytes 786436
  12.0 20.2 %copy-start.2 = (s32[16,32,128]{2,1,0:T(8,128)S(1)}, s32[16,32,128]{2,1,0:T(8,128)}, u32[]{:S(2)}) copy-start(s32[16,32,128]{2,1,0:T(8,128)} %layer.2) | copy-start | bytes 786436
  28.6 3.7 %copy-start = (f32[2,16,32,128]{3,2,1,0:T(8,128)S(1)}, f32[2,16,32,128]{3,2,1,0:T(8,128)}, u32[]{:S(2)}) copy-start(f32[2,16,32,128]{3,2,1,0:T(8,128)} %refs_18_) | copy-start | bytes 1572868
  28.6 3.6 %copy-start.1 = (f32[16,32,128]{2,1,0:T(8,128)S(1)}, f32[16,32,128]{2,1,0:T(8,128)}, u32[]{:S(2)}) copy-start(f32[16,32,128]{2,1,0:T(8,128)} %wave.2) | copy-start | bytes 786436
  28.7 5.5 %collective-permute-start.4 = (f32[5,4,16,128]{3,2,1,0:T(8,128)S(1)}, f32[5,4,16,128]{3,2,1,0:T(8,128)S(1)}, u32[]{:S(2)}, u32[]{:S(2)}) collective-permute-start(f32[5,4,16,128]{3,2,1,0:T(8,128)S(1)} %get-tuple-element.68), channel_id=1, source_target_pairs={{0,8},{8,16},{16,24},{1,9},{9,17},{17,25},{2,10},{10,18},{18,26},{... | collective-permute-start | bytes 491528 | tf_op jit(solution)/shard_map/ppermute | solution.py:690
  30.8 3.5 %collective-permute-start.5 = (f32[5,4,16,128]{3,2,1,0:T(8,128)S(1)}, f32[5,4,16,128]{3,2,1,0:T(8,128)S(1)}, u32[]{:S(2)}, u32[]{:S(2)}) collective-permute-start(f32[5,4,16,128]{3,2,1,0:T(8,128)S(1)} %get-tuple-element.69), channel_id=1, source_target_pairs={{8,0},{16,8},{24,16},{9,1},{17,9},{25,17},{10,2},{18,10},{26,18},{... | collective-permute-start | bytes 491528 | tf_op jit(solution)/shard_map/ppermute | solution.py:691

commit v5 on v4

--- a/solution.py
+++ b/solution.py
@@ -108,14 +108,14 @@
     return jnp.where(r <= lanes((256, 128)), 1.0, 0.0).astype(jnp.bfloat16)
 
 
-def restrict(parts, ends, i, ones, acc):
+def restrict(parts, ends, where, ones, acc):
     cy = parts[0][0].shape[0]
     sums = jnp.dot(
         jnp.concatenate([p for pair in parts for p in pair], axis=0), ones, preferred_element_type=F32
     )
     acc = list(acc)
     for k in range(len(parts)):
-        index = ends[i + k]
+        index = ends[where[k]]
         for c in range(2):
             part = sums[cy * (2 * k + c) : cy * (2 * k + c + 1)]
             acc[c] = acc[c] + fold8(jnp.take_along_axis(part, index, axis=1, mode="promise_in_bounds"))
@@ -152,8 +152,8 @@
             ok = (group == k % 4) & (place + dy >= 0) & (place + dy < gy)
             outs[k // 4] = jnp.where(ok, piece, outs[k // 4])
     outs[2] = outs[2] + jnp.broadcast_to(scalars, (n, 128))
-    for r in range(3):
-        out_ref[:, 128 * r : 128 * (r + 1)] = outs[r]
+    for r in range(4):
+        out_ref[pl.ds(r, n, stride=4), :] = outs[r] if r < 3 else jnp.zeros((n, 128), F32)
 
 
 def scalar_row(items):
@@ -189,17 +189,18 @@
         fn(y, high(y), HALO - x)
 
 
-def centre(f, g, u, t, t_rim, places, halo, s, ends, own, rows, t_rows):
+def centre(f, g, u, t, t_rim, places, halo, s, ends, own, rows, t_rows, inner=None):
     mine, low, high = places
     cx, cy = own
     size = cx + 2 * HALO
     y0, y1 = HALO, HALO + cy
-    r0, r1 = t_rows
     pairs(
         HALO - halo + 1, size,
         lambda k, c, far: smooth_plane(f, g, u, k, c, *window(halo - 1 - far, cy)), low, high,
     )
-    planes(HALO, HALO + cx, lambda x: smooth_plane(f, g, u, x, mine(x), *rows))
+    for x in range(HALO, HALO + cx) if inner is None else (HALO, HALO + cx - 1):
+        smooth_plane(f, g, u, x, mine(x), *rows)
+    u_own = lambda i: (u[0, i + HALO, y0:y1, :], u[1, i + HALO, y0:y1, :])
 
     def outer(k, c, far):
         q0, q1 = window(halo - 2 - far, cy)
@@ -211,22 +212,31 @@
     ones = below_ones()
 
     def middle(b, acc):
-        parts = []
-        for k in range(GROUP):
-            i = b * GROUP + k
-            x = HALO + i
-            a0, a1 = operate_plane(g, x, mine(x), r0, r1)
-            t[0, i, r0:r1, :], t[1, i, r0:r1, :] = a0, a1
-            lo = y0 - r0
-            s[0, i] = g[0, x, 8 + y0 : 8 + y1, :]
-            s[1, i] = g[1, x, 8 + y0 : 8 + y1, :]
-            parts.append((
-                halves(u[0, x, y0:y1, :] - a0[lo : lo + cy]), halves(u[1, x, y0:y1, :] - a1[lo : lo + cy])
-            ))
-        return restrict(parts, ends, b * GROUP, ones, acc)
+        where = [b * GROUP + k for k in range(GROUP)]
+        return last_planes(g, u_own, t, s, mine, where, ends, own, t_rows, ones, acc)
 
     zero = jnp.zeros((8, 128), F32)
-    return planes(0, cx // GROUP, middle, (zero, zero), width=16 // GROUP)
+    if inner is None:
+        return planes(0, cx // GROUP, middle, (zero, zero), width=16 // GROUP)
+    where = [0, 1, cx - 2, cx - 1]
+    return last_planes(g, u_own, t, s, mine, where, ends, own, t_rows, ones, inner)
+
+
+def last_planes(g, u_own, t, s, mine, where, ends, own, t_rows, ones, acc, shift=HALO):
+    cy = own[1]
+    y0, y1 = HALO, HALO + cy
+    r0, r1 = t_rows
+    parts = []
+    for i in where:
+        k = i + shift
+        a0, a1 = operate_plane(g, k, mine(i + HALO), r0, r1)
+        t[0, i, r0:r1, :], t[1, i, r0:r1, :] = a0, a1
+        lo = y0 - r0
+        s[0, i] = g[0, k, 8 + y0 : 8 + y1, :]
+        s[1, i] = g[1, k, 8 + y0 : 8 + y1, :]
+        v0, v1 = u_own(i)
+        parts.append((halves(v0 - a0[lo : lo + cy]), halves(v1 - a1[lo : lo + cy])))
+    return restrict(parts, ends, where, ones, acc)
 
 
 def fill(store, y0, y1, wave, layer, a):
@@ -242,7 +252,8 @@
     refs[4][i, y0:y1, :] = a
 
 
-def own_kernel(own, rhs, wave, layer, agg, ylo, yhi, diag, absorb, sre, sim, ids, ends, sq_out):
+def own_kernel(own, rhs, wave, layer, agg, ylo, yhi, diag, absorb, sre, sim, ids, ends, sq_out,
+               t, s, share, g_edge, u, f, g):
     cx, cy = own
     ey = cy + 2 * HALO
     home = (diag, absorb, sre, sim, ids)
@@ -274,11 +285,40 @@
 
     planes(0, cx, find, width=8)
 
+    def first(i, lo, hi, r0, r1):
+        p, q = sre[i, lo:hi, :], sim[i, lo:hi, :]
+        u[0, i, lo:hi, :] = r0
+        u[1, i, lo:hi, :] = r1
+        f[0, i, 8 + lo : 8 + hi, :] = p * r0 - q * r1
+        f[1, i, 8 + lo : 8 + hi, :] = p * r1 + q * r0
+
+    for i in range(cx):
+        first(i, 0, HALO, ylo[0, i], ylo[1, i])
+        first(i, HALO, HALO + cy, rhs[0, i], rhs[1, i])
+        first(i, HALO + cy, ey, yhi[0, i], yhi[1, i])
+    for i in range(1, cx - 1):
+        smooth_plane(f, g, u, i, (home, i), 0, ey)
+    for k, i in enumerate((1, 2, cx - 3, cx - 2)):
+        for c in range(2):
+            g_edge[c, k] = g[c, i]
+    zero = jnp.zeros((8, 128), F32)
+    acc = zero, zero
+    ones = below_ones()
+    for b in range(2, cx - 2, GROUP):
+        acc = last_planes(
+            g, lambda i: (rhs[0, i], rhs[1, i]), t, s, lambda x: (home, x - HALO),
+            list(range(b, b + GROUP)), ends, own, (0, ey), ones, acc, shift=0,
+        )
+    for i in (1, cx - 2):
+        for c in range(2):
+            s[c, i] = g[c, i, 8 + HALO : 8 + HALO + cy, :]
+    share[0:8, :], share[8:16, :] = acc
+
 
 def start_kernel(grid, own, *refs):
-    rhs, ylo, yhi, xlo, xhi, clo, chi, cols, ends, sq = refs[:10]
-    home, rim = refs[10:15], refs[15:20]
-    t, t_rim, s, out_ref, u, f, g, pad = refs[20:]
+    rhs, ylo, yhi, xlo, xhi, clo, chi, cols, ends, sq, _, _, share, g_edge = refs[:14]
+    home, rim = refs[14:19], refs[19:24]
+    t, t_rim, s, out_ref, u, f, g, pad = refs[24:]
     cx, cy = own
     ey = cy + 2 * HALO
     y0, y1 = HALO, HALO + cy
@@ -308,8 +348,14 @@
         first(mine(x), x, y0, y1, rhs[0, i], rhs[1, i])
         first(mine(x), x, y1, ey, yhi[0, i], yhi[1, i])
 
-    planes(HALO, HALO + cx, inner)
-    g0, g1 = centre(f, g, u, t, t_rim, (mine, low, high), HALO, s, ends, own, (0, ey), (0, ey))
+    for i in (0, 1, cx - 2, cx - 1):
+        inner(HALO + i)
+    for k, i in enumerate((1, 2, cx - 3, cx - 2)):
+        for c in range(2):
+            g[c, HALO + i] = g_edge[c, k]
+    g0, g1 = centre(
+        f, g, u, t, t_rim, (mine, low, high), HALO, s, ends, own, (0, ey), (0, ey), (share[0:8, :], share[8:16, :])
+    )
     spread_rhs(g0, g1, cols, pad, out_ref, sq[...], grid)
 
 
@@ -439,7 +485,10 @@
     rows = window(halo, cy)
     size = cx + 2 * HALO
 
-    row = jnp.sum(rcv[...], axis=0, keepdims=True)
+    n = rcv.shape[0] // 4
+    row = jnp.concatenate(
+        [jnp.sum(rcv[pl.ds(r, n, stride=4), :], axis=0, keepdims=True) for r in range(3)], axis=1
+    )
     h, length = read_scalars(row[:, 256:384], [r[...] for r in h_old], j)
     inv = 1.0 / length
     write_scalars(h_out, h, length, inv)
@@ -487,10 +536,7 @@
     items = [(32 + k, acc[k]) for k in range(2 * j + 2)] + [(40, acc[-1])]
     dots = scalar_row(items)
     if last:
-        n = out_ref.shape[0]
-        for r in range(2):
-            out_ref[:, 128 * r : 128 * r + 128] = jnp.zeros((n, 128), F32)
-        out_ref[:, 256:384] = jnp.broadcast_to(dots, (n, 128))
+        out_ref[...] = jnp.broadcast_to(dots, out_ref.shape)
         return
     t_rows = rows if j < ITERS - 2 else (y0, y1)
     g0, g1 = centre(f, pc, u, t, tr_out, (mine, low, high), halo, s_out, ends, own, rows, t_rows)
@@ -577,7 +623,7 @@
     rows = refs[2 + 2 * ITERS : 2 + 3 * ITERS]
     sol, hess = refs[2 + 3 * ITERS :]
     cx, cy = own
-    final = jnp.sum(rcv[:, 256:384], axis=0, keepdims=True)
+    final = jnp.sum(rcv[pl.ds(2, rcv.shape[0] // 4, stride=4), :], axis=0, keepdims=True)
     scal = [r[...] for r in rows]
     beta = pick(scal[0], 40)
     upper, sub = [], []
@@ -658,13 +704,14 @@
     return jax.ShapeDtypeStruct(dims, dtype)
 
 
-def call(kernel, outs, scratch, args, flops=100_000_000, space=pltpu.VMEM):
+def call(kernel, outs, scratch, args, flops=100_000_000, space=pltpu.VMEM, aliases=None):
     return pl.pallas_call(
         kernel,
         out_shape=outs,
         in_specs=[pl.BlockSpec(memory_space=space)] * len(args),
         out_specs=[pl.BlockSpec(memory_space=pltpu.VMEM)] * len(outs),
         scratch_shapes=scratch,
+        input_output_aliases=aliases or {},
         compiler_params=pltpu.CompilerParams(vmem_limit_bytes=VLIMIT),
         cost_estimate=pl.CostEstimate(flops=flops, bytes_accessed=1_000_000, transcendentals=0),
     )(*args)
@@ -717,22 +764,25 @@
     rim = [shape(2 * HALO, ey, cz)] * 4 + [shape(2 * HALO, ey, cz, dtype=I32)]
     home2, rim2 = shape(2, cx, ey, cz), shape(2, 2 * HALO, ey, cz)
     mine = shape(2, cx, cy, cz)
-    chunk = shape(n, 384)
+    chunk = shape(4 * n, 128)
     vmem = lambda *dims, dtype=F32: pltpu.VMEM(dims, dtype)
     tall = vmem(2, ex, ey + 16, cz)
     flat = vmem(2, ex, ey, cz)
     pad = vmem(n + 2 * margin, 128)
 
-    *own_coefs, ends, sq = call(
+    short_tall = vmem(2, cx, ey + 16, cz)
+    *own_coefs, ends, sq, t_own, s, share, g_edge = call(
         functools.partial(own_kernel, own),
-        home + [shape(cx, cy, cz, dtype=I32), shape(1, 128)], [],
+        home + [shape(cx, cy, cz, dtype=I32), shape(1, 128), home2, mine, shape(16, 128), shape(2, 4, ey + 16, cz)],
+        [vmem(2, cx, ey, cz), short_tall, short_tall],
         [right_side, wavenumber, pml_layer, aggregate, ylo, yhi],
     )
     res = call(
         functools.partial(start_kernel, grid, own),
         rim + [home2, rim2, mine, chunk],
         [flat, tall, tall, pad],
-        [right_side, ylo, yhi, xlo, xhi, clo, chi, cols, ends, sq] + own_coefs,
+        [right_side, ylo, yhi, xlo, xhi, clo, chi, cols, ends, sq, t_own, s, share, g_edge] + own_coefs,
+        aliases={10: 5, 11: 7},
     )
     rim_coefs = list(res[:5])
     t_own, t_rim, s, send = res[5:]

time: 105 us -> 104 us (level)
  transfers between devices with their start and end apart: 6 -> 6, of which waited for: 1 -> 0; matrix products, arithmetic and copies ran while one was open for 0% -> 0% of each run, Pallas kernels for 2% -> 4%
where the time goes in v5:
time: 104 us; the launch traced here: 103 us
  blocking collectives  66.5 us (64%)
  Pallas kernels  23 us (22%)
  starting transfers between devices  12.7 us (12%)
    all_to_all x6, blocking collectives, exchange(): return lax.all_to_all(x, AXES, 0, 0, tiled=True)  66.5 us
    pallas_call x11, Pallas kernels, call(): pl.pallas_call(kernel, out_shape=outs, in_specs=[pl.BlockSpec(memory_spac...  23 us
    ppermute x3, starting transfers between devices, swap(): low_in = lax.ppermute(high, axis, up)  8.86 us
    ppermute x3, starting transfers between devices, swap(): high_in = lax.ppermute(low, axis, down)  3.88 us
  transfers between devices with their start and end apart: 6, of which 0 were waited for; matrix products, arithmetic and copies ran while one was open for 0% of the time, Pallas kernels for 4%

profile of v5, /device:TPU:0, one launch (start us, length us, event | category | flops | bytes accessed | tf_op | source)
XLA Modules:
  0.0 103.1 jit_solution(8748340708041090908)
XLA Ops:
  0.6 0.0 copy-start.4
  0.6 1.8 %shard_map.68 = (f32[5,16,8,128]{3,2,1,0:T(8,128)S(1)}, f32[5,16,8,128]{3,2,1,0:T(8,128)S(1)}, f32[5,8,32,128]{3,2,1,0:T(8,128)S(1)}, f32[5,8,32,128]{3,2,1,0:T(8,128)S(1)}) custom-call(f32[2,16,32,128]{3,2,1,0:T(8,128)} %refs_18_, f32[16,32,128]{2,1,0:T(8,128)} %wave.2, s32[16,32,128]{2,1,0:T(8,128)} %layer.2, s32[16,32,128]{2,1,0:T(8,128)} %agg.2), custom_call_target="tpu_custom_call" | custom-call | flops 100000000 | bytes 1000000 | tf_op jit(solution)/shard_map/pallas_call | solution.py:708
  2.4 2.4 %collective-permute-start.2 = (f32[5,8,32,128]{3,2,1,0:T(8,128)S(1)}, f32[5,8,32,128]{3,2,1,0:T(8,128)S(1)}, u32[]{:S(2)}, u32[]{:S(2)}) collective-permute-start(f32[5,8,32,128]{3,2,1,0:T(8,128)S(1)} %get-tuple-element.70), channel_id=1, source_target_pairs={{0,8},{8,16},{16,24},{1,9},{9,17},{17,25},{2,10},{10,18},{18,26},{... | collective-permute-start | bytes 1966088 | tf_op jit(solution)/shard_map/ppermute | solution.py:737
  4.9 1.3 %collective-permute-start.3 = (f32[5,8,32,128]{3,2,1,0:T(8,128)S(1)}, f32[5,8,32,128]{3,2,1,0:T(8,128)S(1)}, u32[]{:S(2)}, u32[]{:S(2)}) collective-permute-start(f32[5,8,32,128]{3,2,1,0:T(8,128)S(1)} %get-tuple-element.71), channel_id=1, source_target_pairs={{8,0},{16,8},{24,16},{9,1},{17,9},{25,17},{10,2},{18,10},{26,18},{... | collective-permute-start | bytes 1966088 | tf_op jit(solution)/shard_map/ppermute | solution.py:738
  6.2 4.3 %collective-permute-start = (f32[5,16,8,128]{3,2,1,0:T(8,128)S(1)}, f32[5,16,8,128]{3,2,1,0:T(8,128)S(1)}, u32[]{:S(2)}, u32[]{:S(2)}) collective-permute-start(f32[5,16,8,128]{3,2,1,0:T(8,128)S(1)} %get-tuple-element.65), channel_id=1, source_target_pairs={{0,1},{1,2},{2,3},{3,4},{4,5},{5,6},{6,7},{8,9},{9,10},{10,11},{11... | collective-permute-start | bytes 983048 | tf_op jit(solution)/shard_map/ppermute | solution.py:737
  10.4 1.3 %collective-permute-start.1 = (f32[5,16,8,128]{3,2,1,0:T(8,128)S(1)}, f32[5,16,8,128]{3,2,1,0:T(8,128)S(1)}, u32[]{:S(2)}, u32[]{:S(2)}) collective-permute-start(f32[5,16,8,128]{3,2,1,0:T(8,128)S(1)} %get-tuple-element.66), channel_id=1, source_target_pairs={{1,0},{2,1},{3,2},{4,3},{5,4},{6,5},{7,6},{9,8},{10,9},{11,10},{12... | collective-permute-start | bytes 983048 | tf_op jit(solution)/shard_map/ppermute | solution.py:738
  11.7 0.0 copy-done.4
  11.8 0.0 copy-start.3
  11.8 0.3 shard_map.69
  12.0 0.0 copy-start.2
  12.0 16.5 %all_to_all.67 = f32[32,4,128]{2,1,0:T(4,128)S(1)} all-to-all(f32[32,4,128]{2,1,0:T(4,128)S(1)} %bitcast.25), channel_id=1, replica_groups=mesh['gx'=4,'gy'=8] {'gx','gy'}, dimensions={0} | all-to-all | bytes 131072 | tf_op jit(solution)/shard_map/all_to_all | solution.py:721
  28.6 0.0 copy-start
  28.6 0.0 collective-permute-done.ylo.refs_1_
  28.6 0.0 collective-permute-done.1.yhi.refs_2_
  28.7 0.0 copy-start.1
  28.7 2.2 %collective-permute-start.4 = (f32[5,4,16,128]{3,2,1,0:T(8,128)S(1)}, f32[5,4,16,128]{3,2,1,0:T(8,128)S(1)}, u32[]{:S(2)}, u32[]{:S(2)}) collective-permute-start(f32[5,4,16,128]{3,2,1,0:T(8,128)S(1)} %get-tuple-element.72), channel_id=1, source_target_pairs={{0,8},{8,16},{16,24},{1,9},{9,17},{17,25},{2,10},{10,18},{18,26},{... | collective-permute-start | bytes 491528 | tf_op jit(solution)/shard_map/ppermute | solution.py:737
  30.8 1.3 %collective-permute-start.5 = (f32[5,4,16,128]{3,2,1,0:T(8,128)S(1)}, f32[5,4,16,128]{3,2,1,0:T(8,128)S(1)}, u32[]{:S(2)}, u32[]{:S(2)}) collective-permute-start(f32[5,4,16,128]{3,2,1,0:T(8,128)S(1)} %get-tuple-element.73), channel_id=1, source_target_pairs={{8,0},{16,8},{24,16},{9,1},{17,9},{25,17},{10,2},{18,10},{26,18},{... | collective-permute-start | bytes 491528 | tf_op jit(solution)/shard_map/ppermute | solution.py:738
  32.1 0.1 shard_map.71.refs_7_.refs_12_
  32.2 0.0 copy-done.3
  32.2 0.0 copy-done.2
  32.3 0.0 copy-done
  32.3 0.0 copy-done.1
  32.3 3.4 %shard_map.72 = (f32[16,48,128]{2,1,0:T(8,128)S(1)}, f32[16,48,128]{2,1,0:T(8,128)S(1)}, f32[16,48,128]{2,1,0:T(8,128)S(1)}, f32[16,48,128]{2,1,0:T(8,128)S(1)},...) custom-call(f32[2,16,32,128]{3,2,1,0:T(8,128)S(1)} %copy-done, ...), custom_call_target="tpu_custom_call" | custom-call | flops 100000000 | bytes 1000000 | tf_op jit(solution)/shard_map/pallas_call | solution.py:708
  35.6 0.0 collective-permute-done.4.refs_5_
  35.7 0.0 collective-permute-done.5.refs_6_
  35.7 0.0 collective-permute-done.2.refs_3_
  35.7 0.0 collective-permute-done.3.refs_4_
  35.7 1.6 %shard_map.73 = (f32[16,48,128]{2,1,0:T(8,128)S(1)}, f32[16,48,128]{2,1,0:T(8,128)S(1)}, f32[16,48,128]{2,1,0:T(8,128)S(1)}, f32[16,48,128]{2,1,0:T(8,128)S(1)},...) custom-call(f32[2,16,32,128]{3,2,1,0:T(8,128)S(1)} %copy-done, ...), custom_call_target="tpu_custom_call", output_to_operand_aliasing={{5}: (10, {}), {7}: (11, {})} | custom-call | flops 100000000 | bytes 1000000 | tf_op jit(solution)/shard_map/pallas_call | solution.py:708
  37.3 14.1 %all_to_all.68 = f32[32,4,128]{2,1,0:T(4,128)S(1)} all-to-all(f32[32,4,128]{2,1,0:T(4,128)S(1)} %bitcast.21), channel_id=1, replica_groups=mesh['gx'=4,'gy'=8] {'gx','gy'}, dimensions={0} | all-to-all | bytes 131072 | tf_op jit(solution)/shard_map/all_to_all | solution.py:721
  51.3 4.6 %shard_map.74 = (f32[1,384]{1,0:T(1,128)S(1)}, f32[1,128]{1,0:T(1,128)S(1)}, f32[128,128]{1,0:T(8,128)S(1)}, f32[2,16,48,128]{3,2,1,0:T(8,128)S(1)}, f32[2,16,48...) custom-call(f32[128,128]{1,0:T(8,128)S(1)} %bitcast.15, ...), custom_call_target="tpu_custom_call" | custom-call | flops 100000000 | bytes 1000000 | tf_op jit(solution)/shard_map/pallas_call | solution.py:708
  55.9 9.0 %all_to_all.69 = f32[32,4,128]{2,1,0:T(4,128)S(1)} all-to-all(f32[32,4,128]{2,1,0:T(4,128)S(1)} %bitcast.22), channel_id=1, replica_groups=mesh['gx'=4,'gy'=8] {'gx','gy'}, dimensions={0} | all-to-all | bytes 131072 | tf_op jit(solution)/shard_map/all_to_all | solution.py:721
  64.9 4.3 %shard_map.75 = (f32[1,384]{1,0:T(1,128)S(1)}, f32[1,128]{1,0:T(1,128)S(1)}, f32[128,128]{1,0:T(8,128)S(1)}, f32[2,16,48,128]{3,2,1,0:T(8,128)S(1)}, f32[2,16,48...) custom-call(f32[128,128]{1,0:T(8,128)S(1)} %bitcast.16, ...), custom_call_target="tpu_custom_call" | custom-call | flops 100000000 | bytes 1000000 | tf_op jit(solution)/shard_map/pallas_call | solution.py:708
  69.1 9.0 %all_to_all.70 = f32[32,4,128]{2,1,0:T(4,128)S(1)} all-to-all(f32[32,4,128]{2,1,0:T(4,128)S(1)} %bitcast.23), channel_id=1, replica_groups=mesh['gx'=4,'gy'=8] {'gx','gy'}, dimensions={0} | all-to-all | bytes 131072 | tf_op jit(solution)/shard_map/all_to_all | solution.py:721
  78.1 3.8 %shard_map.76 = (f32[1,384]{1,0:T(1,128)S(1)}, f32[1,128]{1,0:T(1,128)S(1)}, f32[128,128]{1,0:T(8,128)S(1)}, f32[2,16,48,128]{3,2,1,0:T(8,128)S(1)}, f32[2,16,48...) custom-call(f32[128,128]{1,0:T(8,128)S(1)} %bitcast.17, ...), custom_call_target="tpu_custom_call" | custom-call | flops 100000000 | bytes 1000000 | tf_op jit(solution)/shard_map/pallas_call | solution.py:708
  81.9 9.0 %all_to_all.71 = f32[32,4,128]{2,1,0:T(4,128)S(1)} all-to-all(f32[32,4,128]{2,1,0:T(4,128)S(1)} %bitcast.24), channel_id=1, replica_groups=mesh['gx'=4,'gy'=8] {'gx','gy'}, dimensions={0} | all-to-all | bytes 131072 | tf_op jit(solution)/shard_map/all_to_all | solution.py:721
  90.9 1.7 %shard_map.77 = (f32[1,384]{1,0:T(1,128)S(1)}, f32[1,128]{1,0:T(1,128)S(1)}, f32[128,128]{1,0:T(8,128)S(1)}) custom-call(f32[128,128]{1,0:T(8,128)S(1)} %bitcast.14, f32[16,48,128]{2,1,0:T(8,128)S(1)} %get-tuple-element.84.refs_14_.refs_1_, f32[16,48,128]{2,1,0:T(8,128)S(1)} %get-tuple-element.85.refs_15_.refs_2_, ...), custom_call_target="tpu_custom_call" | custom-call | flops 100000000 | bytes 1000000 | tf_op jit(solution)/shard_map/pallas_call | solution.py:708
  92.6 9.0 %all_to_all.72 = f32[32,4,128]{2,1,0:T(4,128)S(1)} all-to-all(f32[32,4,128]{2,1,0:T(4,128)S(1)} %bitcast.19), channel_id=1, replica_groups=mesh['gx'=4,'gy'=8] {'gx','gy'}, dimensions={0} | all-to-all | bytes 131072 | tf_op jit(solution)/shard_map/all_to_all | solution.py:721
  101.6 1.5 %shard_map.78 = (f32[2,16,32,128]{3,2,1,0:T(8,128)}, f32[2,4,5]{2,1,0:T(4,128)}) custom-call(f32[128,128]{1,0:T(8,128)S(1)} %bitcast.18, s32[16,48,128]{2,1,0:T(8,128)S(1)} %get-tuple-element.88.refs_18_.refs_5_.refs_1_, f32[2,16,32,128]{3,2,1,0:T(8,128)S(1)} %get-tuple-element.120.refs_2_, f32[2,16,32,128]{3,2,1,0:T(8,128)S(1)} %get-tuple-element.121.refs_3_, ...), custom_call_target="tpu_custom_call" | custom-call | flops 100000000 | bytes 1000000 | tf_op jit(solution)/shard_map/pallas_call | solution.py:708
  (1 shorter events, 0.0 us)
Async XLA Ops:
  0.6 11.1 %copy-start.4 = (f32[2,16,512]{2,1,0:T(8,128)S(1)}, f32[2,16,512]{2,1,0:T(8,128)}, u32[]{:S(2)}) copy-start(f32[2,16,512]{2,1,0:T(8,128)} %param.9) | copy-start | bytes 196612
  2.4 33.2 %collective-permute-start.2 = (f32[5,8,32,128]{3,2,1,0:T(8,128)S(1)}, f32[5,8,32,128]{3,2,1,0:T(8,128)S(1)}, u32[]{:S(2)}, u32[]{:S(2)}) collective-permute-start(f32[5,8,32,128]{3,2,1,0:T(8,128)S(1)} %get-tuple-element.70), channel_id=1, source_target_pairs={{0,8},{8,16},{16,24},{1,9},{9,17},{17,25},{2,10},{10,18},{18,26},{... | collective-permute-start | bytes 1966088 | tf_op jit(solution)/shard_map/ppermute | solution.py:737
  4.9 30.8 %collective-permute-start.3 = (f32[5,8,32,128]{3,2,1,0:T(8,128)S(1)}, f32[5,8,32,128]{3,2,1,0:T(8,128)S(1)}, u32[]{:S(2)}, u32[]{:S(2)}) collective-permute-start(f32[5,8,32,128]{3,2,1,0:T(8,128)S(1)} %get-tuple-element.71), channel_id=1, source_target_pairs={{8,0},{16,8},{24,16},{9,1},{17,9},{25,17},{10,2},{18,10},{26,18},{... | collective-permute-start | bytes 1966088 | tf_op jit(solution)/shard_map/ppermute | solution.py:738
  6.2 22.4 %collective-permute-start = (f32[5,16,8,128]{3,2,1,0:T(8,128)S(1)}, f32[5,16,8,128]{3,2,1,0:T(8,128)S(1)}, u32[]{:S(2)}, u32[]{:S(2)}) collective-permute-start(f32[5,16,8,128]{3,2,1,0:T(8,128)S(1)} %get-tuple-element.65), channel_id=1, source_target_pairs={{0,1},{1,2},{2,3},{3,4},{4,5},{5,6},{6,7},{8,9},{9,10},{10,11},{11... | collective-permute-start | bytes 983048 | tf_op jit(solution)/shard_map/ppermute | solution.py:737
  10.4 18.2 %collective-permute-start.1 = (f32[5,16,8,128]{3,2,1,0:T(8,128)S(1)}, f32[5,16,8,128]{3,2,1,0:T(8,128)S(1)}, u32[]{:S(2)}, u32[]{:S(2)}) collective-permute-start(f32[5,16,8,128]{3,2,1,0:T(8,128)S(1)} %get-tuple-element.66), channel_id=1, source_target_pairs={{1,0},{2,1},{3,2},{4,3},{5,4},{6,5},{7,6},{9,8},{10,9},{11,10},{12... | collective-permute-start | bytes 983048 | tf_op jit(solution)/shard_map/ppermute | solution.py:738
  11.8 20.5 %copy-start.3 = (s32[16,32,128]{2,1,0:T(8,128)S(1)}, s32[16,32,128]{2,1,0:T(8,128)}, u32[]{:S(2)}) copy-start(s32[16,32,128]{2,1,0:T(8,128)} %agg.2) | copy-start | bytes 786436
  12.0 20.2 %copy-start.2 = (s32[16,32,128]{2,1,0:T(8,128)S(1)}, s32[16,32,128]{2,1,0:T(8,128)}, u32[]{:S(2)}) copy-start(s32[16,32,128]{2,1,0:T(8,128)} %layer.2) | copy-start | bytes 786436
  28.6 3.7 %copy-start = (f32[2,16,32,128]{3,2,1,0:T(8,128)S(1)}, f32[2,16,32,128]{3,2,1,0:T(8,128)}, u32[]{:S(2)}) copy-start(f32[2,16,32,128]{3,2,1,0:T(8,128)} %refs_18_) | copy-start | bytes 1572868
  28.7 3.6 %copy-start.1 = (f32[16,32,128]{2,1,0:T(8,128)S(1)}, f32[16,32,128]{2,1,0:T(8,128)}, u32[]{:S(2)}) copy-start(f32[16,32,128]{2,1,0:T(8,128)} %wave.2) | copy-start | bytes 786436
  28.7 7.0 %collective-permute-start.4 = (f32[5,4,16,128]{3,2,1,0:T(8,128)S(1)}, f32[5,4,16,128]{3,2,1,0:T(8,128)S(1)}, u32[]{:S(2)}, u32[]{:S(2)}) collective-permute-start(f32[5,4,16,128]{3,2,1,0:T(8,128)S(1)} %get-tuple-element.72), channel_id=1, source_target_pairs={{0,8},{8,16},{16,24},{1,9},{9,17},{17,25},{2,10},{10,18},{18,26},{... | collective-permute-start | bytes 491528 | tf_op jit(solution)/shard_map/ppermute | solution.py:737
  30.8 4.8 %collective-permute-start.5 = (f32[5,4,16,128]{3,2,1,0:T(8,128)S(1)}, f32[5,4,16,128]{3,2,1,0:T(8,128)S(1)}, u32[]{:S(2)}, u32[]{:S(2)}) collective-permute-start(f32[5,4,16,128]{3,2,1,0:T(8,128)S(1)} %get-tuple-element.73), channel_id=1, source_target_pairs={{8,0},{16,8},{24,16},{9,1},{17,9},{25,17},{10,2},{18,10},{26,18},{... | collective-permute-start | bytes 491528 | tf_op jit(solution)/shard_map/ppermute | solution.py:738

commit v6 on v5

--- a/solution.py
+++ b/solution.py
@@ -210,14 +210,15 @@
     pairs(HALO - halo + 2, size, outer, low, high)
 
     ones = below_ones()
+    size_of = 2 * GROUP
 
     def middle(b, acc):
-        where = [b * GROUP + k for k in range(GROUP)]
+        where = [b * size_of + k for k in range(size_of)]
         return last_planes(g, u_own, t, s, mine, where, ends, own, t_rows, ones, acc)
 
     zero = jnp.zeros((8, 128), F32)
     if inner is None:
-        return planes(0, cx // GROUP, middle, (zero, zero), width=16 // GROUP)
+        return planes(0, cx // size_of, middle, (zero, zero), width=16 // size_of)
     where = [0, 1, cx - 2, cx - 1]
     return last_planes(g, u_own, t, s, mine, where, ends, own, t_rows, ones, inner)
 

time: 104 us -> 103 us (level)
  no operation moved by 1% of the time
where the time goes in v6:
time: 103 us; the launch traced here: 102 us
  blocking collectives  66.5 us (65%)
  Pallas kernels  22.2 us (22%)
  starting transfers between devices  12.7 us (12%)
    all_to_all x6, blocking collectives, exchange(): return lax.all_to_all(x, AXES, 0, 0, tiled=True)  66.5 us
    pallas_call x11, Pallas kernels, call(): pl.pallas_call(kernel, out_shape=outs, in_specs=[pl.BlockSpec(memory_spac...  22.2 us
    ppermute x3, starting transfers between devices, swap(): low_in = lax.ppermute(high, axis, up)  8.86 us
    ppermute x3, starting transfers between devices, swap(): high_in = lax.ppermute(low, axis, down)  3.88 us
  transfers between devices with their start and end apart: 6, of which 0 were waited for; matrix products, arithmetic and copies ran while one was open for 0% of the time, Pallas kernels for 4%

profile of v6, /device:TPU:0, one launch (start us, length us, event | category | flops | bytes accessed | tf_op | source)
XLA Modules:
  0.0 102.3 jit_solution(12781741383505917020)
XLA Ops:
  0.6 0.0 copy-start.4
  0.6 1.8 %shard_map.68 = (f32[5,16,8,128]{3,2,1,0:T(8,128)S(1)}, f32[5,16,8,128]{3,2,1,0:T(8,128)S(1)}, f32[5,8,32,128]{3,2,1,0:T(8,128)S(1)}, f32[5,8,32,128]{3,2,1,0:T(8,128)S(1)}) custom-call(f32[2,16,32,128]{3,2,1,0:T(8,128)} %refs_18_, f32[16,32,128]{2,1,0:T(8,128)} %wave.2, s32[16,32,128]{2,1,0:T(8,128)} %layer.2, s32[16,32,128]{2,1,0:T(8,128)} %agg.2), custom_call_target="tpu_custom_call" | custom-call | flops 100000000 | bytes 1000000 | tf_op jit(solution)/shard_map/pallas_call | solution.py:709
  2.4 2.4 %collective-permute-start.2 = (f32[5,8,32,128]{3,2,1,0:T(8,128)S(1)}, f32[5,8,32,128]{3,2,1,0:T(8,128)S(1)}, u32[]{:S(2)}, u32[]{:S(2)}) collective-permute-start(f32[5,8,32,128]{3,2,1,0:T(8,128)S(1)} %get-tuple-element.70), channel_id=1, source_target_pairs={{0,8},{8,16},{16,24},{1,9},{9,17},{17,25},{2,10},{10,18},{18,26},{... | collective-permute-start | bytes 1966088 | tf_op jit(solution)/shard_map/ppermute | solution.py:738
  4.9 1.3 %collective-permute-start.3 = (f32[5,8,32,128]{3,2,1,0:T(8,128)S(1)}, f32[5,8,32,128]{3,2,1,0:T(8,128)S(1)}, u32[]{:S(2)}, u32[]{:S(2)}) collective-permute-start(f32[5,8,32,128]{3,2,1,0:T(8,128)S(1)} %get-tuple-element.71), channel_id=1, source_target_pairs={{8,0},{16,8},{24,16},{9,1},{17,9},{25,17},{10,2},{18,10},{26,18},{... | collective-permute-start | bytes 1966088 | tf_op jit(solution)/shard_map/ppermute | solution.py:739
  6.2 4.3 %collective-permute-start = (f32[5,16,8,128]{3,2,1,0:T(8,128)S(1)}, f32[5,16,8,128]{3,2,1,0:T(8,128)S(1)}, u32[]{:S(2)}, u32[]{:S(2)}) collective-permute-start(f32[5,16,8,128]{3,2,1,0:T(8,128)S(1)} %get-tuple-element.65), channel_id=1, source_target_pairs={{0,1},{1,2},{2,3},{3,4},{4,5},{5,6},{6,7},{8,9},{9,10},{10,11},{11... | collective-permute-start | bytes 983048 | tf_op jit(solution)/shard_map/ppermute | solution.py:738
  10.4 1.3 %collective-permute-start.1 = (f32[5,16,8,128]{3,2,1,0:T(8,128)S(1)}, f32[5,16,8,128]{3,2,1,0:T(8,128)S(1)}, u32[]{:S(2)}, u32[]{:S(2)}) collective-permute-start(f32[5,16,8,128]{3,2,1,0:T(8,128)S(1)} %get-tuple-element.66), channel_id=1, source_target_pairs={{1,0},{2,1},{3,2},{4,3},{5,4},{6,5},{7,6},{9,8},{10,9},{11,10},{12... | collective-permute-start | bytes 983048 | tf_op jit(solution)/shard_map/ppermute | solution.py:739
  11.7 0.0 copy-done.4
  11.8 0.0 copy-start.3
  11.8 0.3 shard_map.69
  12.0 0.0 copy-start.2
  12.0 16.5 %all_to_all.67 = f32[32,4,128]{2,1,0:T(4,128)S(1)} all-to-all(f32[32,4,128]{2,1,0:T(4,128)S(1)} %bitcast.25), channel_id=1, replica_groups=mesh['gx'=4,'gy'=8] {'gx','gy'}, dimensions={0} | all-to-all | bytes 131072 | tf_op jit(solution)/shard_map/all_to_all | solution.py:722
  28.6 0.0 copy-start
  28.6 0.0 collective-permute-done.ylo.refs_1_
  28.6 0.0 collective-permute-done.1.yhi.refs_2_
  28.7 0.0 copy-start.1
  28.7 2.2 %collective-permute-start.4 = (f32[5,4,16,128]{3,2,1,0:T(8,128)S(1)}, f32[5,4,16,128]{3,2,1,0:T(8,128)S(1)}, u32[]{:S(2)}, u32[]{:S(2)}) collective-permute-start(f32[5,4,16,128]{3,2,1,0:T(8,128)S(1)} %get-tuple-element.72), channel_id=1, source_target_pairs={{0,8},{8,16},{16,24},{1,9},{9,17},{17,25},{2,10},{10,18},{18,26},{... | collective-permute-start | bytes 491528 | tf_op jit(solution)/shard_map/ppermute | solution.py:738
  30.8 1.3 %collective-permute-start.5 = (f32[5,4,16,128]{3,2,1,0:T(8,128)S(1)}, f32[5,4,16,128]{3,2,1,0:T(8,128)S(1)}, u32[]{:S(2)}, u32[]{:S(2)}) collective-permute-start(f32[5,4,16,128]{3,2,1,0:T(8,128)S(1)} %get-tuple-element.73), channel_id=1, source_target_pairs={{8,0},{16,8},{24,16},{9,1},{17,9},{25,17},{10,2},{18,10},{26,18},{... | collective-permute-start | bytes 491528 | tf_op jit(solution)/shard_map/ppermute | solution.py:739
  32.1 0.1 shard_map.71.refs_7_.refs_12_
  32.2 0.0 copy-done.3
  32.2 0.0 copy-done.2
  32.3 0.0 copy-done
  32.3 0.0 copy-done.1
  32.3 3.4 %shard_map.72 = (f32[16,48,128]{2,1,0:T(8,128)S(1)}, f32[16,48,128]{2,1,0:T(8,128)S(1)}, f32[16,48,128]{2,1,0:T(8,128)S(1)}, f32[16,48,128]{2,1,0:T(8,128)S(1)},...) custom-call(f32[2,16,32,128]{3,2,1,0:T(8,128)S(1)} %copy-done, ...), custom_call_target="tpu_custom_call" | custom-call | flops 100000000 | bytes 1000000 | tf_op jit(solution)/shard_map/pallas_call | solution.py:709
  35.6 0.0 collective-permute-done.4.refs_5_
  35.7 0.0 collective-permute-done.5.refs_6_
  35.7 0.0 collective-permute-done.2.refs_3_
  35.7 0.0 collective-permute-done.3.refs_4_
  35.7 1.6 %shard_map.73 = (f32[16,48,128]{2,1,0:T(8,128)S(1)}, f32[16,48,128]{2,1,0:T(8,128)S(1)}, f32[16,48,128]{2,1,0:T(8,128)S(1)}, f32[16,48,128]{2,1,0:T(8,128)S(1)},...) custom-call(f32[2,16,32,128]{3,2,1,0:T(8,128)S(1)} %copy-done, ...), custom_call_target="tpu_custom_call", output_to_operand_aliasing={{5}: (10, {}), {7}: (11, {})} | custom-call | flops 100000000 | bytes 1000000 | tf_op jit(solution)/shard_map/pallas_call | solution.py:709
  37.3 14.1 %all_to_all.68 = f32[32,4,128]{2,1,0:T(4,128)S(1)} all-to-all(f32[32,4,128]{2,1,0:T(4,128)S(1)} %bitcast.21), channel_id=1, replica_groups=mesh['gx'=4,'gy'=8] {'gx','gy'}, dimensions={0} | all-to-all | bytes 131072 | tf_op jit(solution)/shard_map/all_to_all | solution.py:722
  51.3 4.3 %shard_map.74 = (f32[1,384]{1,0:T(1,128)S(1)}, f32[1,128]{1,0:T(1,128)S(1)}, f32[128,128]{1,0:T(8,128)S(1)}, f32[2,16,48,128]{3,2,1,0:T(8,128)S(1)}, f32[2,16,48...) custom-call(f32[128,128]{1,0:T(8,128)S(1)} %bitcast.15, ...), custom_call_target="tpu_custom_call" | custom-call | flops 100000000 | bytes 1000000 | tf_op jit(solution)/shard_map/pallas_call | solution.py:709
  55.6 9.0 %all_to_all.69 = f32[32,4,128]{2,1,0:T(4,128)S(1)} all-to-all(f32[32,4,128]{2,1,0:T(4,128)S(1)} %bitcast.22), channel_id=1, replica_groups=mesh['gx'=4,'gy'=8] {'gx','gy'}, dimensions={0} | all-to-all | bytes 131072 | tf_op jit(solution)/shard_map/all_to_all | solution.py:722
  64.6 4.0 %shard_map.75 = (f32[1,384]{1,0:T(1,128)S(1)}, f32[1,128]{1,0:T(1,128)S(1)}, f32[128,128]{1,0:T(8,128)S(1)}, f32[2,16,48,128]{3,2,1,0:T(8,128)S(1)}, f32[2,16,48...) custom-call(f32[128,128]{1,0:T(8,128)S(1)} %bitcast.16, ...), custom_call_target="tpu_custom_call" | custom-call | flops 100000000 | bytes 1000000 | tf_op jit(solution)/shard_map/pallas_call | solution.py:709
  68.6 9.0 %all_to_all.70 = f32[32,4,128]{2,1,0:T(4,128)S(1)} all-to-all(f32[32,4,128]{2,1,0:T(4,128)S(1)} %bitcast.23), channel_id=1, replica_groups=mesh['gx'=4,'gy'=8] {'gx','gy'}, dimensions={0} | all-to-all | bytes 131072 | tf_op jit(solution)/shard_map/all_to_all | solution.py:722
  77.6 3.6 %shard_map.76 = (f32[1,384]{1,0:T(1,128)S(1)}, f32[1,128]{1,0:T(1,128)S(1)}, f32[128,128]{1,0:T(8,128)S(1)}, f32[2,16,48,128]{3,2,1,0:T(8,128)S(1)}, f32[2,16,48...) custom-call(f32[128,128]{1,0:T(8,128)S(1)} %bitcast.17, ...), custom_call_target="tpu_custom_call" | custom-call | flops 100000000 | bytes 1000000 | tf_op jit(solution)/shard_map/pallas_call | solution.py:709
  81.2 9.0 %all_to_all.71 = f32[32,4,128]{2,1,0:T(4,128)S(1)} all-to-all(f32[32,4,128]{2,1,0:T(4,128)S(1)} %bitcast.24), channel_id=1, replica_groups=mesh['gx'=4,'gy'=8] {'gx','gy'}, dimensions={0} | all-to-all | bytes 131072 | tf_op jit(solution)/shard_map/all_to_all | solution.py:722
  90.1 1.7 %shard_map.77 = (f32[1,384]{1,0:T(1,128)S(1)}, f32[1,128]{1,0:T(1,128)S(1)}, f32[128,128]{1,0:T(8,128)S(1)}) custom-call(f32[128,128]{1,0:T(8,128)S(1)} %bitcast.14, f32[16,48,128]{2,1,0:T(8,128)S(1)} %get-tuple-element.84.refs_14_.refs_1_, f32[16,48,128]{2,1,0:T(8,128)S(1)} %get-tuple-element.85.refs_15_.refs_2_, ...), custom_call_target="tpu_custom_call" | custom-call | flops 100000000 | bytes 1000000 | tf_op jit(solution)/shard_map/pallas_call | solution.py:709
  91.9 9.0 %all_to_all.72 = f32[32,4,128]{2,1,0:T(4,128)S(1)} all-to-all(f32[32,4,128]{2,1,0:T(4,128)S(1)} %bitcast.19), channel_id=1, replica_groups=mesh['gx'=4,'gy'=8] {'gx','gy'}, dimensions={0} | all-to-all | bytes 131072 | tf_op jit(solution)/shard_map/all_to_all | solution.py:722
  100.8 1.5 %shard_map.78 = (f32[2,16,32,128]{3,2,1,0:T(8,128)}, f32[2,4,5]{2,1,0:T(4,128)}) custom-call(f32[128,128]{1,0:T(8,128)S(1)} %bitcast.18, s32[16,48,128]{2,1,0:T(8,128)S(1)} %get-tuple-element.88.refs_18_.refs_5_.refs_1_, f32[2,16,32,128]{3,2,1,0:T(8,128)S(1)} %get-tuple-element.120.refs_2_, f32[2,16,32,128]{3,2,1,0:T(8,128)S(1)} %get-tuple-element.121.refs_3_, ...), custom_call_target="tpu_custom_call" | custom-call | flops 100000000 | bytes 1000000 | tf_op jit(solution)/shard_map/pallas_call | solution.py:709
  (1 shorter events, 0.0 us)
Async XLA Ops:
  0.6 11.1 %copy-start.4 = (f32[2,16,512]{2,1,0:T(8,128)S(1)}, f32[2,16,512]{2,1,0:T(8,128)}, u32[]{:S(2)}) copy-start(f32[2,16,512]{2,1,0:T(8,128)} %param.9) | copy-start | bytes 196612
  2.4 33.2 %collective-permute-start.2 = (f32[5,8,32,128]{3,2,1,0:T(8,128)S(1)}, f32[5,8,32,128]{3,2,1,0:T(8,128)S(1)}, u32[]{:S(2)}, u32[]{:S(2)}) collective-permute-start(f32[5,8,32,128]{3,2,1,0:T(8,128)S(1)} %get-tuple-element.70), channel_id=1, source_target_pairs={{0,8},{8,16},{16,24},{1,9},{9,17},{17,25},{2,10},{10,18},{18,26},{... | collective-permute-start | bytes 1966088 | tf_op jit(solution)/shard_map/ppermute | solution.py:738
  4.9 30.8 %collective-permute-start.3 = (f32[5,8,32,128]{3,2,1,0:T(8,128)S(1)}, f32[5,8,32,128]{3,2,1,0:T(8,128)S(1)}, u32[]{:S(2)}, u32[]{:S(2)}) collective-permute-start(f32[5,8,32,128]{3,2,1,0:T(8,128)S(1)} %get-tuple-element.71), channel_id=1, source_target_pairs={{8,0},{16,8},{24,16},{9,1},{17,9},{25,17},{10,2},{18,10},{26,18},{... | collective-permute-start | bytes 1966088 | tf_op jit(solution)/shard_map/ppermute | solution.py:739
  6.2 22.4 %collective-permute-start = (f32[5,16,8,128]{3,2,1,0:T(8,128)S(1)}, f32[5,16,8,128]{3,2,1,0:T(8,128)S(1)}, u32[]{:S(2)}, u32[]{:S(2)}) collective-permute-start(f32[5,16,8,128]{3,2,1,0:T(8,128)S(1)} %get-tuple-element.65), channel_id=1, source_target_pairs={{0,1},{1,2},{2,3},{3,4},{4,5},{5,6},{6,7},{8,9},{9,10},{10,11},{11... | collective-permute-start | bytes 983048 | tf_op jit(solution)/shard_map/ppermute | solution.py:738
  10.4 18.2 %collective-permute-start.1 = (f32[5,16,8,128]{3,2,1,0:T(8,128)S(1)}, f32[5,16,8,128]{3,2,1,0:T(8,128)S(1)}, u32[]{:S(2)}, u32[]{:S(2)}) collective-permute-start(f32[5,16,8,128]{3,2,1,0:T(8,128)S(1)} %get-tuple-element.66), channel_id=1, source_target_pairs={{1,0},{2,1},{3,2},{4,3},{5,4},{6,5},{7,6},{9,8},{10,9},{11,10},{12... | collective-permute-start | bytes 983048 | tf_op jit(solution)/shard_map/ppermute | solution.py:739
  11.8 20.5 %copy-start.3 = (s32[16,32,128]{2,1,0:T(8,128)S(1)}, s32[16,32,128]{2,1,0:T(8,128)}, u32[]{:S(2)}) copy-start(s32[16,32,128]{2,1,0:T(8,128)} %agg.2) | copy-start | bytes 786436
  12.0 20.2 %copy-start.2 = (s32[16,32,128]{2,1,0:T(8,128)S(1)}, s32[16,32,128]{2,1,0:T(8,128)}, u32[]{:S(2)}) copy-start(s32[16,32,128]{2,1,0:T(8,128)} %layer.2) | copy-start | bytes 786436
  28.6 3.7 %copy-start = (f32[2,16,32,128]{3,2,1,0:T(8,128)S(1)}, f32[2,16,32,128]{3,2,1,0:T(8,128)}, u32[]{:S(2)}) copy-start(f32[2,16,32,128]{3,2,1,0:T(8,128)} %refs_18_) | copy-start | bytes 1572868
  28.7 3.6 %copy-start.1 = (f32[16,32,128]{2,1,0:T(8,128)S(1)}, f32[16,32,128]{2,1,0:T(8,128)}, u32[]{:S(2)}) copy-start(f32[16,32,128]{2,1,0:T(8,128)} %wave.2) | copy-start | bytes 786436
  28.7 7.0 %collective-permute-start.4 = (f32[5,4,16,128]{3,2,1,0:T(8,128)S(1)}, f32[5,4,16,128]{3,2,1,0:T(8,128)S(1)}, u32[]{:S(2)}, u32[]{:S(2)}) collective-permute-start(f32[5,4,16,128]{3,2,1,0:T(8,128)S(1)} %get-tuple-element.72), channel_id=1, source_target_pairs={{0,8},{8,16},{16,24},{1,9},{9,17},{17,25},{2,10},{10,18},{18,26},{... | collective-permute-start | bytes 491528 | tf_op jit(solution)/shard_map/ppermute | solution.py:738
  30.8 4.8 %collective-permute-start.5 = (f32[5,4,16,128]{3,2,1,0:T(8,128)S(1)}, f32[5,4,16,128]{3,2,1,0:T(8,128)S(1)}, u32[]{:S(2)}, u32[]{:S(2)}) collective-permute-start(f32[5,4,16,128]{3,2,1,0:T(8,128)S(1)} %get-tuple-element.73), channel_id=1, source_target_pairs={{8,0},{16,8},{24,16},{9,1},{17,9},{25,17},{10,2},{18,10},{26,18},{... | collective-permute-start | bytes 491528 | tf_op jit(solution)/shard_map/ppermute | solution.py:739
